TPU v7x, 32 devices: a whole 2x2x4 slice. The times are simulated.
32 devices in a mesh: lat: 4 (over z), lon: 8 (over y, x, core).
Axes of the slice: x: 2, y: 2, z: 4, core: 2. Of those that a mesh axis runs over, the one named last changes fastest.
Arguments:
- tokens: bfloat16 [96, 384, 512], P('lat', 'lon'), may hold values from -8 to 8
- lat_band: int32 [96], replicated, may hold values from 0 to 7, as said below
- gain_attn: float32 [512], replicated, may hold values from 0.1 to 1.9
- w_qkv: bfloat16 [512, 1536], replicated, may hold values from -1.5 to 1.5
- w_out: bfloat16 [512, 512], replicated, may hold values from -0.25 to 0.25
- gain_merge: float32 [2048], replicated, may hold values from 0.1 to 1.9
- w_merge: bfloat16 [2048, 1024], replicated, may hold values from -0.125 to 0.125
- grad_merged: bfloat16 [48, 192, 1024], P('lat', 'lon'), may hold values from -6 to 6
Outputs:
- merged: bfloat16 [48, 192, 1024], P('lat', 'lon')
- grad_tokens: float32 [96, 384, 512], P('lat', 'lon')
- grad_gain_attn: float32 [512], replicated
- grad_w_qkv: float32 [512, 1536], replicated
- grad_w_out: float32 [512, 512], replicated
- grad_gain_merge: float32 [2048], replicated
- grad_w_merge: float32 [2048, 1024], replicated
Inputs may be any that keep to these rules, and one draw needn't show every extreme that they name: `lat_band`: band number of each latitude row; it never falls from one row to the next, and every band holds at least one row.
All inputs are finite; a program needn't handle non-finite values.
Results may differ from a plain program's by a relative error of at most 0.025.
Values may be sent and summed in bfloat16 or wider, within the bound.
No kernel may reach another device: no remote copies, remote signals or barrier semaphores. Data moves between devices by JAX's collectives and lax.ppermute only.
A program may use at most 192 MiB of HBM per device.

v0:
```python
import functools

import jax
import jax.numpy as jnp
import numpy as np
from jax import lax
from jax.experimental import pallas as pl
from jax.experimental.pallas import tpu as pltpu
from jax.sharding import PartitionSpec as P


WLAT = 6
WLON = 12
EPSILON = 1e-05
EDGE = 8
BF = jnp.bfloat16
F32 = jnp.float32

CALLS = 4


def dot_nn(a, b):
    return lax.dot_general(a, b, (((1,), (0,)), ((), ())), preferred_element_type=F32)


def dot_nt(a, b):
    return lax.dot_general(a, b, (((1,), (1,)), ((), ())), preferred_element_type=F32)


def dot_tn(a, b):
    return lax.dot_general(a, b, (((0,), (0,)), ((), ())), preferred_element_type=F32)


def params(steps):
    return pltpu.CompilerParams(
        dimension_semantics=("arbitrary",) * steps, vmem_limit_bytes=60 * 1024 * 1024
    )


def cost(flops, nbytes):
    return pl.CostEstimate(flops=int(flops), transcendentals=0, bytes_accessed=int(nbytes))


def window_matrix(cols, stride):
    count_b = cols // WLON
    mat = np.zeros((count_b * stride, WLAT * cols), np.float32)
    for b in range(count_b):
        for r in range(WLAT):
            for c in range(WLON):
                mat[b * stride + r * WLON + c, r * cols + b * WLON + c] = 1.0
    return mat


def halo_matrices(rows, cols, stride):
    hr, hc = WLAT // 2, WLON // 2
    count_a, count_b = rows // WLAT, cols // WLON
    padded = count_b * stride
    own = np.zeros((2, padded, WLAT * cols), np.float32)
    west = np.zeros((count_a, padded, rows * EDGE), np.float32)
    south = np.zeros((padded, hr * cols), np.float32)
    corner = np.zeros((padded, hr * EDGE), np.float32)
    for a in range(count_a):
        for b in range(count_b):
            for r in range(WLAT):
                for c in range(WLON):
                    place = b * stride + r * WLON + c
                    row, col = a * WLAT + r - hr, b * WLON + c - hc
                    if row >= 0 and col >= 0:
                        base = row if a == 0 else r
                        own[min(a, 1), place, base * cols + col] = 1.0
                    elif row >= 0:
                        west[a, place, row * EDGE + col + EDGE] = 1.0
                    elif col >= 0:
                        south[place, (row + hr) * cols + col] = 1.0
                    else:
                        corner[place, (row + hr) * EDGE + col + EDGE] = 1.0
    return [jnp.asarray(m, BF) for m in (own, west, south, corner)]


def patch_matrix(cols):
    half = cols // 2
    mat = np.zeros((4 * half, 2 * cols), np.float32)
    for j in range(half):
        for g, (dr, dc) in enumerate(((0, 0), (1, 0), (0, 1), (1, 1))):
            mat[g * half + j, dr * cols + 2 * j + dc] = 1.0
    return mat


def lane_masks():
    lane = lax.broadcasted_iota(jnp.int32, (1, 128), 1)
    even = (lane < 64).astype(F32)
    return even.astype(BF), (1.0 - even).astype(BF)


def halo_rows(own_ref, west_ref, south_ref, corner_ref, po_ref, pw_ref, ps_ref, pc_ref, first):
    step = pl.program_id(0)
    block = po_ref.shape[2]
    half = block // 2
    start = pl.multiple_of(jnp.maximum(step * block - half, 0), 16)
    take = jnp.where(step == 0, 0, 1)
    value = dot_nn(po_ref[take], own_ref[pl.ds(start, block), :])
    value = value + dot_nn(pw_ref[0], west_ref[...])
    first[...] = value

    @pl.when(step == 0)
    def _():
        first[...] += dot_nn(ps_ref[...], south_ref[...]) + dot_nn(pc_ref[...], corner_ref[...])

    return first[...]


def stack_heads(value, masks):
    return jnp.concatenate([value * masks[0], value * masks[1]], axis=0)


def forward_kernel(stride, count_b, own_ref, west_ref, south_ref, corner_ref, po_ref, pw_ref, ps_ref,
                   pc_ref, allow_ref, gain_ref, w_ref, to_grid_ref,
                   att_ref, qkv_ref, normed_ref, prob_ref, lon_ref, lat_ref, corner_out_ref, first,
                   att_win_ref):
    features = own_ref.shape[1]
    x = halo_rows(own_ref, west_ref, south_ref, corner_ref, po_ref, pw_ref, ps_ref, pc_ref, first)
    average = jnp.mean(x, axis=-1, keepdims=True)
    centered = x - average
    variance = jnp.mean(centered * centered, axis=-1, keepdims=True)
    normed = (centered * lax.rsqrt(variance + EPSILON) * gain_ref[...]).astype(BF)
    normed_ref[...] = normed
    for t in range(3):
        qkv_ref[t] = dot_nn(normed, w_ref[:, features * t : features * (t + 1)]).astype(BF)
    allow = allow_ref[0] > 0.5
    masks = lane_masks()
    spans = [slice(b * stride, (b + 1) * stride) for b in range(count_b)]
    for pair in range(features // 128):
        lanes = pl.ds(128 * pair, 128)
        scores = []
        for rows in spans:
            q2 = qkv_ref[0, rows, lanes] * jnp.asarray(0.125, BF)
            scores.append(dot_nt(stack_heads(qkv_ref[1, rows, lanes], masks), q2))
        stacked = []
        for b, s2 in enumerate(scores):
            probs = []
            for h in range(2):
                s = jnp.where(allow, s2[h * stride : (h + 1) * stride], -1e30)
                e = jnp.exp(s - jnp.max(s, axis=0, keepdims=True))
                probs.append((e * (1.0 / jnp.sum(e, axis=0, keepdims=True))).astype(BF))
            p2 = jnp.concatenate(probs, axis=0)
            prob_ref[pair, pl.ds(2 * stride * b, 2 * stride), :] = p2
            stacked.append(p2)
        for rows, p2 in zip(spans, stacked):
            o2 = dot_tn(p2, stack_heads(qkv_ref[2, rows, lanes], masks))
            att_win_ref[rows, lanes] = o2.astype(BF)
    write_edges(dot_nn(to_grid_ref[...], att_win_ref[...]), att_ref, lon_ref, lat_ref, corner_out_ref)


def write_edges(values, out_ref, lon_ref, lat_ref, corner_ref):
    cols = values.shape[0] // WLAT
    out_ref[...] = values.astype(out_ref.dtype)
    edge = jnp.concatenate([values[r * cols : r * cols + EDGE] for r in range(WLAT)], axis=0).astype(BF)
    lon_ref[...] = edge

    @pl.when(pl.program_id(0) == 0)
    def _():
        lat_ref[...] = values[: lat_ref.shape[0]].astype(BF)
        corner_ref[...] = edge[: corner_ref.shape[0]]


def assemble_kernel(own_ref, west_ref, south_ref, corner_ref, po_ref, pw_ref, ps_ref, pc_ref, out_ref,
                    first):
    out_ref[...] = halo_rows(own_ref, west_ref, south_ref, corner_ref, po_ref, pw_ref, ps_ref, pc_ref,
                             first).astype(BF)


def middle_kernel(cols, tok_ref, att_ref, w_out_ref, gain_ref, grad_in_ref, to_patch_ref,
                  from_patch_ref, merged_in_ref, grad_mixed_ref, grad_att_ref, lon_ref, lat_ref,
                  corner_ref):
    tokens, features = tok_ref.shape
    pairs = tokens // (2 * cols)
    half = cols // 2
    mixed = (tok_ref[...].astype(F32) + dot_nn(att_ref[...], w_out_ref[...])).astype(BF)
    parts = [dot_nn(to_patch_ref[...], mixed[2 * cols * i : 2 * cols * (i + 1)]) for i in range(pairs)]
    groups = [
        jnp.concatenate([part[half * g : half * (g + 1)] for part in parts], axis=0) for g in range(4)
    ]
    width = 4 * features
    average = sum(jnp.sum(v, axis=-1, keepdims=True) for v in groups) / width
    groups = [v - average for v in groups]
    variance = sum(jnp.sum(v * v, axis=-1, keepdims=True) for v in groups) / width
    inv = lax.rsqrt(variance + EPSILON)
    groups = [v * inv for v in groups]
    grads = []
    for g in range(4):
        span = slice(features * g, features * (g + 1))
        gain = gain_ref[:, span]
        merged_in_ref[:, span] = (groups[g] * gain).astype(BF)
        grads.append(grad_in_ref[:, span].astype(F32) * gain)
    mean_one = sum(jnp.sum(v, axis=-1, keepdims=True) for v in grads) / width
    mean_two = sum(
        jnp.sum(v * h, axis=-1, keepdims=True) for v, h in zip(grads, groups)
    ) / width
    outs = [(v - mean_one - h * mean_two) * inv for v, h in zip(grads, groups)]
    for i in range(pairs):
        piece = jnp.concatenate([v[half * i : half * (i + 1)] for v in outs], axis=0).astype(BF)
        back = dot_nn(from_patch_ref[...], piece).astype(BF)
        grad_mixed_ref[pl.ds(2 * cols * i, 2 * cols), :] = back
    grad_att = dot_nt(grad_mixed_ref[...], w_out_ref[...])
    grad_att_ref[...] = grad_att.astype(BF)
    edge = [grad_att[r * cols - EDGE : r * cols] for r in range(1, tokens // cols + 1)]
    lon_ref[...] = jnp.concatenate(edge, axis=0).astype(BF)

    @pl.when(pl.program_id(0) == pl.num_programs(0) - 1)
    def _():
        lat_ref[...] = grad_att[tokens - lat_ref.shape[0] :].astype(BF)
        corner_ref[...] = jnp.concatenate(edge[-(WLAT // 2) :], axis=0).astype(BF)


def grad_in_kernel(gm_ref, w_merge_ref, out_ref):
    out_ref[...] = dot_nt(gm_ref[...], w_merge_ref[...]).astype(BF)


def merge_grad_kernel(merged_in_ref, gm_ref, att_ref, gmix_ref, out_ref):
    step = pl.program_id(0)
    last = pl.num_programs(0) - 1
    height = out_ref.shape[0]
    narrow = gmix_ref.shape[1]

    @pl.when(step < last)
    def _():
        out_ref[...] = dot_tn(merged_in_ref[...], gm_ref[...]).astype(BF)

    @pl.when(step == last)
    def _():
        for k in range(att_ref.shape[1] // height):
            part = dot_tn(att_ref[:, height * k : height * (k + 1)], gmix_ref[...])
            out_ref[:, narrow * k : narrow * (k + 1)] = part.astype(BF)


def backward_kernel(stride, count_b, ga_ref, qkv_ref, prob_ref, prev_ref, gqkv_ref):
    del prev_ref
    masks = lane_masks()
    low = lax.broadcasted_iota(jnp.int32, (1, 128), 1) < 64
    spans = [slice(b * stride, (b + 1) * stride) for b in range(count_b)]
    for pair in range(ga_ref.shape[1] // 128):
        lanes = pl.ds(128 * pair, 128)
        work = []
        for b, rows in enumerate(spans):
            do2 = ga_ref[rows, lanes]
            p2 = prob_ref[pair, pl.ds(2 * stride * b, 2 * stride), :]
            dp2 = dot_nt(stack_heads(qkv_ref[2, rows, lanes], masks), do2)
            dv = dot_nn(p2, do2)
            gqkv_ref[2, rows, lanes] = jnp.where(low, dv[:stride], dv[stride:]).astype(BF)
            work.append((p2, dp2))
        scores = []
        for p2, dp2 in work:
            grads = []
            for h in range(2):
                p = p2[h * stride : (h + 1) * stride].astype(F32)
                dp = dp2[h * stride : (h + 1) * stride]
                grads.append((p * (dp - jnp.sum(dp * p, axis=0, keepdims=True))).astype(BF))
            scores.append(jnp.concatenate(grads, axis=0))
        for rows, ds2 in zip(spans, scores):
            q2 = qkv_ref[0, rows, lanes] * jnp.asarray(0.125, BF)
            dk = dot_nn(ds2, q2)
            dq = dot_tn(ds2, stack_heads(qkv_ref[1, rows, lanes], masks))
            gqkv_ref[0, rows, lanes] = (dq * 0.125).astype(BF)
            gqkv_ref[1, rows, lanes] = jnp.where(low, dk[:stride], dk[stride:]).astype(BF)


def qkv_grad_kernel(normed_ref, gqkv_ref, out_ref):
    for t in range(3):
        out_ref[t] = dot_tn(normed_ref[...], gqkv_ref[t]).astype(BF)


def input_grad_kernel(gqkv_ref, x_ref, gain_ref, w_ref, to_grid_ref, out_ref, lon_ref, lat_ref,
                      corner_ref):
    features = x_ref.shape[1]
    grad = sum(dot_nt(gqkv_ref[t], w_ref[:, features * t : features * (t + 1)]) for t in range(3))
    grad = dot_nn(to_grid_ref[...], grad.astype(BF))
    x = x_ref[...].astype(F32)
    centered = x - jnp.mean(x, axis=-1, keepdims=True)
    inv = lax.rsqrt(jnp.mean(centered * centered, axis=-1, keepdims=True) + EPSILON)
    hat = centered * inv
    grad = grad * gain_ref[...]
    one = jnp.mean(grad, axis=-1, keepdims=True)
    two = jnp.mean(grad * hat, axis=-1, keepdims=True)
    write_edges((grad - one - hat * two) * inv, out_ref, lon_ref, lat_ref, corner_ref)


def merged_kernel(a_ref, w_ref, out_ref):
    out_ref[...] = dot_nn(a_ref[...], w_ref[...]).astype(BF)


def whole(shape):
    return pl.BlockSpec(shape, lambda i: (0,) * len(shape))


def rows_of(height, width):
    return pl.BlockSpec((height, width), lambda i: (i, 0))


def shift_pairs(count_lat, count_lon, dlat, dlon):
    return [
        (a * count_lon + b, ((a + dlat) % count_lat) * count_lon + (b + dlon) % count_lon)
        for a in range(count_lat)
        for b in range(count_lon)
    ]


def send(value, dlat, dlon):
    pairs = shift_pairs(lax.axis_size("lat"), lax.axis_size("lon"), dlat, dlon)
    return lax.ppermute(value, ("lat", "lon"), pairs)


def exchange(parts, sign):
    lon_edge, lat_edge, corner = parts
    lon_edge = send(lon_edge, 0, sign)
    lat_edge = send(lat_edge, sign, 0)
    corner = send(corner, sign, sign)
    return lon_edge, lat_edge, corner


def edges(values):
    rows, cols, features = values.shape
    hr = WLAT // 2
    parts = (values[:, cols - EDGE :], values[rows - hr :], values[rows - hr :, cols - EDGE :])
    return [v.reshape(-1, features) for v in parts]


def to_shifted(values, parts):
    rows, cols, features = values.shape
    hr, hc = WLAT // 2, WLON // 2
    west, south, corner = parts
    corner = corner.reshape(hr, EDGE, features)[:, EDGE - hc :]
    top = jnp.concatenate([corner, south.reshape(hr, cols, features)[:, : cols - hc]], 1)
    west = west.reshape(rows, EDGE, features)[: rows - hr, EDGE - hc :]
    bottom = jnp.concatenate([west, values[: rows - hr, : cols - hc]], 1)
    return jnp.concatenate([top, bottom], axis=0)


def to_own(values, parts):
    rows, cols, features = values.shape
    hr, hc = WLAT // 2, WLON // 2
    east, north, corner = (v.astype(values.dtype) for v in parts)
    top = jnp.concatenate([values[hr:, hc:], east.reshape(rows, EDGE, features)[hr:, :hc]], axis=1)
    north = north.reshape(hr, cols, features)[:, hc:]
    bottom = jnp.concatenate([north, corner.reshape(hr, EDGE, features)[:, :hc]], axis=1)
    return jnp.concatenate([top, bottom], axis=0)


def part_sum(terms, index, height):
    parts = [lax.dynamic_slice_in_dim(t, index * height, height, 0).astype(F32) for t in terms]
    return sum(parts[1:], parts[0]).astype(BF)


def join(value, received, keep):
    first = jnp.where(keep == 0, value, received)
    second = jnp.where(keep == 0, received, value)
    return jnp.concatenate([first, second], axis=0)


def reduce_all(value):
    count_lat, count_lon = lax.axis_size("lat"), lax.axis_size("lon")
    bits = count_lon.bit_length() - 1
    me, lat = lax.axis_index("lon"), lax.axis_index("lat")
    odd = lax.rem(me, 2)
    plans = [([(i, i ^ 1) for i in range(count_lon)], odd)]
    for k in range(bits - 1):
        low, high = 2 << k, 2 << (bits - 2 - k)
        pairs = [(i, i ^ (low if i % 2 == 0 else high)) for i in range(count_lon)]
        keep = jnp.where(odd == 0, lax.rem(me // low, 2), lax.rem(me // high, 2))
        plans.append((pairs, keep))
    terms, height = [value], value.shape[0]
    for pairs, keep in plans:
        height = height // 2
        sent = part_sum(terms, 1 - keep, height)
        received = lax.ppermute(sent, "lon", pairs)
        terms = [lax.dynamic_slice_in_dim(t, keep * height, height, 0) for t in terms] + [received]
    height = height // count_lat
    total = [lax.dynamic_slice_in_dim(t, lat * height, height, 0).astype(F32) for t in terms]
    for d in range(1, count_lat):
        sent = part_sum(terms, lat ^ d, height)
        received = lax.ppermute(sent, "lat", [(i, i ^ d) for i in range(count_lat)])
        total.append(received.astype(F32))
    mine = sum(total[1:], total[0]).astype(BF)
    value = jnp.zeros((count_lat * height,) + mine.shape[1:], BF)
    value = lax.dynamic_update_slice_in_dim(value, mine, lat * height, 0)
    for d in range(1, count_lat):
        received = lax.ppermute(mine, "lat", [(i, i ^ d) for i in range(count_lat)])
        value = lax.dynamic_update_slice_in_dim(value, received, (lat ^ d) * height, 0)
    for k, (pairs, keep) in reversed(list(enumerate(plans))):
        received = lax.ppermute(value, "lon", pairs)
        value = join(value, received, keep)
    return value


def on_device_body(tokens, lat_band, gain_attn, w_qkv, w_out, gain_merge, w_merge, grad_merged):
    rows, cols, features = tokens.shape
    width2 = grad_merged.shape[2]
    count_a, count_b = rows // WLAT, cols // WLON
    window = WLAT * WLON
    stride = -(-window // 16) * 16
    half_lat = WLAT // 2
    block = WLAT * cols
    padded = count_b * stride
    total = rows * cols
    to_grid = jnp.asarray(window_matrix(cols, stride).T, BF)
    patch_np = patch_matrix(cols)
    to_patch = jnp.asarray(patch_np, BF)
    from_patch = jnp.asarray(patch_np.T, BF)

    band_count = lat_band.shape[0]
    extended = jnp.concatenate([lat_band[band_count - half_lat :], lat_band])
    band_rows = lax.dynamic_slice_in_dim(extended, lax.axis_index("lat") * rows, rows)
    labels = jnp.repeat(band_rows.reshape(count_a, WLAT), WLON, axis=1)
    labels = jnp.pad(labels, ((0, 0), (0, stride - window)), constant_values=-1)
    allow = (labels[:, :, None] == labels[:, None, :]).astype(F32)
    gain_a = gain_attn.reshape(1, features)
    gain_m = gain_merge.reshape(1, 4 * features)

    own_tok = tokens.reshape(total, features)
    mats = halo_matrices(rows, cols, stride)
    edge_shapes = [(rows * EDGE, features), (half_lat * cols, features), (half_lat * EDGE, features)]
    edge_types = [jax.ShapeDtypeStruct(shape, BF) for shape in edge_shapes]
    edge_specs = [rows_of(WLAT * EDGE, features), whole(edge_shapes[1]), whole(edge_shapes[2])]
    halo_specs = [whole((total, features))] + [whole(shape) for shape in edge_shapes] + [
        whole(mats[0].shape), pl.BlockSpec((1,) + mats[1].shape[1:], lambda i: (i, 0, 0)),
        whole(mats[2].shape), whole(mats[3].shape)]
    tok_halos = exchange(edges(tokens), 1)
    allow_spec = pl.BlockSpec((1, stride, stride), lambda i: (i, 0, 0))
    pairs = features // 128
    tall3 = count_a * padded
    qkv_spec = pl.BlockSpec((3, padded, features), lambda i: (0, i, 0))
    prob_rows = 2 * stride * count_b
    attended, qkv, normed, probs, *att_edges = pl.pallas_call(
        functools.partial(forward_kernel, stride, count_b),
        grid=(count_a,),
        in_specs=halo_specs + [allow_spec, whole((1, features)), whole((features, 3 * features)),
                               whole((block, padded))],
        out_specs=[rows_of(block, features), qkv_spec, rows_of(padded, features),
                   pl.BlockSpec((pairs, prob_rows, stride), lambda i: (0, i, 0))] + edge_specs,
        out_shape=[jax.ShapeDtypeStruct((total, features), BF),
                   jax.ShapeDtypeStruct((3, tall3, features), BF),
                   jax.ShapeDtypeStruct((tall3, features), BF),
                   jax.ShapeDtypeStruct((pairs, count_a * prob_rows, stride), BF)] + edge_types,
        scratch_shapes=[pltpu.VMEM((padded, features), F32), pltpu.VMEM((padded, features), BF)],
        compiler_params=params(1),
        cost_estimate=cost(4 * total * features * 3 * features, 2 * total * features * 8),
        name="attn_fwd",
    )(own_tok, *tok_halos, *mats, allow, gain_a, w_qkv, to_grid)

    att_parts = exchange(att_edges, -1)
    own_att = to_own(attended.reshape(rows, cols, features), att_parts).reshape(total, features)
    gm = grad_merged.reshape(total // 4, width2)
    grad_in = pl.pallas_call(
        grad_in_kernel,
        grid=(4,),
        in_specs=[whole((total // 4, width2)), rows_of(features, width2)],
        out_specs=pl.BlockSpec((total // 4, features), lambda i: (0, i)),
        out_shape=jax.ShapeDtypeStruct((total // 4, 4 * features), BF),
        compiler_params=params(1),
        cost_estimate=cost(2 * total * features * width2, 2 * total * features * 4),
        name="grad_in",
    )(gm, w_merge)

    steps = 2
    tall = total // steps
    short = tall // 4
    merged_in, grad_mixed, grad_att, *grad_edges = pl.pallas_call(
        functools.partial(middle_kernel, cols),
        grid=(steps,),
        in_specs=[rows_of(tall, features), rows_of(tall, features), whole((features, features)),
                  whole((1, 4 * features)), rows_of(short, 4 * features),
                  whole((2 * cols, 2 * cols)), whole((2 * cols, 2 * cols))],
        out_specs=[rows_of(short, 4 * features), rows_of(tall, features), rows_of(tall, features),
                   rows_of(edge_shapes[0][0] // steps, features)] + edge_specs[1:],
        out_shape=[jax.ShapeDtypeStruct((total // 4, 4 * features), BF),
                   jax.ShapeDtypeStruct((total, features), BF),
                   jax.ShapeDtypeStruct((total, features), BF)] + edge_types,
        compiler_params=params(1),
        cost_estimate=cost(8 * total * features * features, 2 * total * features * 6),
        name="merge_mid",
    )(own_tok, own_att, w_out, gain_m, grad_in, to_patch, from_patch)

    att_halos = exchange(grad_edges, 1)
    rest = features * features // width2
    pieces = 4 * features // rest
    dw_merge = pl.pallas_call(
        merge_grad_kernel,
        grid=(pieces + 1,),
        in_specs=[pl.BlockSpec((total // 4, rest), lambda i: (0, jnp.minimum(i, pieces - 1))),
                  whole((total // 4, width2)), whole((total, features)), whole((total, features))],
        out_specs=rows_of(rest, width2),
        out_shape=jax.ShapeDtypeStruct((4 * features + rest, width2), BF),
        compiler_params=params(1),
        cost_estimate=cost(4 * total * features * features * 2, 2 * total * features * 6),
        name="merge_dw",
    )(merged_in, gm, own_att, grad_mixed)
    sum_merge = reduce_all(dw_merge)

    grad_win = pl.pallas_call(
        assemble_kernel,
        grid=(count_a,),
        in_specs=halo_specs,
        out_specs=rows_of(padded, features),
        out_shape=jax.ShapeDtypeStruct((tall3, features), BF),
        scratch_shapes=[pltpu.VMEM((padded, features), F32)],
        compiler_params=params(1),
        cost_estimate=cost(total * features * 1200, 2 * total * features * 3),
        name="assemble",
    )(grad_att, *att_halos, *mats)
    calls = CALLS
    wide = features // calls
    grad_qkv = None
    for j in range(calls):
        spec = pl.BlockSpec((3, padded, wide), lambda i, j=j: (0, i, j))
        operands = [grad_win, qkv, probs]
        specs = [pl.BlockSpec((padded, wide), lambda i, j=j: (i, j)), spec,
                 pl.BlockSpec((pairs // calls, prob_rows, stride), lambda i, j=j: (j, i, 0))]
        if grad_qkv is not None:
            operands.append(grad_qkv)
            specs.append(pl.BlockSpec(memory_space=pl.ANY))
            body = functools.partial(backward_kernel, stride, count_b)
        else:
            def body(ga_ref, qkv_ref, prob_ref, gqkv_ref):
                backward_kernel(stride, count_b, ga_ref, qkv_ref, prob_ref, None, gqkv_ref)
        grad_qkv = pl.pallas_call(
            body,
            grid=(count_a,),
            in_specs=specs,
            out_specs=spec,
            out_shape=jax.ShapeDtypeStruct((3, tall3, features), BF),
            input_output_aliases={3: 0} if j else {},
            compiler_params=params(1),
            cost_estimate=cost(4 * total * features * 3 * features // calls,
                               2 * total * features * 8 // calls),
        )(*operands)
    dw_q = pl.pallas_call(
        qkv_grad_kernel,
        grid=(2,),
        in_specs=[pl.BlockSpec((tall3, features // 2), lambda i: (0, i)),
                  whole((3, tall3, features))],
        out_specs=pl.BlockSpec((3, features // 2, features), lambda i: (0, i, 0)),
        out_shape=jax.ShapeDtypeStruct((3, features, features), BF),
        compiler_params=params(1),
        cost_estimate=cost(2 * total * features * 3 * features, 2 * total * features * 5),
        name="qkv_dw",
    )(normed, grad_qkv)
    sum_q = reduce_all(dw_q.reshape(3 * features, features)).reshape(3, features, features)

    shifted = to_shifted(tokens, tok_halos).reshape(total, features)
    grad_inputs, *in_edges = pl.pallas_call(
        input_grad_kernel,
        grid=(count_a,),
        in_specs=[qkv_spec, rows_of(block, features), whole((1, features)),
                  whole((features, 3 * features)), whole((block, padded))],
        out_specs=[rows_of(block, features)] + edge_specs,
        out_shape=[jax.ShapeDtypeStruct((total, features), F32)] + edge_types,
        compiler_params=params(1),
        cost_estimate=cost(2 * total * features * 3 * features, 2 * total * features * 6),
        name="input_grad",
    )(grad_qkv, shifted, gain_a, w_qkv, to_grid)
    in_parts = exchange(in_edges, -1)
    grad_own = to_own(grad_inputs.reshape(rows, cols, features), in_parts)
    grad_tokens = grad_own + grad_mixed.reshape(rows, cols, features).astype(F32)

    merged = pl.pallas_call(
        merged_kernel,
        grid=(2,),
        in_specs=[rows_of(total // 8, 4 * features), whole((4 * features, width2))],
        out_specs=rows_of(total // 8, width2),
        out_shape=jax.ShapeDtypeStruct((total // 4, width2), BF),
        compiler_params=params(1),
        cost_estimate=cost(2 * total * features * width2, 2 * total * features * 4),
        name="merged",
    )(merged_in, w_merge).reshape(grad_merged.shape)

    grad_w_merge = sum_merge[: 4 * features].astype(F32)
    grad_w_out = jnp.concatenate(
        [sum_merge[4 * features :, k * features : (k + 1) * features] for k in range(features // rest)], 0
    ).astype(F32)
    grad_w_qkv = jnp.concatenate([sum_q[t] for t in range(3)], axis=1).astype(F32)
    grad_gain_merge = jnp.sum(grad_w_merge * w_merge.astype(F32), axis=1) / gain_merge
    grad_gain_attn = jnp.sum(grad_w_qkv * w_qkv.astype(F32), axis=1) / gain_attn
    return (merged, grad_tokens, grad_gain_attn, grad_w_qkv, grad_w_out, grad_gain_merge,
            grad_w_merge)


def solution(mesh):
    return jax.shard_map(
        on_device_body,
        mesh=mesh,
        in_specs=(P("lat", "lon", None), P(), P(), P(), P(), P(), P(), P("lat", "lon", None)),
        out_specs=(P("lat", "lon", None), P("lat", "lon", None), P(), P(), P(), P(), P()),
        check_vma=False,
    )
```

profile of v0, /device:TPU:0, one launch (start us, length us, event | category | flops | bytes accessed | tf_op | source)
XLA Modules:
  0.0 235.7 jit_solution(12535973746034990042)
XLA Ops:
  3.0 2.6 %collective-permute-start.1 = (bf16[144,512]{1,0:T(8,128)(2,1)S(1)}, bf16[144,512]{1,0:T(8,128)(2,1)S(1)}, u32[]{:S(2)}, u32[]{:S(2)}) collective-permute-start(bf16[144,512]{1,0:T(8,128)(2,1)S(1)} %bitcast.49), channel_id=1, source_target_pairs={{0,8},{1,9},{2,10},{3,11},{4,12},{5,13},{6,14},{7,15},{8,16},{9,17... | collective-permute-start | bytes 442376 | tf_op jit(solution)/shard_map/ppermute | solution.py:309
  6.4 2.5 %collective-permute-start.2 = (bf16[24,512]{1,0:T(8,128)(2,1)S(1)}, bf16[24,512]{1,0:T(8,128)(2,1)S(1)}, u32[]{:S(2)}, u32[]{:S(2)}) collective-permute-start(bf16[24,512]{1,0:T(8,128)(2,1)S(1)} %slice_bitcast_fusion.1), channel_id=1, source_target_pairs={{0,9},{1,10},{2,11},{3,12},{4,13},{5,14},{6,15},{7,8},{8,17},{9,18... | collective-permute-start | bytes 73736 | tf_op jit(solution)/shard_map/ppermute | solution.py:309
  11.5 2.9 %collective-permute-done.2.corner_ref = bf16[24,512]{1,0:T(8,128)(2,1)S(1)} collective-permute-done((bf16[24,512]{1,0:T(8,128)(2,1)S(1)}, bf16[24,512]{1,0:T(8,128)(2,1)S(1)}, u32[]{:S(2)}, u32[]{:S(2)}) %collective-permute-start.2) | collective-permute-done | bytes 24608 | tf_op jit(solution)/shard_map/ppermute | solution.py:309
  15.1 16.1 %attn_fwd.1 = (bf16[1152,512]{1,0:T(8,128)(2,1)}, bf16[3,1280,512]{2,1,0:T(8,128)(2,1)}, bf16[1280,512]{1,0:T(8,128)(2,1)}, bf16[4,2560,80]{2,1,0:T(8,128)(2,1)}...) custom-call(bf16[1152,512]{1,0:T(8,128)(2,1)} %bitcast.36, ...), custom_call_target="tpu_custom_call" | custom-call | flops 3623878656 | bytes 9437184 | tf_op jit(solution)/shard_map/attn_fwd/pallas_call | solution.py:432
  31.9 1.7 collective-permute-start.4
  34.0 5.2 %grad_in.1.grad_in_ref = bf16[288,2048]{1,0:T(8,128)(2,1)} custom-call(bf16[288,1024]{1,0:T(8,128)(2,1)} %bitcast.42, bf16[2048,1024]{1,0:T(8,128)(2,1)} %w_ref.4), custom_call_target="tpu_custom_call" | custom-call | flops 1207959552 | bytes 4718592 | tf_op jit(solution)/shard_map/grad_in/pallas_call | solution.py:452
  39.7 1.2 maximum_maximum_fusion
  40.9 6.8 %merge_mid.1 = (bf16[288,2048]{1,0:T(8,128)(2,1)}, bf16[1152,512]{1,0:T(8,128)(2,1)}, bf16[1152,512]{1,0:T(8,128)(2,1)}, bf16[192,512]{1,0:T(8,128)(2,1)}, bf16[...) custom-call(bf16[1152,512]{1,0:T(8,128)(2,1)} %bitcast.37, bf16[1152,512]{1,0:T(8,128)(2,1)} %bitcast.38, ...), custom_call_target="tpu_custom_call" | custom-call | flops 2415919104 | bytes 7077888 | tf_op jit(solution)/shard_map/merge_mid/pallas_call | solution.py:466
  47.7 9.6 %merge_dw.1 = bf16[2304,1024]{1,0:T(8,128)(2,1)} custom-call(bf16[288,2048]{1,0:T(8,128)(2,1)} %get-tuple-element.28.a_ref.merged_in_ref, bf16[288,1024]{1,0:T(8,128)(2,1)} %bitcast.43, bf16[1152,512]{1,0:T(8,128)(2,1)} %bitcast.39, bf16[1152,512]{1,0:T(8,128)(2,1)} %get-tuple-element.39.gmix_ref), custom_call_target="tpu_custom_call" | custom-call | flops 2415919104 | bytes 7077888 | tf_op jit(solution)/shard_map/merge_dw/pallas_call | solution.py:485
  57.3 1.9 constant_dynamic-slice_fusion
  59.5 4.4 %collective-permute-done.24 = bf16[1152,1024]{1,0:T(8,128)(2,1)} collective-permute-done((bf16[1152,1024]{1,0:T(8,128)(2,1)S(1)}, bf16[1152,1024]{1,0:T(8,128)(2,1)}, u32[]{:S(2)}, u32[]{:S(2)}) %collective-permute-start.24) | collective-permute-done | bytes 2359328 | tf_op jit(solution)/shard_map/ppermute | solution.py:374
  63.9 2.1 add_convert_fusion
  66.9 15.4 %collective-permute-done.25 = bf16[576,1024]{1,0:T(8,128)(2,1)S(1)} collective-permute-done((bf16[576,1024]{1,0:T(8,128)(2,1)S(1)}, bf16[576,1024]{1,0:T(8,128)(2,1)S(1)}, u32[]{:S(2)}, u32[]{:S(2)}) %collective-permute-start.25) | collective-permute-done | bytes 1179680 | tf_op jit(solution)/shard_map/ppermute | solution.py:374
  82.3 1.6 add_convert_fusion.1
  84.7 1.5 collective-permute-start.7
  86.2 1.4 collective-permute-start.8
  87.6 7.3 %collective-permute-done.8.corner_ref = bf16[24,512]{1,0:T(8,128)(2,1)S(1)} collective-permute-done((bf16[24,512]{1,0:T(8,128)(2,1)S(1)}, bf16[24,512]{1,0:T(8,128)(2,1)S(1)}, u32[]{:S(2)}, u32[]{:S(2)}) %collective-permute-start.8) | collective-permute-done | bytes 24608 | tf_op jit(solution)/shard_map/ppermute | solution.py:309
  95.7 5.3 %assemble.1.ga_ref = bf16[1280,512]{1,0:T(8,128)(2,1)} custom-call(bf16[1152,512]{1,0:T(8,128)(2,1)} %get-tuple-element.29.own_ref, bf16[192,512]{1,0:T(8,128)(2,1)} %copy-done.6, bf16[144,512]{1,0:T(8,128)(2,1)} %copy-done.11, bf16[24,512]{1,0:T(8,128)(2,1)} %copy-done.12, bf16[2,320,288]{2,1,0:T(8,128)(2,1)} %constant.423.clone.po_ref, ...), custom_call_target="tpu_custom_call" | custom-call | flops 707788800 | bytes 3538944 | tf_op jit(solution)/shard_map/assemble/pallas_call | solution.py:498
  101.0 4.5 %shard_map.198.prev_ref = bf16[3,1280,512]{2,1,0:T(8,128)(2,1)} custom-call(bf16[1280,512]{1,0:T(8,128)(2,1)} %assemble.1.ga_ref, bf16[3,1280,512]{2,1,0:T(8,128)(2,1)} %get-tuple-element.33.qkv_ref, bf16[4,2560,80]{2,1,0:T(8,128)(2,1)} %get-tuple-element.34.prob_ref), custom_call_target="tpu_custom_call" | custom-call | flops 905969664 | bytes 2359296 | tf_op jit(solution)/shard_map/pallas_call | solution.py:524
  105.6 4.6 %shard_map.199.prev_ref = bf16[3,1280,512]{2,1,0:T(8,128)(2,1)} custom-call(bf16[1280,512]{1,0:T(8,128)(2,1)} %assemble.1.ga_ref, bf16[3,1280,512]{2,1,0:T(8,128)(2,1)} %get-tuple-element.33.qkv_ref, bf16[4,2560,80]{2,1,0:T(8,128)(2,1)} %get-tuple-element.34.prob_ref, bf16[3,1280,512]{2,1,0:T(8,128)(2,1)} %shard_map.198.prev_ref), custom_call_target="tpu_custom_call", output_to_operand_aliasing={{}: (3, {})} | custom-call | flops 905969664 | bytes 2359296 | tf_op jit(solution)/shard_map/pallas_call | solution.py:524
  110.1 1.7 add_convert_fusion.7
  111.9 2.3 collective-permute-start.29
  114.8 1.5 collective-permute-start.27
  116.3 4.5 %shard_map.200.prev_ref = bf16[3,1280,512]{2,1,0:T(8,128)(2,1)} custom-call(bf16[1280,512]{1,0:T(8,128)(2,1)} %assemble.1.ga_ref, bf16[3,1280,512]{2,1,0:T(8,128)(2,1)} %get-tuple-element.33.qkv_ref, bf16[4,2560,80]{2,1,0:T(8,128)(2,1)} %get-tuple-element.34.prob_ref, bf16[3,1280,512]{2,1,0:T(8,128)(2,1)} %shard_map.199.prev_ref), custom_call_target="tpu_custom_call", output_to_operand_aliasing={{}: (3, {})} | custom-call | flops 905969664 | bytes 2359296 | tf_op jit(solution)/shard_map/pallas_call | solution.py:524
  120.8 4.5 %shard_map.201.gqkv_ref = bf16[3,1280,512]{2,1,0:T(8,128)(2,1)} custom-call(bf16[1280,512]{1,0:T(8,128)(2,1)} %assemble.1.ga_ref, bf16[3,1280,512]{2,1,0:T(8,128)(2,1)} %get-tuple-element.33.qkv_ref, bf16[4,2560,80]{2,1,0:T(8,128)(2,1)} %get-tuple-element.34.prob_ref, bf16[3,1280,512]{2,1,0:T(8,128)(2,1)} %shard_map.200.prev_ref), custom_call_target="tpu_custom_call", output_to_operand_aliasing={{}: (3, {})} | custom-call | flops 905969664 | bytes 2359296 | tf_op jit(solution)/shard_map/pallas_call | solution.py:524
  126.2 1.2 constant_dynamic-update-slice_fusion.5
  127.5 5.7 %qkv_dw.1 = bf16[3,512,512]{2,1,0:T(8,128)(2,1)} custom-call(bf16[1280,512]{1,0:T(8,128)(2,1)} %get-tuple-element.40.normed_ref, bf16[3,1280,512]{2,1,0:T(8,128)(2,1)} %shard_map.201.gqkv_ref), custom_call_target="tpu_custom_call" | custom-call | flops 1811939328 | bytes 5898240 | tf_op jit(solution)/shard_map/qkv_dw/pallas_call | solution.py:535
  133.1 2.8 %collective-permute-start.31 = (bf16[72,1024]{1,0:T(8,128)(2,1)S(1)}, bf16[72,1024]{1,0:T(8,128)(2,1)S(1)}, u32[]{:S(2)}, u32[]{:S(2)}) collective-permute-start(bf16[72,1024]{1,0:T(8,128)(2,1)S(1)} %get-tuple-element.44), channel_id=1, source_target_pairs={{0,16},{8,24},{16,0},{24,8},{1,17},{9,25},{17,1},{25,9},{2,18},{10... | collective-permute-start | bytes 442376 | tf_op jit(solution)/shard_map/ppermute | solution.py:386
  136.0 1.2 constant_dynamic-slice_fusion.1
  137.2 1.6 collective-permute-start.32
  138.8 7.1 %collective-permute-done.31 = bf16[72,1024]{1,0:T(8,128)(2,1)S(1)} collective-permute-done((bf16[72,1024]{1,0:T(8,128)(2,1)S(1)}, bf16[72,1024]{1,0:T(8,128)(2,1)S(1)}, u32[]{:S(2)}, u32[]{:S(2)}) %collective-permute-start.31) | collective-permute-done | bytes 147488 | tf_op jit(solution)/shard_map/ppermute | solution.py:386
  145.9 1.1 collective-permute-start.33
  147.0 1.9 add_convert_fusion.2
  148.9 1.1 collective-permute-start.13
  150.0 10.2 %collective-permute-done.33 = bf16[288,1024]{1,0:T(8,128)(2,1)} collective-permute-done((bf16[288,1024]{1,0:T(8,128)(2,1)S(1)}, bf16[288,1024]{1,0:T(8,128)(2,1)}, u32[]{:S(2)}, u32[]{:S(2)}) %collective-permute-start.33) | collective-permute-done | bytes 589856 | tf_op jit(solution)/shard_map/ppermute | solution.py:389
  160.2 1.1 broadcast_select_fusion.7
  161.4 1.1 pad_maximum_fusion.3
  162.5 2.5 %collective-permute-start.34 = (bf16[576,1024]{1,0:T(8,128)(2,1)}, bf16[576,1024]{1,0:T(8,128)(2,1)}, u32[]{:S(2)}, u32[]{:S(2)}) collective-permute-start(bf16[576,1024]{1,0:T(8,128)(2,1)} %pad_maximum_fusion.3), channel_id=1, source_target_pairs={{0,2},{1,5},{2,0},{3,7},{4,6},{5,1},{6,4},{7,3},{8,10},{9,13},{10,... | collective-permute-start | bytes 3538952 | tf_op jit(solution)/shard_map/ppermute | solution.py:389
  164.9 1.2 add_convert_fusion.3
  167.1 6.8 %collective-permute-done.14 = bf16[192,512]{1,0:T(8,128)(2,1)S(1)} collective-permute-done((bf16[192,512]{1,0:T(8,128)(2,1)S(1)}, bf16[192,512]{1,0:T(8,128)(2,1)S(1)}, u32[]{:S(2)}, u32[]{:S(2)}) %collective-permute-start.14) | collective-permute-done | bytes 196640 | tf_op jit(solution)/shard_map/ppermute | solution.py:374
  173.9 1.1 add_convert_fusion.11
  175.3 2.8 %collective-permute-start.16 = (bf16[48,512]{1,0:T(8,128)(2,1)S(1)}, bf16[48,512]{1,0:T(8,128)(2,1)S(1)}, u32[]{:S(2)}, u32[]{:S(2)}) collective-permute-start(bf16[48,512]{1,0:T(8,128)(2,1)S(1)} %get-tuple-element.56), channel_id=1, source_target_pairs={{0,16},{8,24},{16,0},{24,8},{1,17},{9,25},{17,1},{25,9},{2,18},{10... | collective-permute-start | bytes 147464 | tf_op jit(solution)/shard_map/ppermute | solution.py:380
  178.1 1.4 collective-permute-start.15
  179.5 2.0 collective-permute-done.17
  181.5 1.2 collective-permute-done.16
  184.6 1.4 collective-permute-start.19
  186.0 2.1 collective-permute-start.20
  188.1 1.5 collective-permute-done.19
  189.6 2.3 collective-permute-done.20
  191.9 1.2 collective-permute-start.21
  193.1 2.0 broadcast_select_fusion.3
  195.1 1.6 pad_maximum_fusion.1
  198.8 1.6 maximum_maximum_fusion.1
  200.4 7.6 %input_grad.1 = (f32[1152,512]{1,0:T(8,128)}, bf16[192,512]{1,0:T(8,128)(2,1)}, bf16[144,512]{1,0:T(8,128)(2,1)}, bf16[24,512]{1,0:T(8,128)(2,1)}) custom-call(bf16[3,1280,512]{2,1,0:T(8,128)(2,1)} %shard_map.201.gqkv_ref, bf16[1152,512]{1,0:T(8,128)(2,1)} %bitcast.34, f32[1,512]{1,0:T(1,128)} %bitcast.54, bf16[512,1536]{1,0:T(8,128)(2,1)} %w_ref.5, ...), custom_call_target="tpu_custom_call" | custom-call | flops 1811939328 | bytes 7077888 | tf_op jit(solution)/shard_map/input_grad/pallas_call | solution.py:549
  208.0 2.1 collective-permute-start.10
  210.4 1.1 collective-permute-start.11
  212.0 4.7 %merged.1 = bf16[288,1024]{1,0:T(8,128)(2,1)} custom-call(bf16[288,2048]{1,0:T(8,128)(2,1)} %get-tuple-element.28.a_ref.merged_in_ref, bf16[2048,1024]{1,0:T(8,128)(2,1)} %w_ref.4), custom_call_target="tpu_custom_call" | custom-call | flops 1207959552 | bytes 4718592 | tf_op jit(solution)/shard_map/merged/pallas_call | solution.py:564
  216.7 2.0 slice.106
  220.5 1.9 maximum_add_fusion
  222.5 1.5 broadcast_select_fusion.5
  224.1 2.1 multiply_reduce_fusion.1
  226.8 3.2 %broadcast_select_fusion = (bf16[1152,1024]{1,0:T(8,128)(2,1)S(1)}, bf16[1152,1024]{1,0:T(8,128)(2,1)S(1)}) fusion(bf16[1152,1024]{1,0:T(8,128)(2,1)} %collective-permute-done.35, pred[]{:T(512)S(6)} %eq.15, bf16[576,1024]{1,0:T(8,128)(2,1)S(1)} %get-tuple-element.60, bf16[576,1024]{1,0:T(8,128)(2,1)S(1)} %get-tuple-element.59), kind=kLoop, calls=%fused_computation.7 | loop fusion | flops 7077888 | bytes 9437185 | tf_op jit(solution)/shard_map/jit(_where)/select_n | solution.py:354
  230.0 4.0 %multiply_reduce_fusion = (f32[2048]{0:T(1024)S(1)}, f32[2048,1024]{1,0:T(8,128)}) fusion(bf16[2048,1024]{1,0:T(8,128)(2,1)S(1)} %copy-done, bf16[1152,1024]{1,0:T(8,128)(2,1)S(1)} %get-tuple-element.53, bf16[1152,1024]{1,0:T(8,128)(2,1)S(1)} %get-tuple-element.52), kind=kLoop, calls=%fused_computation | loop fusion | flops 14678016 | bytes 17309696 | tf_op jit(solution)/shard_map/reduce_sum | solution.py:580
  234.6 1.1 maximum_convert_fusion
  (120 shorter events, 21.4 us)
Async XLA Ops:
  1.6 12.8 %collective-permute-start = (bf16[192,512]{1,0:T(8,128)(2,1)S(1)}, bf16[192,512]{1,0:T(8,128)(2,1)S(1)}, u32[]{:S(2)}, u32[]{:S(2)}) collective-permute-start(bf16[192,512]{1,0:T(8,128)(2,1)S(1)} %slice_bitcast_fusion), channel_id=1, source_target_pairs={{0,1},{1,2},{2,3},{3,4},{4,5},{5,6},{6,7},{7,0},{8,9},{9,10},{10,1... | collective-permute-start | bytes 589832 | tf_op jit(solution)/shard_map/ppermute | solution.py:309
  3.0 11.3 %collective-permute-start.1 = (bf16[144,512]{1,0:T(8,128)(2,1)S(1)}, bf16[144,512]{1,0:T(8,128)(2,1)S(1)}, u32[]{:S(2)}, u32[]{:S(2)}) collective-permute-start(bf16[144,512]{1,0:T(8,128)(2,1)S(1)} %bitcast.49), channel_id=1, source_target_pairs={{0,8},{1,9},{2,10},{3,11},{4,12},{5,13},{6,14},{7,15},{8,16},{9,17... | collective-permute-start | bytes 442376 | tf_op jit(solution)/shard_map/ppermute | solution.py:309
  6.4 8.0 %collective-permute-start.2 = (bf16[24,512]{1,0:T(8,128)(2,1)S(1)}, bf16[24,512]{1,0:T(8,128)(2,1)S(1)}, u32[]{:S(2)}, u32[]{:S(2)}) collective-permute-start(bf16[24,512]{1,0:T(8,128)(2,1)S(1)} %slice_bitcast_fusion.1), channel_id=1, source_target_pairs={{0,9},{1,10},{2,11},{3,12},{4,13},{5,14},{6,15},{7,8},{8,17},{9,18... | collective-permute-start | bytes 73736 | tf_op jit(solution)/shard_map/ppermute | solution.py:309
  14.4 0.6 copy-start.13
  14.4 0.7 copy-start.9
  14.4 0.7 copy-start.7
  31.2 8.4 %collective-permute-start.3 = (bf16[192,512]{1,0:T(8,128)(2,1)}, bf16[192,512]{1,0:T(8,128)(2,1)S(1)}, u32[]{:S(2)}, u32[]{:S(2)}) collective-permute-start(bf16[192,512]{1,0:T(8,128)(2,1)} %get-tuple-element.25), channel_id=1, source_target_pairs={{0,7},{1,0},{2,1},{3,2},{4,3},{5,4},{6,5},{7,6},{8,15},{9,8},{10,9... | collective-permute-start | bytes 589832 | tf_op jit(solution)/shard_map/ppermute | solution.py:309
  31.9 7.7 %collective-permute-start.4 = (bf16[144,512]{1,0:T(8,128)(2,1)}, bf16[144,512]{1,0:T(8,128)(2,1)S(1)}, u32[]{:S(2)}, u32[]{:S(2)}) collective-permute-start(bf16[144,512]{1,0:T(8,128)(2,1)} %get-tuple-element.26), channel_id=1, source_target_pairs={{0,24},{1,25},{2,26},{3,27},{4,28},{5,29},{6,30},{7,31},{8,0},{9,1... | collective-permute-start | bytes 442376 | tf_op jit(solution)/shard_map/ppermute | solution.py:309
  33.7 6.0 %collective-permute-start.5 = (bf16[24,512]{1,0:T(8,128)(2,1)}, bf16[24,512]{1,0:T(8,128)(2,1)S(1)}, u32[]{:S(2)}, u32[]{:S(2)}) collective-permute-start(bf16[24,512]{1,0:T(8,128)(2,1)} %get-tuple-element.27), channel_id=1, source_target_pairs={{0,31},{1,24},{2,25},{3,26},{4,27},{5,28},{6,29},{7,30},{8,7},{9,0... | collective-permute-start | bytes 73736 | tf_op jit(solution)/shard_map/ppermute | solution.py:309
  34.0 5.2 %copy-start.5 = (bf16[1152,512]{1,0:T(8,128)(2,1)S(1)}, bf16[1152,512]{1,0:T(8,128)(2,1)}, u32[]{:S(2)}) copy-start(bf16[1152,512]{1,0:T(8,128)(2,1)} %get-tuple-element.24) | copy-start | bytes 3538948
  59.2 4.7 %collective-permute-start.24 = (bf16[1152,1024]{1,0:T(8,128)(2,1)S(1)}, bf16[1152,1024]{1,0:T(8,128)(2,1)}, u32[]{:S(2)}, u32[]{:S(2)}) collective-permute-start(bf16[1152,1024]{1,0:T(8,128)(2,1)S(1)} %constant_dynamic-slice_fusion), channel_id=1, source_target_pairs={{0,1},{1,0},{2,3},{3,2},{4,5},{5,4},{6,7},{7,6},{8,9},{9,8},{10,11... | collective-permute-start | bytes 7077896 | tf_op jit(solution)/shard_map/ppermute | solution.py:374
  59.5 25.2 %copy-start.17 = (bf16[192,512]{1,0:T(8,128)(2,1)S(1)}, bf16[192,512]{1,0:T(8,128)(2,1)}, u32[]{:S(2)}) copy-start(bf16[192,512]{1,0:T(8,128)(2,1)} %get-tuple-element.30) | copy-start | bytes 589828
  59.5 25.2 %copy-start.18 = (bf16[144,512]{1,0:T(8,128)(2,1)S(1)}, bf16[144,512]{1,0:T(8,128)(2,1)}, u32[]{:S(2)}) copy-start(bf16[144,512]{1,0:T(8,128)(2,1)} %get-tuple-element.31) | copy-start | bytes 442372
  59.5 26.7 %copy-start.19 = (bf16[24,512]{1,0:T(8,128)(2,1)S(1)}, bf16[24,512]{1,0:T(8,128)(2,1)}, u32[]{:S(2)}) copy-start(bf16[24,512]{1,0:T(8,128)(2,1)} %get-tuple-element.32) | copy-start | bytes 73732
  66.0 16.3 %collective-permute-start.25 = (bf16[576,1024]{1,0:T(8,128)(2,1)S(1)}, bf16[576,1024]{1,0:T(8,128)(2,1)S(1)}, u32[]{:S(2)}, u32[]{:S(2)}) collective-permute-start(bf16[576,1024]{1,0:T(8,128)(2,1)S(1)} %add_convert_fusion), channel_id=1, source_target_pairs={{0,2},{1,5},{2,0},{3,7},{4,6},{5,1},{6,4},{7,3},{8,10},{9,13},{10,... | collective-permute-start | bytes 3538952 | tf_op jit(solution)/shard_map/ppermute | solution.py:374
  83.9 26.2 %collective-permute-start.26 = (bf16[288,1024]{1,0:T(8,128)(2,1)S(1)}, bf16[288,1024]{1,0:T(8,128)(2,1)S(1)}, u32[]{:S(2)}, u32[]{:S(2)}) collective-permute-start(bf16[288,1024]{1,0:T(8,128)(2,1)S(1)} %add_convert_fusion.1), channel_id=1, source_target_pairs={{0,4},{1,3},{2,6},{3,1},{4,0},{5,7},{6,2},{7,5},{8,12},{9,11},{10,... | collective-permute-start | bytes 1769480 | tf_op jit(solution)/shard_map/ppermute | solution.py:374
  84.7 10.3 %collective-permute-start.6 = (bf16[192,512]{1,0:T(8,128)(2,1)S(1)}, bf16[192,512]{1,0:T(8,128)(2,1)S(1)}, u32[]{:S(2)}, u32[]{:S(2)}) collective-permute-start(bf16[192,512]{1,0:T(8,128)(2,1)S(1)} %copy-done.17), channel_id=1, source_target_pairs={{0,1},{1,2},{2,3},{3,4},{4,5},{5,6},{6,7},{7,0},{8,9},{9,10},{10,1... | collective-permute-start | bytes 589832 | tf_op jit(solution)/shard_map/ppermute | solution.py:309
  84.7 10.2 %collective-permute-start.7 = (bf16[144,512]{1,0:T(8,128)(2,1)S(1)}, bf16[144,512]{1,0:T(8,128)(2,1)S(1)}, u32[]{:S(2)}, u32[]{:S(2)}) collective-permute-start(bf16[144,512]{1,0:T(8,128)(2,1)S(1)} %copy-done.18), channel_id=1, source_target_pairs={{0,8},{1,9},{2,10},{3,11},{4,12},{5,13},{6,14},{7,15},{8,16},{9,17... | collective-permute-start | bytes 442376 | tf_op jit(solution)/shard_map/ppermute | solution.py:309
  86.2 8.7 %collective-permute-start.8 = (bf16[24,512]{1,0:T(8,128)(2,1)S(1)}, bf16[24,512]{1,0:T(8,128)(2,1)S(1)}, u32[]{:S(2)}, u32[]{:S(2)}) collective-permute-start(bf16[24,512]{1,0:T(8,128)(2,1)S(1)} %copy-done.19), channel_id=1, source_target_pairs={{0,9},{1,10},{2,11},{3,12},{4,13},{5,14},{6,15},{7,8},{8,17},{9,18... | collective-permute-start | bytes 73736 | tf_op jit(solution)/shard_map/ppermute | solution.py:309
  94.9 0.6 copy-start.12
  94.9 0.7 copy-start.11
  95.0 0.7 copy-start.6
  111.9 13.5 %collective-permute-start.29 = (bf16[72,1024]{1,0:T(8,128)(2,1)S(1)}, bf16[72,1024]{1,0:T(8,128)(2,1)S(1)}, u32[]{:S(2)}, u32[]{:S(2)}) collective-permute-start(bf16[72,1024]{1,0:T(8,128)(2,1)S(1)} %get-tuple-element.50), channel_id=1, source_target_pairs={{0,24},{8,16},{16,8},{24,0},{1,25},{9,17},{17,9},{25,1},{2,26},{10... | collective-permute-start | bytes 442376 | tf_op jit(solution)/shard_map/ppermute | solution.py:380
  114.2 11.9 %collective-permute-start.28 = (bf16[72,1024]{1,0:T(8,128)(2,1)S(1)}, bf16[72,1024]{1,0:T(8,128)(2,1)S(1)}, u32[]{:S(2)}, u32[]{:S(2)}) collective-permute-start(bf16[72,1024]{1,0:T(8,128)(2,1)S(1)} %get-tuple-element.51), channel_id=1, source_target_pairs={{0,16},{8,24},{16,0},{24,8},{1,17},{9,25},{17,1},{25,9},{2,18},{10... | collective-permute-start | bytes 442376 | tf_op jit(solution)/shard_map/ppermute | solution.py:380
  114.8 11.3 %collective-permute-start.27 = (bf16[72,1024]{1,0:T(8,128)(2,1)S(1)}, bf16[72,1024]{1,0:T(8,128)(2,1)S(1)}, u32[]{:S(2)}, u32[]{:S(2)}) collective-permute-start(bf16[72,1024]{1,0:T(8,128)(2,1)S(1)} %get-tuple-element.49), channel_id=1, source_target_pairs={{0,8},{8,0},{16,24},{24,16},{1,9},{9,1},{17,25},{25,17},{2,10},{10... | collective-permute-start | bytes 442376 | tf_op jit(solution)/shard_map/ppermute | solution.py:380
  127.4 11.4 %collective-permute-start.30 = (bf16[72,1024]{1,0:T(8,128)(2,1)S(1)}, bf16[72,1024]{1,0:T(8,128)(2,1)S(1)}, u32[]{:S(2)}, u32[]{:S(2)}) collective-permute-start(bf16[72,1024]{1,0:T(8,128)(2,1)S(1)} %get-tuple-element.44), channel_id=1, source_target_pairs={{0,8},{8,0},{16,24},{24,16},{1,9},{9,1},{17,25},{25,17},{2,10},{10... | collective-permute-start | bytes 442376 | tf_op jit(solution)/shard_map/ppermute | solution.py:386
  133.1 13.9 %copy-start.2 = (bf16[3,512,512]{2,1,0:T(8,128)(2,1)S(1)}, bf16[3,512,512]{2,1,0:T(8,128)(2,1)}, u32[]{:S(2)}) copy-start(bf16[3,512,512]{2,1,0:T(8,128)(2,1)} %qkv_dw.1) | copy-start | bytes 4718596
  133.1 12.8 %collective-permute-start.31 = (bf16[72,1024]{1,0:T(8,128)(2,1)S(1)}, bf16[72,1024]{1,0:T(8,128)(2,1)S(1)}, u32[]{:S(2)}, u32[]{:S(2)}) collective-permute-start(bf16[72,1024]{1,0:T(8,128)(2,1)S(1)} %get-tuple-element.44), channel_id=1, source_target_pairs={{0,16},{8,24},{16,0},{24,8},{1,17},{9,25},{17,1},{25,9},{2,18},{10... | collective-permute-start | bytes 442376 | tf_op jit(solution)/shard_map/ppermute | solution.py:386
  137.2 9.9 %collective-permute-start.12 = (bf16[768,512]{1,0:T(8,128)(2,1)S(1)}, bf16[768,512]{1,0:T(8,128)(2,1)}, u32[]{:S(2)}, u32[]{:S(2)}) collective-permute-start(bf16[768,512]{1,0:T(8,128)(2,1)S(1)} %constant_dynamic-slice_fusion.1), channel_id=1, source_target_pairs={{0,1},{1,0},{2,3},{3,2},{4,5},{5,4},{6,7},{7,6},{8,9},{9,8},{10,11... | collective-permute-start | bytes 2359304 | tf_op jit(solution)/shard_map/ppermute | solution.py:374
  137.2 8.7 %collective-permute-start.32 = (bf16[72,1024]{1,0:T(8,128)(2,1)S(1)}, bf16[72,1024]{1,0:T(8,128)(2,1)S(1)}, u32[]{:S(2)}, u32[]{:S(2)}) collective-permute-start(bf16[72,1024]{1,0:T(8,128)(2,1)S(1)} %get-tuple-element.44), channel_id=1, source_target_pairs={{0,24},{8,16},{16,8},{24,0},{1,25},{9,17},{17,9},{25,1},{2,26},{10... | collective-permute-start | bytes 442376 | tf_op jit(solution)/shard_map/ppermute | solution.py:386
  145.9 14.3 %collective-permute-start.33 = (bf16[288,1024]{1,0:T(8,128)(2,1)S(1)}, bf16[288,1024]{1,0:T(8,128)(2,1)}, u32[]{:S(2)}, u32[]{:S(2)}) collective-permute-start(bf16[288,1024]{1,0:T(8,128)(2,1)S(1)} %constant_dynamic-update-slice_fusion.6), channel_id=1, source_target_pairs={{0,4},{1,3},{2,6},{3,1},{4,0},{5,7},{6,2},{7,5},{8,12},{9,11},{10,... | collective-permute-start | bytes 1769480 | tf_op jit(solution)/shard_map/ppermute | solution.py:389
  148.9 16.0 %collective-permute-start.13 = (bf16[384,512]{1,0:T(8,128)(2,1)}, bf16[384,512]{1,0:T(8,128)(2,1)}, u32[]{:S(2)}, u32[]{:S(2)}) collective-permute-start(bf16[384,512]{1,0:T(8,128)(2,1)} %add_convert_fusion.2), channel_id=1, source_target_pairs={{0,2},{1,5},{2,0},{3,7},{4,6},{5,1},{6,4},{7,3},{8,10},{9,13},{10,... | collective-permute-start | bytes 1179656 | tf_op jit(solution)/shard_map/ppermute | solution.py:374
  162.5 30.7 %collective-permute-start.34 = (bf16[576,1024]{1,0:T(8,128)(2,1)}, bf16[576,1024]{1,0:T(8,128)(2,1)}, u32[]{:S(2)}, u32[]{:S(2)}) collective-permute-start(bf16[576,1024]{1,0:T(8,128)(2,1)} %pad_maximum_fusion.3), channel_id=1, source_target_pairs={{0,2},{1,5},{2,0},{3,7},{4,6},{5,1},{6,4},{7,3},{8,10},{9,13},{10,... | collective-permute-start | bytes 3538952 | tf_op jit(solution)/shard_map/ppermute | solution.py:389
  166.1 7.8 %collective-permute-start.14 = (bf16[192,512]{1,0:T(8,128)(2,1)S(1)}, bf16[192,512]{1,0:T(8,128)(2,1)S(1)}, u32[]{:S(2)}, u32[]{:S(2)}) collective-permute-start(bf16[192,512]{1,0:T(8,128)(2,1)S(1)} %add_convert_fusion.3), channel_id=1, source_target_pairs={{0,4},{1,3},{2,6},{3,1},{4,0},{5,7},{6,2},{7,5},{8,12},{9,11},{10,... | collective-permute-start | bytes 589832 | tf_op jit(solution)/shard_map/ppermute | solution.py:374
  175.0 6.5 %collective-permute-start.17 = (bf16[48,512]{1,0:T(8,128)(2,1)S(1)}, bf16[48,512]{1,0:T(8,128)(2,1)S(1)}, u32[]{:S(2)}, u32[]{:S(2)}) collective-permute-start(bf16[48,512]{1,0:T(8,128)(2,1)S(1)} %get-tuple-element.55), channel_id=1, source_target_pairs={{0,24},{8,16},{16,8},{24,0},{1,25},{9,17},{17,9},{25,1},{2,26},{10... | collective-permute-start | bytes 147464 | tf_op jit(solution)/shard_map/ppermute | solution.py:380
  175.3 7.4 %collective-permute-start.16 = (bf16[48,512]{1,0:T(8,128)(2,1)S(1)}, bf16[48,512]{1,0:T(8,128)(2,1)S(1)}, u32[]{:S(2)}, u32[]{:S(2)}) collective-permute-start(bf16[48,512]{1,0:T(8,128)(2,1)S(1)} %get-tuple-element.56), channel_id=1, source_target_pairs={{0,16},{8,24},{16,0},{24,8},{1,17},{9,25},{17,1},{25,9},{2,18},{10... | collective-permute-start | bytes 147464 | tf_op jit(solution)/shard_map/ppermute | solution.py:380
  178.1 4.6 %collective-permute-start.15 = (bf16[48,512]{1,0:T(8,128)(2,1)S(1)}, bf16[48,512]{1,0:T(8,128)(2,1)S(1)}, u32[]{:S(2)}, u32[]{:S(2)}) collective-permute-start(bf16[48,512]{1,0:T(8,128)(2,1)S(1)} %get-tuple-element.54), channel_id=1, source_target_pairs={{0,8},{8,0},{16,24},{24,16},{1,9},{9,1},{17,25},{25,17},{2,10},{10... | collective-permute-start | bytes 147464 | tf_op jit(solution)/shard_map/ppermute | solution.py:380
  183.6 4.5 %collective-permute-start.18 = (bf16[48,512]{1,0:T(8,128)(2,1)S(1)}, bf16[48,512]{1,0:T(8,128)(2,1)S(1)}, u32[]{:S(2)}, u32[]{:S(2)}) collective-permute-start(bf16[48,512]{1,0:T(8,128)(2,1)S(1)} %get-tuple-element.48), channel_id=1, source_target_pairs={{0,8},{8,0},{16,24},{24,16},{1,9},{9,1},{17,25},{25,17},{2,10},{10... | collective-permute-start | bytes 147464 | tf_op jit(solution)/shard_map/ppermute | solution.py:386
  184.6 5.0 %collective-permute-start.19 = (bf16[48,512]{1,0:T(8,128)(2,1)S(1)}, bf16[48,512]{1,0:T(8,128)(2,1)S(1)}, u32[]{:S(2)}, u32[]{:S(2)}) collective-permute-start(bf16[48,512]{1,0:T(8,128)(2,1)S(1)} %get-tuple-element.48), channel_id=1, source_target_pairs={{0,16},{8,24},{16,0},{24,8},{1,17},{9,25},{17,1},{25,9},{2,18},{10... | collective-permute-start | bytes 147464 | tf_op jit(solution)/shard_map/ppermute | solution.py:386
  186.0 5.9 %collective-permute-start.20 = (bf16[48,512]{1,0:T(8,128)(2,1)S(1)}, bf16[48,512]{1,0:T(8,128)(2,1)S(1)}, u32[]{:S(2)}, u32[]{:S(2)}) collective-permute-start(bf16[48,512]{1,0:T(8,128)(2,1)S(1)} %get-tuple-element.48), channel_id=1, source_target_pairs={{0,24},{8,16},{16,8},{24,0},{1,25},{9,17},{17,9},{25,1},{2,26},{10... | collective-permute-start | bytes 147464 | tf_op jit(solution)/shard_map/ppermute | solution.py:386
  191.9 5.7 %collective-permute-start.21 = (bf16[192,512]{1,0:T(8,128)(2,1)S(1)}, bf16[192,512]{1,0:T(8,128)(2,1)S(1)}, u32[]{:S(2)}, u32[]{:S(2)}) collective-permute-start(bf16[192,512]{1,0:T(8,128)(2,1)S(1)} %constant_dynamic-update-slice_fusion), channel_id=1, source_target_pairs={{0,4},{1,3},{2,6},{3,1},{4,0},{5,7},{6,2},{7,5},{8,12},{9,11},{10,... | collective-permute-start | bytes 589832 | tf_op jit(solution)/shard_map/ppermute | solution.py:389
  195.1 3.5 %copy-start.3 = (bf16[24,48,512]{2,1,0:T(8,128)(2,1)S(1)}, bf16[24,48,512]{2,1,0:T(8,128)(2,1)}, u32[]{:S(2)}) copy-start(bf16[24,48,512]{2,1,0:T(8,128)(2,1)} %param.15) | copy-start | bytes 3538948
  196.7 2.0 copy-start.14
  196.7 2.0 copy-start.8
  196.7 2.0 copy-start.10
  196.7 30.1 %collective-permute-start.35 = (bf16[1152,1024]{1,0:T(8,128)(2,1)}, bf16[1152,1024]{1,0:T(8,128)(2,1)}, u32[]{:S(2)}, u32[]{:S(2)}) collective-permute-start(bf16[1152,1024]{1,0:T(8,128)(2,1)} %pad_maximum_fusion.1), channel_id=1, source_target_pairs={{0,1},{1,0},{2,3},{3,2},{4,5},{5,4},{6,7},{7,6},{8,9},{9,8},{10,11... | collective-permute-start | bytes 7077896 | tf_op jit(solution)/shard_map/ppermute | solution.py:389
  197.7 12.4 %collective-permute-start.22 = (bf16[384,512]{1,0:T(8,128)(2,1)S(1)}, bf16[384,512]{1,0:T(8,128)(2,1)S(1)}, u32[]{:S(2)}, u32[]{:S(2)}) collective-permute-start(bf16[384,512]{1,0:T(8,128)(2,1)S(1)} %pad_maximum_fusion.5), channel_id=1, source_target_pairs={{0,2},{1,5},{2,0},{3,7},{4,6},{5,1},{6,4},{7,3},{8,10},{9,13},{10,... | collective-permute-start | bytes 1179656 | tf_op jit(solution)/shard_map/ppermute | solution.py:389
  208.0 10.7 %collective-permute-start.10 = (bf16[144,512]{1,0:T(8,128)(2,1)}, bf16[144,512]{1,0:T(8,128)(2,1)}, u32[]{:S(2)}, u32[]{:S(2)}) collective-permute-start(bf16[144,512]{1,0:T(8,128)(2,1)} %get-tuple-element.37), channel_id=1, source_target_pairs={{0,24},{1,25},{2,26},{3,27},{4,28},{5,29},{6,30},{7,31},{8,0},{9,1... | collective-permute-start | bytes 442376 | tf_op jit(solution)/shard_map/ppermute | solution.py:309
  210.3 12.1 %collective-permute-start.23 = (bf16[768,512]{1,0:T(8,128)(2,1)S(1)}, bf16[768,512]{1,0:T(8,128)(2,1)}, u32[]{:S(2)}, u32[]{:S(2)}) collective-permute-start(bf16[768,512]{1,0:T(8,128)(2,1)S(1)} %pad_maximum_fusion.4), channel_id=1, source_target_pairs={{0,1},{1,0},{2,3},{3,2},{4,5},{5,4},{6,7},{7,6},{8,9},{9,8},{10,11... | collective-permute-start | bytes 2359304 | tf_op jit(solution)/shard_map/ppermute | solution.py:389
  210.4 9.3 %collective-permute-start.11 = (bf16[24,512]{1,0:T(8,128)(2,1)}, bf16[24,512]{1,0:T(8,128)(2,1)}, u32[]{:S(2)}, u32[]{:S(2)}) collective-permute-start(bf16[24,512]{1,0:T(8,128)(2,1)} %get-tuple-element.38), channel_id=1, source_target_pairs={{0,31},{1,24},{2,25},{3,26},{4,27},{5,28},{6,29},{7,30},{8,7},{9,0... | collective-permute-start | bytes 73736 | tf_op jit(solution)/shard_map/ppermute | solution.py:309
  211.5 9.0 %collective-permute-start.9 = (bf16[192,512]{1,0:T(8,128)(2,1)}, bf16[192,512]{1,0:T(8,128)(2,1)S(1)}, u32[]{:S(2)}, u32[]{:S(2)}) collective-permute-start(bf16[192,512]{1,0:T(8,128)(2,1)} %get-tuple-element.36), channel_id=1, source_target_pairs={{0,7},{1,0},{2,1},{3,2},{4,3},{5,4},{6,5},{7,6},{8,15},{9,8},{10,9... | collective-permute-start | bytes 589832 | tf_op jit(solution)/shard_map/ppermute | solution.py:309
  216.7 3.8 %copy-start.4 = (bf16[1152,512]{1,0:T(8,128)(2,1)S(1)}, bf16[1152,512]{1,0:T(8,128)(2,1)}, u32[]{:S(2)}) copy-start(bf16[1152,512]{1,0:T(8,128)(2,1)} %get-tuple-element.39.gmix_ref) | copy-start | bytes 3538948
  222.5 1.6 copy-start.1
  224.1 2.1 copy-start.15
  226.8 3.2 %copy-start = (bf16[2048,1024]{1,0:T(8,128)(2,1)S(1)}, bf16[2048,1024]{1,0:T(8,128)(2,1)}, u32[]{:S(2)}) copy-start(bf16[2048,1024]{1,0:T(8,128)(2,1)} %w_ref.4) | copy-start | bytes 12582916
  230.0 4.0 %copy-start.16 = (f32[2048]{0:T(1024)S(1)}, f32[2048]{0:T(1024)}, u32[]{:S(2)}) copy-start(f32[2048]{0:T(1024)} %param.20) | copy-start | bytes 24580
where the time goes:
time: 237 us; the launch traced here: 236 us
  Pallas kernels  79.2 us (33%)
  waiting for transfers between devices  62.8 us (26%)
  starting transfers between devices  42.7 us (18%)
  other arithmetic  37.9 us (16%)
  local copies, waits for them, and re-layouts  11.9 us (5%)
    ppermute x6, waiting for transfers between devices, reduce_all(): received = lax.ppermute(sent, 'lon', pairs)  26.6 us
    pallas_call x4, Pallas kernels, on_device_body(): pl.pallas_call(body, grid=(count_a,), in_specs=specs, out_specs=spec, out...  18.1 us
    pallas_call x1, Pallas kernels, on_device_body(): pl.pallas_call(functools.partial(forward_kernel, stride, count_b), grid=(...  16.1 us
    ppermute x12, starting transfers between devices, send(): return lax.ppermute(value, ('lat', 'lon'), pairs)  15 us
    ppermute x6, waiting for transfers between devices, reduce_all(): received = lax.ppermute(value, 'lon', pairs)  11.1 us
    ppermute x6, waiting for transfers between devices, reduce_all(): received = lax.ppermute(mine, 'lat', [(i, i ^ d) for i in range(count_lat)])  10.9 us
    ppermute x12, waiting for transfers between devices, send(): return lax.ppermute(value, ('lat', 'lon'), pairs)  10.3 us
    convert_element_type x6, other arithmetic, part_sum(): return sum(parts[1:], parts[0]).astype(BF)  9.65 us
  transfers between devices with their start and end apart: 36, of which 14 were waited for; matrix products, arithmetic and copies ran while one was open for 12% of the time, Pallas kernels for 20%

commit v1 on v0

--- a/solution.py
+++ b/solution.py
@@ -41,42 +41,6 @@
     return pl.CostEstimate(flops=int(flops), transcendentals=0, bytes_accessed=int(nbytes))
 
 
-def window_matrix(cols, stride):
-    count_b = cols // WLON
-    mat = np.zeros((count_b * stride, WLAT * cols), np.float32)
-    for b in range(count_b):
-        for r in range(WLAT):
-            for c in range(WLON):
-                mat[b * stride + r * WLON + c, r * cols + b * WLON + c] = 1.0
-    return mat
-
-
-def halo_matrices(rows, cols, stride):
-    hr, hc = WLAT // 2, WLON // 2
-    count_a, count_b = rows // WLAT, cols // WLON
-    padded = count_b * stride
-    own = np.zeros((2, padded, WLAT * cols), np.float32)
-    west = np.zeros((count_a, padded, rows * EDGE), np.float32)
-    south = np.zeros((padded, hr * cols), np.float32)
-    corner = np.zeros((padded, hr * EDGE), np.float32)
-    for a in range(count_a):
-        for b in range(count_b):
-            for r in range(WLAT):
-                for c in range(WLON):
-                    place = b * stride + r * WLON + c
-                    row, col = a * WLAT + r - hr, b * WLON + c - hc
-                    if row >= 0 and col >= 0:
-                        base = row if a == 0 else r
-                        own[min(a, 1), place, base * cols + col] = 1.0
-                    elif row >= 0:
-                        west[a, place, row * EDGE + col + EDGE] = 1.0
-                    elif col >= 0:
-                        south[place, (row + hr) * cols + col] = 1.0
-                    else:
-                        corner[place, (row + hr) * EDGE + col + EDGE] = 1.0
-    return [jnp.asarray(m, BF) for m in (own, west, south, corner)]
-
-
 def patch_matrix(cols):
     half = cols // 2
     mat = np.zeros((4 * half, 2 * cols), np.float32)
@@ -92,33 +56,58 @@
     return even.astype(BF), (1.0 - even).astype(BF)
 
 
-def halo_rows(own_ref, west_ref, south_ref, corner_ref, po_ref, pw_ref, ps_ref, pc_ref, first):
+def load_windows(own_ref, west_ref, south_ref, corner_ref, buf_ref, win_ref, stride):
     step = pl.program_id(0)
-    block = po_ref.shape[2]
-    half = block // 2
-    start = pl.multiple_of(jnp.maximum(step * block - half, 0), 16)
-    take = jnp.where(step == 0, 0, 1)
-    value = dot_nn(po_ref[take], own_ref[pl.ds(start, block), :])
-    value = value + dot_nn(pw_ref[0], west_ref[...])
-    first[...] = value
+    cols = south_ref.shape[0] // (WLAT // 2)
+    wide = EDGE + cols
+    half = WLAT // 2
+
+    def put(r, edge, line):
+        buf_ref[pl.ds(wide * r, EDGE), :] = edge.astype(F32)
+        buf_ref[pl.ds(wide * r + EDGE, cols), :] = line.astype(F32)
 
     @pl.when(step == 0)
     def _():
-        first[...] += dot_nn(ps_ref[...], south_ref[...]) + dot_nn(pc_ref[...], corner_ref[...])
-
-    return first[...]
+        for r in range(half):
+            put(r, corner_ref[r], south_ref[pl.ds(cols * r, cols), :])
+
+    @pl.when(step > 0)
+    def _():
+        for r in range(half):
+            row = WLAT * step - half + r
+            put(r, west_ref[row], own_ref[pl.ds(pl.multiple_of(cols * row, 16), cols), :])
+
+    for r in range(half, WLAT):
+        row = WLAT * step - half + r
+        put(r, west_ref[row], own_ref[pl.ds(pl.multiple_of(cols * row, 16), cols), :])
+    for b in range(cols // WLON):
+        for r in range(WLAT):
+            piece = buf_ref[pl.ds(wide * r + EDGE - WLON // 2 + WLON * b, WLON), :]
+            win_ref[pl.ds(stride * b + WLON * r, WLON), :] = piece
+        pad = stride - WLAT * WLON
+        win_ref[pl.ds(stride * (b + 1) - pad, pad), :] = jnp.zeros((pad, win_ref.shape[1]), F32)
+
+
+def unload_windows(win_ref, grid_ref, stride):
+    cols = grid_ref.shape[0] // WLAT
+    for b in range(cols // WLON):
+        for r in range(WLAT):
+            piece = win_ref[pl.ds(stride * b + WLON * r, WLON), :]
+            grid_ref[pl.ds(cols * r + WLON * b, WLON), :] = piece
+    return grid_ref[...]
 
 
 def stack_heads(value, masks):
     return jnp.concatenate([value * masks[0], value * masks[1]], axis=0)
 
 
-def forward_kernel(stride, count_b, own_ref, west_ref, south_ref, corner_ref, po_ref, pw_ref, ps_ref,
-                   pc_ref, allow_ref, gain_ref, w_ref, to_grid_ref,
-                   att_ref, qkv_ref, normed_ref, prob_ref, lon_ref, lat_ref, corner_out_ref, first,
-                   att_win_ref):
+def forward_kernel(stride, count_b, own_ref, west_ref, south_ref, corner_ref, allow_ref, gain_ref,
+                   w_ref, att_ref, qkv_ref, normed_ref, tok_ref, prob_ref, lon_ref, lat_ref,
+                   corner_out_ref, buf_ref, win_ref, grid_ref):
     features = own_ref.shape[1]
-    x = halo_rows(own_ref, west_ref, south_ref, corner_ref, po_ref, pw_ref, ps_ref, pc_ref, first)
+    load_windows(own_ref, west_ref, south_ref, corner_ref, buf_ref, win_ref, stride)
+    x = win_ref[...]
+    tok_ref[...] = x.astype(BF)
     average = jnp.mean(x, axis=-1, keepdims=True)
     centered = x - average
     variance = jnp.mean(centered * centered, axis=-1, keepdims=True)
@@ -128,15 +117,12 @@
         qkv_ref[t] = dot_nn(normed, w_ref[:, features * t : features * (t + 1)]).astype(BF)
     allow = allow_ref[0] > 0.5
     masks = lane_masks()
-    spans = [slice(b * stride, (b + 1) * stride) for b in range(count_b)]
-    for pair in range(features // 128):
-        lanes = pl.ds(128 * pair, 128)
-        scores = []
-        for rows in spans:
+    for b in range(count_b):
+        rows = slice(b * stride, (b + 1) * stride)
+        for pair in range(features // 128):
+            lanes = pl.ds(128 * pair, 128)
             q2 = qkv_ref[0, rows, lanes] * jnp.asarray(0.125, BF)
-            scores.append(dot_nt(stack_heads(qkv_ref[1, rows, lanes], masks), q2))
-        stacked = []
-        for b, s2 in enumerate(scores):
+            s2 = dot_nt(stack_heads(qkv_ref[1, rows, lanes], masks), q2)
             probs = []
             for h in range(2):
                 s = jnp.where(allow, s2[h * stride : (h + 1) * stride], -1e30)
@@ -144,11 +130,8 @@
                 probs.append((e * (1.0 / jnp.sum(e, axis=0, keepdims=True))).astype(BF))
             p2 = jnp.concatenate(probs, axis=0)
             prob_ref[pair, pl.ds(2 * stride * b, 2 * stride), :] = p2
-            stacked.append(p2)
-        for rows, p2 in zip(spans, stacked):
-            o2 = dot_tn(p2, stack_heads(qkv_ref[2, rows, lanes], masks))
-            att_win_ref[rows, lanes] = o2.astype(BF)
-    write_edges(dot_nn(to_grid_ref[...], att_win_ref[...]), att_ref, lon_ref, lat_ref, corner_out_ref)
+            win_ref[rows, lanes] = dot_tn(p2, stack_heads(qkv_ref[2, rows, lanes], masks))
+    write_edges(unload_windows(win_ref, grid_ref, stride), att_ref, lon_ref, lat_ref, corner_out_ref)
 
 
 def write_edges(values, out_ref, lon_ref, lat_ref, corner_ref):
@@ -163,10 +146,9 @@
         corner_ref[...] = edge[: corner_ref.shape[0]]
 
 
-def assemble_kernel(own_ref, west_ref, south_ref, corner_ref, po_ref, pw_ref, ps_ref, pc_ref, out_ref,
-                    first):
-    out_ref[...] = halo_rows(own_ref, west_ref, south_ref, corner_ref, po_ref, pw_ref, ps_ref, pc_ref,
-                             first).astype(BF)
+def assemble_kernel(stride, own_ref, west_ref, south_ref, corner_ref, out_ref, buf_ref, win_ref):
+    load_windows(own_ref, west_ref, south_ref, corner_ref, buf_ref, win_ref, stride)
+    out_ref[...] = win_ref[...].astype(BF)
 
 
 def middle_kernel(cols, tok_ref, att_ref, w_out_ref, gain_ref, grad_in_ref, to_patch_ref,
@@ -217,20 +199,60 @@
 
 
 def merge_grad_kernel(merged_in_ref, gm_ref, att_ref, gmix_ref, out_ref):
+    width = gm_ref.shape[1]
+    out_ref[:, :width] = dot_tn(merged_in_ref[...], gm_ref[...]).astype(BF)
+    out_ref[:, width:] = dot_tn(gmix_ref[...], att_ref[...]).T.astype(BF)
+
+
+def row_sums(value):
+    total = sum(value[:, 128 * k : 128 * (k + 1)] for k in range(value.shape[1] // 128))
+    return jnp.sum(total.T, axis=0, keepdims=True)
+
+
+def merge_last_kernel(half, keep_ref, own_ref, got_ref, w_ref, gain_ref, out_ref, out_o_ref, dgain_ref):
+    width = w_ref.shape[1]
+    here = pl.program_id(0) // half == keep_ref[0]
+
+    def finish(ref):
+        value = ref[:, :width].astype(F32)
+        out_ref[...] = value
+        out_o_ref[...] = ref[:, width:].astype(F32)
+        dgain_ref[...] = row_sums(value * w_ref[...].astype(F32)) / gain_ref[...]
+
+    @pl.when(here)
+    def _():
+        finish(own_ref)
+
+    @pl.when(jnp.logical_not(here))
+    def _():
+        finish(got_ref)
+
+
+def qkv_last_kernel(half, keep_ref, own_ref, got_ref, w_ref, gain_ref, out_ref, dgain_ref):
     step = pl.program_id(0)
-    last = pl.num_programs(0) - 1
-    height = out_ref.shape[0]
-    narrow = gmix_ref.shape[1]
-
-    @pl.when(step < last)
-    def _():
-        out_ref[...] = dot_tn(merged_in_ref[...], gm_ref[...]).astype(BF)
-
-    @pl.when(step == last)
-    def _():
-        for k in range(att_ref.shape[1] // height):
-            part = dot_tn(att_ref[:, height * k : height * (k + 1)], gmix_ref[...])
-            out_ref[:, narrow * k : narrow * (k + 1)] = part.astype(BF)
+    here = step // half == keep_ref[0]
+    side = pl.ds(step % 2, 1)
+
+    def finish(ref):
+        value = ref[...].astype(F32)
+        out_ref[...] = value
+        part = row_sums(value * w_ref[...].astype(F32))
+
+        @pl.when(step < 2)
+        def _():
+            dgain_ref[side, :] = part / gain_ref[side, :]
+
+        @pl.when(step >= 2)
+        def _():
+            dgain_ref[side, :] += part / gain_ref[side, :]
+
+    @pl.when(here)
+    def _():
+        finish(own_ref)
+
+    @pl.when(jnp.logical_not(here))
+    def _():
+        finish(got_ref)
 
 
 def backward_kernel(stride, count_b, ga_ref, qkv_ref, prob_ref, prev_ref, gqkv_ref):
@@ -269,11 +291,10 @@
         out_ref[t] = dot_tn(normed_ref[...], gqkv_ref[t]).astype(BF)
 
 
-def input_grad_kernel(gqkv_ref, x_ref, gain_ref, w_ref, to_grid_ref, out_ref, lon_ref, lat_ref,
-                      corner_ref):
+def input_grad_kernel(stride, gqkv_ref, x_ref, gain_ref, w_ref, out_ref, lon_ref, lat_ref, corner_ref,
+                      win_ref, grid_ref):
     features = x_ref.shape[1]
     grad = sum(dot_nt(gqkv_ref[t], w_ref[:, features * t : features * (t + 1)]) for t in range(3))
-    grad = dot_nn(to_grid_ref[...], grad.astype(BF))
     x = x_ref[...].astype(F32)
     centered = x - jnp.mean(x, axis=-1, keepdims=True)
     inv = lax.rsqrt(jnp.mean(centered * centered, axis=-1, keepdims=True) + EPSILON)
@@ -281,7 +302,8 @@
     grad = grad * gain_ref[...]
     one = jnp.mean(grad, axis=-1, keepdims=True)
     two = jnp.mean(grad * hat, axis=-1, keepdims=True)
-    write_edges((grad - one - hat * two) * inv, out_ref, lon_ref, lat_ref, corner_ref)
+    win_ref[...] = (grad - one - hat * two) * inv
+    write_edges(unload_windows(win_ref, grid_ref, stride), out_ref, lon_ref, lat_ref, corner_ref)
 
 
 def merged_kernel(a_ref, w_ref, out_ref):
@@ -322,17 +344,6 @@
     hr = WLAT // 2
     parts = (values[:, cols - EDGE :], values[rows - hr :], values[rows - hr :, cols - EDGE :])
     return [v.reshape(-1, features) for v in parts]
-
-
-def to_shifted(values, parts):
-    rows, cols, features = values.shape
-    hr, hc = WLAT // 2, WLON // 2
-    west, south, corner = parts
-    corner = corner.reshape(hr, EDGE, features)[:, EDGE - hc :]
-    top = jnp.concatenate([corner, south.reshape(hr, cols, features)[:, : cols - hc]], 1)
-    west = west.reshape(rows, EDGE, features)[: rows - hr, EDGE - hc :]
-    bottom = jnp.concatenate([west, values[: rows - hr, : cols - hc]], 1)
-    return jnp.concatenate([top, bottom], axis=0)
 
 
 def to_own(values, parts):
@@ -387,8 +398,9 @@
         value = lax.dynamic_update_slice_in_dim(value, received, (lat ^ d) * height, 0)
     for k, (pairs, keep) in reversed(list(enumerate(plans))):
         received = lax.ppermute(value, "lon", pairs)
-        value = join(value, received, keep)
-    return value
+        if k:
+            value = join(value, received, keep)
+    return value, received, odd.astype(jnp.int32).reshape(1)
 
 
 def on_device_body(tokens, lat_band, gain_attn, w_qkv, w_out, gain_merge, w_merge, grad_merged):
@@ -399,9 +411,9 @@
     stride = -(-window // 16) * 16
     half_lat = WLAT // 2
     block = WLAT * cols
+    wide = WLAT * (cols + EDGE)
     padded = count_b * stride
     total = rows * cols
-    to_grid = jnp.asarray(window_matrix(cols, stride).T, BF)
     patch_np = patch_matrix(cols)
     to_patch = jnp.asarray(patch_np, BF)
     from_patch = jnp.asarray(patch_np.T, BF)
@@ -416,35 +428,42 @@
     gain_m = gain_merge.reshape(1, 4 * features)
 
     own_tok = tokens.reshape(total, features)
-    mats = halo_matrices(rows, cols, stride)
     edge_shapes = [(rows * EDGE, features), (half_lat * cols, features), (half_lat * EDGE, features)]
     edge_types = [jax.ShapeDtypeStruct(shape, BF) for shape in edge_shapes]
     edge_specs = [rows_of(WLAT * EDGE, features), whole(edge_shapes[1]), whole(edge_shapes[2])]
-    halo_specs = [whole((total, features))] + [whole(shape) for shape in edge_shapes] + [
-        whole(mats[0].shape), pl.BlockSpec((1,) + mats[1].shape[1:], lambda i: (i, 0, 0)),
-        whole(mats[2].shape), whole(mats[3].shape)]
+    halo_specs = [whole((total, features)), whole((rows, EDGE, features)), whole(edge_shapes[1]),
+                  whole((half_lat, EDGE, features))]
+    win_scratch = pltpu.VMEM((padded, features), F32)
+    buf_scratch = pltpu.VMEM((wide, features), F32)
+    grid_scratch = pltpu.VMEM((block, features), F32)
+
+    def halo_args(parts):
+        west, south, corner = parts
+        return west.reshape(rows, EDGE, features), south, corner.reshape(half_lat, EDGE, features)
+
     tok_halos = exchange(edges(tokens), 1)
     allow_spec = pl.BlockSpec((1, stride, stride), lambda i: (i, 0, 0))
     pairs = features // 128
     tall3 = count_a * padded
     qkv_spec = pl.BlockSpec((3, padded, features), lambda i: (0, i, 0))
     prob_rows = 2 * stride * count_b
-    attended, qkv, normed, probs, *att_edges = pl.pallas_call(
+    attended, qkv, normed, tok_win, probs, *att_edges = pl.pallas_call(
         functools.partial(forward_kernel, stride, count_b),
         grid=(count_a,),
-        in_specs=halo_specs + [allow_spec, whole((1, features)), whole((features, 3 * features)),
-                               whole((block, padded))],
+        in_specs=halo_specs + [allow_spec, whole((1, features)), whole((features, 3 * features))],
         out_specs=[rows_of(block, features), qkv_spec, rows_of(padded, features),
+                   rows_of(padded, features),
                    pl.BlockSpec((pairs, prob_rows, stride), lambda i: (0, i, 0))] + edge_specs,
         out_shape=[jax.ShapeDtypeStruct((total, features), BF),
                    jax.ShapeDtypeStruct((3, tall3, features), BF),
                    jax.ShapeDtypeStruct((tall3, features), BF),
+                   jax.ShapeDtypeStruct((tall3, features), BF),
                    jax.ShapeDtypeStruct((pairs, count_a * prob_rows, stride), BF)] + edge_types,
-        scratch_shapes=[pltpu.VMEM((padded, features), F32), pltpu.VMEM((padded, features), BF)],
+        scratch_shapes=[buf_scratch, win_scratch, grid_scratch],
         compiler_params=params(1),
         cost_estimate=cost(4 * total * features * 3 * features, 2 * total * features * 8),
         name="attn_fwd",
-    )(own_tok, *tok_halos, *mats, allow, gain_a, w_qkv, to_grid)
+    )(own_tok, *halo_args(tok_halos), allow, gain_a, w_qkv)
 
     att_parts = exchange(att_edges, -1)
     own_att = to_own(attended.reshape(rows, cols, features), att_parts).reshape(total, features)
@@ -480,32 +499,33 @@
     )(own_tok, own_att, w_out, gain_m, grad_in, to_patch, from_patch)
 
     att_halos = exchange(grad_edges, 1)
-    rest = features * features // width2
-    pieces = 4 * features // rest
+    pieces = 4
+    rest = features // pieces
     dw_merge = pl.pallas_call(
         merge_grad_kernel,
-        grid=(pieces + 1,),
-        in_specs=[pl.BlockSpec((total // 4, rest), lambda i: (0, jnp.minimum(i, pieces - 1))),
-                  whole((total // 4, width2)), whole((total, features)), whole((total, features))],
-        out_specs=rows_of(rest, width2),
-        out_shape=jax.ShapeDtypeStruct((4 * features + rest, width2), BF),
+        grid=(pieces,),
+        in_specs=[pl.BlockSpec((total // 4, features), lambda i: (0, i)),
+                  whole((total // 4, width2)), whole((total, features)),
+                  pl.BlockSpec((total, rest), lambda i: (0, i))],
+        out_specs=rows_of(features, width2 + rest),
+        out_shape=jax.ShapeDtypeStruct((pieces * features, width2 + rest), BF),
         compiler_params=params(1),
         cost_estimate=cost(4 * total * features * features * 2, 2 * total * features * 6),
         name="merge_dw",
     )(merged_in, gm, own_att, grad_mixed)
-    sum_merge = reduce_all(dw_merge)
+    sum_m = reduce_all(dw_merge)
 
     grad_win = pl.pallas_call(
-        assemble_kernel,
+        functools.partial(assemble_kernel, stride),
         grid=(count_a,),
         in_specs=halo_specs,
         out_specs=rows_of(padded, features),
         out_shape=jax.ShapeDtypeStruct((tall3, features), BF),
-        scratch_shapes=[pltpu.VMEM((padded, features), F32)],
+        scratch_shapes=[buf_scratch, win_scratch],
         compiler_params=params(1),
         cost_estimate=cost(total * features * 1200, 2 * total * features * 3),
         name="assemble",
-    )(grad_att, *att_halos, *mats)
+    )(grad_att, *halo_args(att_halos))
     calls = CALLS
     wide = features // calls
     grad_qkv = None
@@ -543,23 +563,23 @@
         cost_estimate=cost(2 * total * features * 3 * features, 2 * total * features * 5),
         name="qkv_dw",
     )(normed, grad_qkv)
-    sum_q = reduce_all(dw_q.reshape(3 * features, features)).reshape(3, features, features)
-
-    shifted = to_shifted(tokens, tok_halos).reshape(total, features)
+    sum_q = reduce_all(dw_q.reshape(3 * features, features))
+
     grad_inputs, *in_edges = pl.pallas_call(
-        input_grad_kernel,
+        functools.partial(input_grad_kernel, stride),
         grid=(count_a,),
-        in_specs=[qkv_spec, rows_of(block, features), whole((1, features)),
-                  whole((features, 3 * features)), whole((block, padded))],
+        in_specs=[qkv_spec, rows_of(padded, features), whole((1, features)),
+                  whole((features, 3 * features))],
         out_specs=[rows_of(block, features)] + edge_specs,
-        out_shape=[jax.ShapeDtypeStruct((total, features), F32)] + edge_types,
+        out_shape=[jax.ShapeDtypeStruct((total, features), BF)] + edge_types,
+        scratch_shapes=[win_scratch, grid_scratch],
         compiler_params=params(1),
         cost_estimate=cost(2 * total * features * 3 * features, 2 * total * features * 6),
         name="input_grad",
-    )(grad_qkv, shifted, gain_a, w_qkv, to_grid)
+    )(grad_qkv, tok_win, gain_a, w_qkv)
     in_parts = exchange(in_edges, -1)
     grad_own = to_own(grad_inputs.reshape(rows, cols, features), in_parts)
-    grad_tokens = grad_own + grad_mixed.reshape(rows, cols, features).astype(F32)
+    grad_tokens = grad_own.astype(F32) + grad_mixed.reshape(rows, cols, features).astype(F32)
 
     merged = pl.pallas_call(
         merged_kernel,
@@ -572,13 +592,58 @@
         name="merged",
     )(merged_in, w_merge).reshape(grad_merged.shape)
 
-    grad_w_merge = sum_merge[: 4 * features].astype(F32)
-    grad_w_out = jnp.concatenate(
-        [sum_merge[4 * features :, k * features : (k + 1) * features] for k in range(features // rest)], 0
-    ).astype(F32)
-    grad_w_qkv = jnp.concatenate([sum_q[t] for t in range(3)], axis=1).astype(F32)
-    grad_gain_merge = jnp.sum(grad_w_merge * w_merge.astype(F32), axis=1) / gain_merge
-    grad_gain_attn = jnp.sum(grad_w_qkv * w_qkv.astype(F32), axis=1) / gain_attn
+    def halves(height, width, half):
+        def spot(mine):
+            def index(i, keep):
+                side, place = i // half, i % half
+                other = jnp.where(side < (keep[0] if mine else 1 - keep[0]), 0, half - 1)
+                return jnp.where((side == keep[0]) == mine, place, other), 0
+
+            return index
+
+        return [pl.BlockSpec((height, width), spot(True)), pl.BlockSpec((height, width), spot(False))]
+
+    m_own, m_got, keep = sum_m
+    grad_w_merge, grad_w_out, grad_gain_merge = pl.pallas_call(
+        functools.partial(merge_last_kernel, pieces // 2),
+        grid_spec=pltpu.PrefetchScalarGridSpec(
+            num_scalar_prefetch=1,
+            grid=(pieces,),
+            in_specs=halves(features, width2 + rest, pieces // 2) + [
+                pl.BlockSpec((features, width2), lambda i, k: (i, 0)),
+                pl.BlockSpec((1, features), lambda i, k: (0, i))],
+            out_specs=[pl.BlockSpec((features, width2), lambda i, k: (i, 0)),
+                       pl.BlockSpec((features, rest), lambda i, k: (0, i)),
+                       pl.BlockSpec((1, features), lambda i, k: (0, i))],
+        ),
+        out_shape=[jax.ShapeDtypeStruct((pieces * features, width2), F32),
+                   jax.ShapeDtypeStruct((features, features), F32),
+                   jax.ShapeDtypeStruct((1, pieces * features), F32)],
+        compiler_params=params(1),
+        cost_estimate=cost(total * features * 2000, 2 * total * features * 6),
+        name="m_last",
+    )(keep, m_own, m_got, w_merge, gain_m)
+    q_own, q_got, keep = sum_q
+    tile = features // 2
+    grad_w_qkv, grad_gain_attn = pl.pallas_call(
+        functools.partial(qkv_last_kernel, 3),
+        grid_spec=pltpu.PrefetchScalarGridSpec(
+            num_scalar_prefetch=1,
+            grid=(6,),
+            in_specs=halves(tile, features, 3) + [
+                pl.BlockSpec((tile, features), lambda i, k: (i % 2, i // 2)),
+                pl.BlockSpec((2, tile), lambda i, k: (0, 0))],
+            out_specs=[pl.BlockSpec((tile, features), lambda i, k: (i % 2, i // 2)),
+                       pl.BlockSpec((2, tile), lambda i, k: (0, 0))],
+        ),
+        out_shape=[jax.ShapeDtypeStruct((features, 3 * features), F32),
+                   jax.ShapeDtypeStruct((2, tile), F32)],
+        compiler_params=params(1),
+        cost_estimate=cost(total * features * 1000, 2 * total * features * 3),
+        name="q_last",
+    )(keep, q_own, q_got, w_qkv, gain_attn.reshape(2, tile))
+    grad_gain_merge = grad_gain_merge.reshape(-1)
+    grad_gain_attn = grad_gain_attn.reshape(-1)
     return (merged, grad_tokens, grad_gain_attn, grad_w_qkv, grad_w_out, grad_gain_merge,
             grad_w_merge)
 

time: 237 us -> 235 us (level)
  other arithmetic: 37.9 us -> 20.7 us
  waiting for transfers between devices: 62.8 us -> 75.8 us
  Pallas kernels: 79.2 us -> 83.2 us
    ppermute x6, waiting for transfers between devices: 11.1 us -> 21.6 us  [reduce_all(): received = lax.ppermute(value, 'lon', pairs)]
    pallas_call x3 -> x5, Pallas kernels: 22.5 us -> 31.5 us  [the longest x1 8.26 us: on_device_body(): pl.pallas_call(functools.partial(merge_last_kernel, pieces // 2), grid_sp...]
    reduce_sum x2 -> x0, other arithmetic: 6.02 us -> none  [the longest x1 3.96 us: on_device_body(): jnp.sum(grad_w_merge * w_merge.astype(F32), axis=1) / gain_merge]
    pallas_call x1, Pallas kernels: 16.1 us -> 11.2 us  [on_device_body(): pl.pallas_call(functools.partial(forward_kernel, stride, count_b), grid=(...]
    select_n x6 -> x4, other arithmetic: 7.96 us -> 3.04 us  [join(): first = jnp.where(keep == 0, value, received)]
    concatenate x2 -> x0, other arithmetic: 2.38 us -> none  [the longest x1 1.62 us: to_shifted(): return jnp.concatenate([top, bottom], axis=0)]
  transfers between devices with their start and end apart: 36 -> 36, of which waited for: 14 -> 14; matrix products, arithmetic and copies ran while one was open for 12% -> 9% of each run, Pallas kernels for 20% -> 21%
where the time goes in v1:
time: 235 us; the launch traced here: 234 us
  Pallas kernels  83.2 us (35%)
  waiting for transfers between devices  75.8 us (32%)
  starting transfers between devices  40.8 us (17%)
  other arithmetic  20.7 us (9%)
  local copies, waits for them, and re-layouts  12.5 us (5%)
    ppermute x6, waiting for transfers between devices, reduce_all(): received = lax.ppermute(sent, 'lon', pairs)  27 us
    ppermute x6, waiting for transfers between devices, reduce_all(): received = lax.ppermute(value, 'lon', pairs)  21.6 us
    pallas_call x4, Pallas kernels, on_device_body(): pl.pallas_call(body, grid=(count_a,), in_specs=specs, out_specs=spec, out...  18.2 us
    ppermute x12, starting transfers between devices, send(): return lax.ppermute(value, ('lat', 'lon'), pairs)  14.1 us
    ppermute x6, waiting for transfers between devices, reduce_all(): received = lax.ppermute(mine, 'lat', [(i, i ^ d) for i in range(count_lat)])  11.3 us
    pallas_call x1, Pallas kernels, on_device_body(): pl.pallas_call(functools.partial(forward_kernel, stride, count_b), grid=(...  11.2 us
    ppermute x12, waiting for transfers between devices, send(): return lax.ppermute(value, ('lat', 'lon'), pairs)  10.3 us
    convert_element_type x6, other arithmetic, part_sum(): return sum(parts[1:], parts[0]).astype(BF)  9.54 us
  transfers between devices with their start and end apart: 36, of which 14 were waited for; matrix products, arithmetic and copies ran while one was open for 9% of the time, Pallas kernels for 21%

profile of v1, /device:TPU:0, one launch (start us, length us, event | category | flops | bytes accessed | tf_op | source)
XLA Modules:
  0.0 234.0 jit_solution(9286685851117950458)
XLA Ops:
  0.6 0.9 slice_bitcast_fusion
  2.1 0.9 slice.37
  3.0 2.6 %collective-permute-start.1 = (bf16[144,512]{1,0:T(8,128)(2,1)S(1)}, bf16[144,512]{1,0:T(8,128)(2,1)S(1)}, u32[]{:S(2)}, u32[]{:S(2)}) collective-permute-start(bf16[144,512]{1,0:T(8,128)(2,1)S(1)} %bitcast.48), channel_id=1, source_target_pairs={{0,8},{1,9},{2,10},{3,11},{4,12},{5,13},{6,14},{7,15},{8,16},{9,17... | collective-permute-start | bytes 442376 | tf_op jit(solution)/shard_map/ppermute | solution.py:331
  6.4 2.5 %collective-permute-start.2 = (bf16[24,512]{1,0:T(8,128)(2,1)S(1)}, bf16[24,512]{1,0:T(8,128)(2,1)S(1)}, u32[]{:S(2)}, u32[]{:S(2)}) collective-permute-start(bf16[24,512]{1,0:T(8,128)(2,1)S(1)} %slice_bitcast_fusion.1), channel_id=1, source_target_pairs={{0,9},{1,10},{2,11},{3,12},{4,13},{5,14},{6,15},{7,8},{8,17},{9,18... | collective-permute-start | bytes 73736 | tf_op jit(solution)/shard_map/ppermute | solution.py:331
  11.5 2.9 %collective-permute-done.2 = bf16[24,512]{1,0:T(8,128)(2,1)S(1)} collective-permute-done((bf16[24,512]{1,0:T(8,128)(2,1)S(1)}, bf16[24,512]{1,0:T(8,128)(2,1)S(1)}, u32[]{:S(2)}, u32[]{:S(2)}) %collective-permute-start.2) | collective-permute-done | bytes 24608 | tf_op jit(solution)/shard_map/ppermute | solution.py:331
  15.1 11.2 %attn_fwd.1 = (bf16[1152,512]{1,0:T(8,128)(2,1)}, bf16[3,1280,512]{2,1,0:T(8,128)(2,1)}, bf16[1280,512]{1,0:T(8,128)(2,1)}, bf16[1280,512]{1,0:T(8,128)(2,1)}, b...) custom-call(bf16[1152,512]{1,0:T(8,128)(2,1)} %bitcast.51, ...), custom_call_target="tpu_custom_call" | custom-call | flops 3623878656 | bytes 9437184 | tf_op jit(solution)/shard_map/attn_fwd/pallas_call | solution.py:450
  26.9 1.7 collective-permute-start.4
  29.0 5.2 %grad_in.1.grad_in_ref = bf16[288,2048]{1,0:T(8,128)(2,1)} custom-call(bf16[288,1024]{1,0:T(8,128)(2,1)} %bitcast.42, bf16[2048,1024]{1,0:T(8,128)(2,1)} %w_ref.9), custom_call_target="tpu_custom_call" | custom-call | flops 1207959552 | bytes 4718592 | tf_op jit(solution)/shard_map/grad_in/pallas_call | solution.py:471
  34.7 1.2 maximum_maximum_fusion
  35.9 6.8 %merge_mid.1 = (bf16[288,2048]{1,0:T(8,128)(2,1)}, bf16[1152,512]{1,0:T(8,128)(2,1)}, bf16[1152,512]{1,0:T(8,128)(2,1)}, bf16[192,512]{1,0:T(8,128)(2,1)}, bf16[...) custom-call(bf16[1152,512]{1,0:T(8,128)(2,1)} %bitcast.52, bf16[1152,512]{1,0:T(8,128)(2,1)} %bitcast.37, ...), custom_call_target="tpu_custom_call" | custom-call | flops 2415919104 | bytes 7077888 | tf_op jit(solution)/shard_map/merge_mid/pallas_call | solution.py:485
  42.7 7.2 %merge_dw.1 = bf16[2048,1152]{1,0:T(8,128)(2,1)} custom-call(bf16[288,2048]{1,0:T(8,128)(2,1)} %get-tuple-element.34.a_ref.merged_in_ref, bf16[288,1024]{1,0:T(8,128)(2,1)} %bitcast.43, bf16[1152,512]{1,0:T(8,128)(2,1)} %bitcast.38, bf16[1152,512]{1,0:T(8,128)(2,1)} %get-tuple-element.46.gmix_ref), custom_call_target="tpu_custom_call" | custom-call | flops 2415919104 | bytes 7077888 | tf_op jit(solution)/shard_map/merge_dw/pallas_call | solution.py:504
  49.9 1.8 constant_dynamic-slice_fusion
  52.1 4.4 %collective-permute-done.24 = bf16[1024,1152]{1,0:T(8,128)(2,1)} collective-permute-done((bf16[1024,1152]{1,0:T(8,128)(2,1)S(1)}, bf16[1024,1152]{1,0:T(8,128)(2,1)}, u32[]{:S(2)}, u32[]{:S(2)}) %collective-permute-start.24) | collective-permute-done | bytes 2359328 | tf_op jit(solution)/shard_map/ppermute | solution.py:385
  56.5 2.1 add_convert_fusion
  58.6 0.8 collective-permute-start.25
  59.4 15.4 %collective-permute-done.25 = bf16[512,1152]{1,0:T(8,128)(2,1)S(1)} collective-permute-done((bf16[512,1152]{1,0:T(8,128)(2,1)S(1)}, bf16[512,1152]{1,0:T(8,128)(2,1)S(1)}, u32[]{:S(2)}, u32[]{:S(2)}) %collective-permute-start.25) | collective-permute-done | bytes 1179680 | tf_op jit(solution)/shard_map/ppermute | solution.py:385
  74.9 1.6 add_convert_fusion.1
  77.3 1.5 collective-permute-start.7
  78.8 1.4 collective-permute-start.8
  80.2 7.3 %collective-permute-done.8 = bf16[24,512]{1,0:T(8,128)(2,1)S(1)} collective-permute-done((bf16[24,512]{1,0:T(8,128)(2,1)S(1)}, bf16[24,512]{1,0:T(8,128)(2,1)S(1)}, u32[]{:S(2)}, u32[]{:S(2)}) %collective-permute-start.8) | collective-permute-done | bytes 24608 | tf_op jit(solution)/shard_map/ppermute | solution.py:331
  88.3 3.3 %assemble.1.ga_ref = bf16[1280,512]{1,0:T(8,128)(2,1)} custom-call(bf16[1152,512]{1,0:T(8,128)(2,1)} %get-tuple-element.35.own_ref, bf16[24,8,512]{2,1,0:T(8,128)(2,1)} %bitcast.45, bf16[144,512]{1,0:T(8,128)(2,1)} %copy-done.6, bf16[3,8,512]{2,1,0:T(8,128)(2,1)} %bitcast.53), custom_call_target="tpu_custom_call" | custom-call | flops 707788800 | bytes 3538944 | tf_op jit(solution)/shard_map/assemble/pallas_call | solution.py:518
  91.6 4.5 %shard_map.153.prev_ref = bf16[3,1280,512]{2,1,0:T(8,128)(2,1)} custom-call(bf16[1280,512]{1,0:T(8,128)(2,1)} %assemble.1.ga_ref, bf16[3,1280,512]{2,1,0:T(8,128)(2,1)} %get-tuple-element.39.qkv_ref, bf16[4,2560,80]{2,1,0:T(8,128)(2,1)} %get-tuple-element.40.prob_ref), custom_call_target="tpu_custom_call" | custom-call | flops 905969664 | bytes 2359296 | tf_op jit(solution)/shard_map/pallas_call | solution.py:544
  96.1 4.6 %shard_map.154.prev_ref = bf16[3,1280,512]{2,1,0:T(8,128)(2,1)} custom-call(bf16[1280,512]{1,0:T(8,128)(2,1)} %assemble.1.ga_ref, bf16[3,1280,512]{2,1,0:T(8,128)(2,1)} %get-tuple-element.39.qkv_ref, bf16[4,2560,80]{2,1,0:T(8,128)(2,1)} %get-tuple-element.40.prob_ref, bf16[3,1280,512]{2,1,0:T(8,128)(2,1)} %shard_map.153.prev_ref), custom_call_target="tpu_custom_call", output_to_operand_aliasing={{}: (3, {})} | custom-call | flops 905969664 | bytes 2359296 | tf_op jit(solution)/shard_map/pallas_call | solution.py:544
  100.7 1.7 add_convert_fusion.7
  102.4 2.3 collective-permute-start.29
  105.4 1.5 collective-permute-start.27
  106.9 4.5 %shard_map.155.prev_ref = bf16[3,1280,512]{2,1,0:T(8,128)(2,1)} custom-call(bf16[1280,512]{1,0:T(8,128)(2,1)} %assemble.1.ga_ref, bf16[3,1280,512]{2,1,0:T(8,128)(2,1)} %get-tuple-element.39.qkv_ref, bf16[4,2560,80]{2,1,0:T(8,128)(2,1)} %get-tuple-element.40.prob_ref, bf16[3,1280,512]{2,1,0:T(8,128)(2,1)} %shard_map.154.prev_ref), custom_call_target="tpu_custom_call", output_to_operand_aliasing={{}: (3, {})} | custom-call | flops 905969664 | bytes 2359296 | tf_op jit(solution)/shard_map/pallas_call | solution.py:544
  111.4 4.5 %shard_map.156.gqkv_ref = bf16[3,1280,512]{2,1,0:T(8,128)(2,1)} custom-call(bf16[1280,512]{1,0:T(8,128)(2,1)} %assemble.1.ga_ref, bf16[3,1280,512]{2,1,0:T(8,128)(2,1)} %get-tuple-element.39.qkv_ref, bf16[4,2560,80]{2,1,0:T(8,128)(2,1)} %get-tuple-element.40.prob_ref, bf16[3,1280,512]{2,1,0:T(8,128)(2,1)} %shard_map.155.prev_ref), custom_call_target="tpu_custom_call", output_to_operand_aliasing={{}: (3, {})} | custom-call | flops 905969664 | bytes 2359296 | tf_op jit(solution)/shard_map/pallas_call | solution.py:544
  116.7 1.2 constant_dynamic-update-slice_fusion.5
  118.0 5.7 %qkv_dw.1 = bf16[3,512,512]{2,1,0:T(8,128)(2,1)} custom-call(bf16[1280,512]{1,0:T(8,128)(2,1)} %get-tuple-element.47.normed_ref, bf16[3,1280,512]{2,1,0:T(8,128)(2,1)} %shard_map.156.gqkv_ref), custom_call_target="tpu_custom_call" | custom-call | flops 1811939328 | bytes 5898240 | tf_op jit(solution)/shard_map/qkv_dw/pallas_call | solution.py:555
  123.7 1.3 constant_dynamic-slice_fusion.1
  125.0 2.9 %collective-permute-start.31 = (bf16[64,1152]{1,0:T(8,128)(2,1)S(1)}, bf16[64,1152]{1,0:T(8,128)(2,1)S(1)}, u32[]{:S(2)}, u32[]{:S(2)}) collective-permute-start(bf16[64,1152]{1,0:T(8,128)(2,1)S(1)} %get-tuple-element.54), channel_id=1, source_target_pairs={{0,16},{8,24},{16,0},{24,8},{1,17},{9,25},{17,1},{25,9},{2,18},{10... | collective-permute-start | bytes 442376 | tf_op jit(solution)/shard_map/ppermute | solution.py:397
  128.0 1.5 collective-permute-start.32
  129.5 9.6 %collective-permute-done.31 = bf16[64,1152]{1,0:T(8,128)(2,1)S(1)} collective-permute-done((bf16[64,1152]{1,0:T(8,128)(2,1)S(1)}, bf16[64,1152]{1,0:T(8,128)(2,1)S(1)}, u32[]{:S(2)}, u32[]{:S(2)}) %collective-permute-start.31) | collective-permute-done | bytes 147488 | tf_op jit(solution)/shard_map/ppermute | solution.py:397
  139.1 1.4 collective-permute-start.33
  140.5 1.9 add_convert_fusion.2
  143.2 10.2 %collective-permute-done.33 = bf16[256,1152]{1,0:T(8,128)(2,1)} collective-permute-done((bf16[256,1152]{1,0:T(8,128)(2,1)S(1)}, bf16[256,1152]{1,0:T(8,128)(2,1)}, u32[]{:S(2)}, u32[]{:S(2)}) %collective-permute-start.33) | collective-permute-done | bytes 589856 | tf_op jit(solution)/shard_map/ppermute | solution.py:400
  153.4 1.2 broadcast_select_fusion.3
  154.6 1.1 pad_maximum_fusion.1
  155.7 1.4 collective-permute-start.34
  157.1 1.2 add_convert_fusion.3
  159.0 7.1 %collective-permute-done.14 = bf16[192,512]{1,0:T(8,128)(2,1)S(1)} collective-permute-done((bf16[192,512]{1,0:T(8,128)(2,1)S(1)}, bf16[192,512]{1,0:T(8,128)(2,1)S(1)}, u32[]{:S(2)}, u32[]{:S(2)}) %collective-permute-start.14) | collective-permute-done | bytes 196640 | tf_op jit(solution)/shard_map/ppermute | solution.py:385
  166.1 1.1 add_convert_fusion.11
  167.2 1.5 collective-permute-start.17
  168.7 3.2 %collective-permute-start.16 = (bf16[48,512]{1,0:T(8,128)(2,1)S(1)}, bf16[48,512]{1,0:T(8,128)(2,1)S(1)}, u32[]{:S(2)}, u32[]{:S(2)}) collective-permute-start(bf16[48,512]{1,0:T(8,128)(2,1)S(1)} %get-tuple-element.62), channel_id=1, source_target_pairs={{0,16},{8,24},{16,0},{24,8},{1,17},{9,25},{17,1},{25,9},{2,18},{10... | collective-permute-start | bytes 147464 | tf_op jit(solution)/shard_map/ppermute | solution.py:391
  171.9 1.4 collective-permute-done.17
  173.3 3.5 %collective-permute-done.16 = bf16[48,512]{1,0:T(8,128)(2,1)S(1)} collective-permute-done((bf16[48,512]{1,0:T(8,128)(2,1)S(1)}, bf16[48,512]{1,0:T(8,128)(2,1)S(1)}, u32[]{:S(2)}, u32[]{:S(2)}) %collective-permute-start.16) | collective-permute-done | bytes 49184 | tf_op jit(solution)/shard_map/ppermute | solution.py:391
  176.8 0.9 constant_dynamic-update-slice_fusion.3
  177.9 2.2 collective-permute-start.19
  180.1 2.1 collective-permute-start.20
  182.2 1.7 broadcast_select_fusion.1
  184.3 1.7 collective-permute-done.20
  186.0 0.9 collective-permute-start.21
  186.9 4.8 %collective-permute-done.21 = bf16[192,512]{1,0:T(8,128)(2,1)S(1)} collective-permute-done((bf16[192,512]{1,0:T(8,128)(2,1)S(1)}, bf16[192,512]{1,0:T(8,128)(2,1)S(1)}, u32[]{:S(2)}, u32[]{:S(2)}) %collective-permute-start.21) | collective-permute-done | bytes 196640 | tf_op jit(solution)/shard_map/ppermute | solution.py:400
  191.7 1.2 collective-permute-start.22
  193.0 6.6 %collective-permute-done.22 = bf16[384,512]{1,0:T(8,128)(2,1)S(1)} collective-permute-done((bf16[384,512]{1,0:T(8,128)(2,1)S(1)}, bf16[384,512]{1,0:T(8,128)(2,1)S(1)}, u32[]{:S(2)}, u32[]{:S(2)}) %collective-permute-start.22) | collective-permute-done | bytes 393248 | tf_op jit(solution)/shard_map/ppermute | solution.py:400
  199.9 7.0 %input_grad.1 = (bf16[1152,512]{1,0:T(8,128)(2,1)}, bf16[192,512]{1,0:T(8,128)(2,1)}, bf16[144,512]{1,0:T(8,128)(2,1)}, bf16[24,512]{1,0:T(8,128)(2,1)}) custom-call(bf16[3,1280,512]{2,1,0:T(8,128)(2,1)} %shard_map.156.gqkv_ref, bf16[1280,512]{1,0:T(8,128)(2,1)} %get-tuple-element.41.x_ref, f32[1,512]{1,0:T(1,128)} %bitcast.57, bf16[512,1536]{1,0:T(8,128)(2,1)} %w_ref.8), custom_call_target="tpu_custom_call" | custom-call | flops 1811939328 | bytes 7077888 | tf_op jit(solution)/shard_map/input_grad/pallas_call | solution.py:568
  207.5 2.3 collective-permute-start.10
  210.4 4.7 %merged.1 = bf16[288,1024]{1,0:T(8,128)(2,1)} custom-call(bf16[288,2048]{1,0:T(8,128)(2,1)} %get-tuple-element.34.a_ref.merged_in_ref, bf16[2048,1024]{1,0:T(8,128)(2,1)} %w_ref.9), custom_call_target="tpu_custom_call" | custom-call | flops 1207959552 | bytes 4718592 | tf_op jit(solution)/shard_map/merged/pallas_call | solution.py:584
  215.1 1.7 slice.52
  216.9 1.9 convert_add_fusion
  218.8 5.7 %q_last.1 = (f32[512,1536]{1,0:T(8,128)}, f32[2,256]{1,0:T(2,128)}) custom-call(s32[1]{0:T(128)} %bitcast.22.keep_ref, bf16[768,512]{1,0:T(8,128)(2,1)} %copy-done.2, bf16[768,512]{1,0:T(8,128)(2,1)} %collective-permute-done.23.got_ref, bf16[512,1536]{1,0:T(8,128)(2,1)} %w_ref.8, f32[2,256]{1,0:T(2,128)} %reshape.129.gain_ref), custom_call_target="tpu_custom_call" | custom-call | flops 589824000 | bytes 3538944 | tf_op jit(solution)/shard_map/q_last/pallas_call | solution.py:628
  224.5 1.3 copy.20
  225.7 8.3 %m_last.1 = (f32[2048,1024]{1,0:T(8,128)}, f32[512,512]{1,0:T(8,128)}, f32[1,2048]{1,0:T(1,128)}) custom-call(s32[1]{0:T(128)} %bitcast.22.keep_ref, bf16[1024,1152]{1,0:T(8,128)(2,1)} %copy-done, bf16[1024,1152]{1,0:T(8,128)(2,1)} %collective-permute-done.35.got_ref, bf16[2048,1024]{1,0:T(8,128)(2,1)} %w_ref.9, f32[1,2048]{1,0:T(1,128)} %bitcast.59), custom_call_target="tpu_custom_call" | custom-call | flops 1179648000 | bytes 7077888 | tf_op jit(solution)/shard_map/m_last/pallas_call | solution.py:607
  (99 shorter events, 13.0 us)
Async XLA Ops:
  1.6 12.8 %collective-permute-start = (bf16[192,512]{1,0:T(8,128)(2,1)S(1)}, bf16[192,512]{1,0:T(8,128)(2,1)S(1)}, u32[]{:S(2)}, u32[]{:S(2)}) collective-permute-start(bf16[192,512]{1,0:T(8,128)(2,1)S(1)} %slice_bitcast_fusion), channel_id=1, source_target_pairs={{0,1},{1,2},{2,3},{3,4},{4,5},{5,6},{6,7},{7,0},{8,9},{9,10},{10,1... | collective-permute-start | bytes 589832 | tf_op jit(solution)/shard_map/ppermute | solution.py:331
  3.0 11.3 %collective-permute-start.1 = (bf16[144,512]{1,0:T(8,128)(2,1)S(1)}, bf16[144,512]{1,0:T(8,128)(2,1)S(1)}, u32[]{:S(2)}, u32[]{:S(2)}) collective-permute-start(bf16[144,512]{1,0:T(8,128)(2,1)S(1)} %bitcast.48), channel_id=1, source_target_pairs={{0,8},{1,9},{2,10},{3,11},{4,12},{5,13},{6,14},{7,15},{8,16},{9,17... | collective-permute-start | bytes 442376 | tf_op jit(solution)/shard_map/ppermute | solution.py:331
  6.4 8.0 %collective-permute-start.2 = (bf16[24,512]{1,0:T(8,128)(2,1)S(1)}, bf16[24,512]{1,0:T(8,128)(2,1)S(1)}, u32[]{:S(2)}, u32[]{:S(2)}) collective-permute-start(bf16[24,512]{1,0:T(8,128)(2,1)S(1)} %slice_bitcast_fusion.1), channel_id=1, source_target_pairs={{0,9},{1,10},{2,11},{3,12},{4,13},{5,14},{6,15},{7,8},{8,17},{9,18... | collective-permute-start | bytes 73736 | tf_op jit(solution)/shard_map/ppermute | solution.py:331
  14.4 0.6 copy-start.14
  14.4 0.7 copy-start.12
  14.4 0.7 copy-start.10
  26.3 8.4 %collective-permute-start.3 = (bf16[192,512]{1,0:T(8,128)(2,1)}, bf16[192,512]{1,0:T(8,128)(2,1)S(1)}, u32[]{:S(2)}, u32[]{:S(2)}) collective-permute-start(bf16[192,512]{1,0:T(8,128)(2,1)} %get-tuple-element.31), channel_id=1, source_target_pairs={{0,7},{1,0},{2,1},{3,2},{4,3},{5,4},{6,5},{7,6},{8,15},{9,8},{10,9... | collective-permute-start | bytes 589832 | tf_op jit(solution)/shard_map/ppermute | solution.py:331
  26.9 7.7 %collective-permute-start.4 = (bf16[144,512]{1,0:T(8,128)(2,1)}, bf16[144,512]{1,0:T(8,128)(2,1)S(1)}, u32[]{:S(2)}, u32[]{:S(2)}) collective-permute-start(bf16[144,512]{1,0:T(8,128)(2,1)} %get-tuple-element.32), channel_id=1, source_target_pairs={{0,24},{1,25},{2,26},{3,27},{4,28},{5,29},{6,30},{7,31},{8,0},{9,1... | collective-permute-start | bytes 442376 | tf_op jit(solution)/shard_map/ppermute | solution.py:331
  28.7 6.0 %collective-permute-start.5 = (bf16[24,512]{1,0:T(8,128)(2,1)}, bf16[24,512]{1,0:T(8,128)(2,1)S(1)}, u32[]{:S(2)}, u32[]{:S(2)}) collective-permute-start(bf16[24,512]{1,0:T(8,128)(2,1)} %get-tuple-element.33), channel_id=1, source_target_pairs={{0,31},{1,24},{2,25},{3,26},{4,27},{5,28},{6,29},{7,30},{8,7},{9,0... | collective-permute-start | bytes 73736 | tf_op jit(solution)/shard_map/ppermute | solution.py:331
  29.0 5.2 %copy-start.4 = (bf16[1152,512]{1,0:T(8,128)(2,1)S(1)}, bf16[1152,512]{1,0:T(8,128)(2,1)}, u32[]{:S(2)}) copy-start(bf16[1152,512]{1,0:T(8,128)(2,1)} %get-tuple-element.30) | copy-start | bytes 3538948
  51.8 4.7 %collective-permute-start.24 = (bf16[1024,1152]{1,0:T(8,128)(2,1)S(1)}, bf16[1024,1152]{1,0:T(8,128)(2,1)}, u32[]{:S(2)}, u32[]{:S(2)}) collective-permute-start(bf16[1024,1152]{1,0:T(8,128)(2,1)S(1)} %constant_dynamic-slice_fusion), channel_id=1, source_target_pairs={{0,1},{1,0},{2,3},{3,2},{4,5},{5,4},{6,7},{7,6},{8,9},{9,8},{10,11... | collective-permute-start | bytes 7077896 | tf_op jit(solution)/shard_map/ppermute | solution.py:385
  58.6 18.7 %copy-start.9 = (bf16[192,512]{1,0:T(8,128)(2,1)S(1)}, bf16[192,512]{1,0:T(8,128)(2,1)}, u32[]{:S(2)}) copy-start(bf16[192,512]{1,0:T(8,128)(2,1)} %get-tuple-element.36) | copy-start | bytes 589828
  58.6 18.7 %copy-start.11 = (bf16[144,512]{1,0:T(8,128)(2,1)S(1)}, bf16[144,512]{1,0:T(8,128)(2,1)}, u32[]{:S(2)}) copy-start(bf16[144,512]{1,0:T(8,128)(2,1)} %get-tuple-element.37) | copy-start | bytes 442372
  58.6 20.2 %copy-start.13 = (bf16[24,512]{1,0:T(8,128)(2,1)S(1)}, bf16[24,512]{1,0:T(8,128)(2,1)}, u32[]{:S(2)}) copy-start(bf16[24,512]{1,0:T(8,128)(2,1)} %get-tuple-element.38) | copy-start | bytes 73732
  58.6 16.3 %collective-permute-start.25 = (bf16[512,1152]{1,0:T(8,128)(2,1)S(1)}, bf16[512,1152]{1,0:T(8,128)(2,1)S(1)}, u32[]{:S(2)}, u32[]{:S(2)}) collective-permute-start(bf16[512,1152]{1,0:T(8,128)(2,1)S(1)} %add_convert_fusion), channel_id=1, source_target_pairs={{0,2},{1,5},{2,0},{3,7},{4,6},{5,1},{6,4},{7,3},{8,10},{9,13},{10,... | collective-permute-start | bytes 3538952 | tf_op jit(solution)/shard_map/ppermute | solution.py:385
  76.5 24.2 %collective-permute-start.26 = (bf16[256,1152]{1,0:T(8,128)(2,1)S(1)}, bf16[256,1152]{1,0:T(8,128)(2,1)S(1)}, u32[]{:S(2)}, u32[]{:S(2)}) collective-permute-start(bf16[256,1152]{1,0:T(8,128)(2,1)S(1)} %add_convert_fusion.1), channel_id=1, source_target_pairs={{0,4},{1,3},{2,6},{3,1},{4,0},{5,7},{6,2},{7,5},{8,12},{9,11},{10,... | collective-permute-start | bytes 1769480 | tf_op jit(solution)/shard_map/ppermute | solution.py:385
  77.3 10.3 %collective-permute-start.6 = (bf16[192,512]{1,0:T(8,128)(2,1)S(1)}, bf16[192,512]{1,0:T(8,128)(2,1)S(1)}, u32[]{:S(2)}, u32[]{:S(2)}) collective-permute-start(bf16[192,512]{1,0:T(8,128)(2,1)S(1)} %copy-done.9), channel_id=1, source_target_pairs={{0,1},{1,2},{2,3},{3,4},{4,5},{5,6},{6,7},{7,0},{8,9},{9,10},{10,1... | collective-permute-start | bytes 589832 | tf_op jit(solution)/shard_map/ppermute | solution.py:331
  77.3 10.2 %collective-permute-start.7 = (bf16[144,512]{1,0:T(8,128)(2,1)S(1)}, bf16[144,512]{1,0:T(8,128)(2,1)S(1)}, u32[]{:S(2)}, u32[]{:S(2)}) collective-permute-start(bf16[144,512]{1,0:T(8,128)(2,1)S(1)} %copy-done.11), channel_id=1, source_target_pairs={{0,8},{1,9},{2,10},{3,11},{4,12},{5,13},{6,14},{7,15},{8,16},{9,17... | collective-permute-start | bytes 442376 | tf_op jit(solution)/shard_map/ppermute | solution.py:331
  78.8 8.7 %collective-permute-start.8 = (bf16[24,512]{1,0:T(8,128)(2,1)S(1)}, bf16[24,512]{1,0:T(8,128)(2,1)S(1)}, u32[]{:S(2)}, u32[]{:S(2)}) collective-permute-start(bf16[24,512]{1,0:T(8,128)(2,1)S(1)} %copy-done.13), channel_id=1, source_target_pairs={{0,9},{1,10},{2,11},{3,12},{4,13},{5,14},{6,15},{7,8},{8,17},{9,18... | collective-permute-start | bytes 73736 | tf_op jit(solution)/shard_map/ppermute | solution.py:331
  87.5 0.6 copy-start.7
  87.5 0.7 copy-start.6
  87.6 0.7 copy-start.5
  102.4 13.5 %collective-permute-start.29 = (bf16[64,1152]{1,0:T(8,128)(2,1)S(1)}, bf16[64,1152]{1,0:T(8,128)(2,1)S(1)}, u32[]{:S(2)}, u32[]{:S(2)}) collective-permute-start(bf16[64,1152]{1,0:T(8,128)(2,1)S(1)} %get-tuple-element.58), channel_id=1, source_target_pairs={{0,24},{8,16},{16,8},{24,0},{1,25},{9,17},{17,9},{25,1},{2,26},{10... | collective-permute-start | bytes 442376 | tf_op jit(solution)/shard_map/ppermute | solution.py:391
  104.7 11.9 %collective-permute-start.28 = (bf16[64,1152]{1,0:T(8,128)(2,1)S(1)}, bf16[64,1152]{1,0:T(8,128)(2,1)S(1)}, u32[]{:S(2)}, u32[]{:S(2)}) collective-permute-start(bf16[64,1152]{1,0:T(8,128)(2,1)S(1)} %get-tuple-element.59), channel_id=1, source_target_pairs={{0,16},{8,24},{16,0},{24,8},{1,17},{9,25},{17,1},{25,9},{2,18},{10... | collective-permute-start | bytes 442376 | tf_op jit(solution)/shard_map/ppermute | solution.py:391
  105.4 11.3 %collective-permute-start.27 = (bf16[64,1152]{1,0:T(8,128)(2,1)S(1)}, bf16[64,1152]{1,0:T(8,128)(2,1)S(1)}, u32[]{:S(2)}, u32[]{:S(2)}) collective-permute-start(bf16[64,1152]{1,0:T(8,128)(2,1)S(1)} %get-tuple-element.57), channel_id=1, source_target_pairs={{0,8},{8,0},{16,24},{24,16},{1,9},{9,1},{17,25},{25,17},{2,10},{10... | collective-permute-start | bytes 442376 | tf_op jit(solution)/shard_map/ppermute | solution.py:391
  117.9 11.5 %collective-permute-start.30 = (bf16[64,1152]{1,0:T(8,128)(2,1)S(1)}, bf16[64,1152]{1,0:T(8,128)(2,1)S(1)}, u32[]{:S(2)}, u32[]{:S(2)}) collective-permute-start(bf16[64,1152]{1,0:T(8,128)(2,1)S(1)} %get-tuple-element.54), channel_id=1, source_target_pairs={{0,8},{8,0},{16,24},{24,16},{1,9},{9,1},{17,25},{25,17},{2,10},{10... | collective-permute-start | bytes 442376 | tf_op jit(solution)/shard_map/ppermute | solution.py:397
  123.7 16.8 %copy-start.1 = (bf16[3,512,512]{2,1,0:T(8,128)(2,1)S(1)}, bf16[3,512,512]{2,1,0:T(8,128)(2,1)}, u32[]{:S(2)}) copy-start(bf16[3,512,512]{2,1,0:T(8,128)(2,1)} %qkv_dw.1) | copy-start | bytes 4718596
  125.0 15.5 %collective-permute-start.12 = (bf16[768,512]{1,0:T(8,128)(2,1)S(1)}, bf16[768,512]{1,0:T(8,128)(2,1)}, u32[]{:S(2)}, u32[]{:S(2)}) collective-permute-start(bf16[768,512]{1,0:T(8,128)(2,1)S(1)} %constant_dynamic-slice_fusion.1), channel_id=1, source_target_pairs={{0,1},{1,0},{2,3},{3,2},{4,5},{5,4},{6,7},{7,6},{8,9},{9,8},{10,11... | collective-permute-start | bytes 2359304 | tf_op jit(solution)/shard_map/ppermute | solution.py:385
  125.0 14.0 %collective-permute-start.31 = (bf16[64,1152]{1,0:T(8,128)(2,1)S(1)}, bf16[64,1152]{1,0:T(8,128)(2,1)S(1)}, u32[]{:S(2)}, u32[]{:S(2)}) collective-permute-start(bf16[64,1152]{1,0:T(8,128)(2,1)S(1)} %get-tuple-element.54), channel_id=1, source_target_pairs={{0,16},{8,24},{16,0},{24,8},{1,17},{9,25},{17,1},{25,9},{2,18},{10... | collective-permute-start | bytes 442376 | tf_op jit(solution)/shard_map/ppermute | solution.py:397
  128.0 11.1 %collective-permute-start.32 = (bf16[64,1152]{1,0:T(8,128)(2,1)S(1)}, bf16[64,1152]{1,0:T(8,128)(2,1)S(1)}, u32[]{:S(2)}, u32[]{:S(2)}) collective-permute-start(bf16[64,1152]{1,0:T(8,128)(2,1)S(1)} %get-tuple-element.54), channel_id=1, source_target_pairs={{0,24},{8,16},{16,8},{24,0},{1,25},{9,17},{17,9},{25,1},{2,26},{10... | collective-permute-start | bytes 442376 | tf_op jit(solution)/shard_map/ppermute | solution.py:397
  139.1 14.3 %collective-permute-start.33 = (bf16[256,1152]{1,0:T(8,128)(2,1)S(1)}, bf16[256,1152]{1,0:T(8,128)(2,1)}, u32[]{:S(2)}, u32[]{:S(2)}) collective-permute-start(bf16[256,1152]{1,0:T(8,128)(2,1)S(1)} %constant_dynamic-update-slice_fusion.6), channel_id=1, source_target_pairs={{0,4},{1,3},{2,6},{3,1},{4,0},{5,7},{6,2},{7,5},{8,12},{9,11},{10,... | collective-permute-start | bytes 1769480 | tf_op jit(solution)/shard_map/ppermute | solution.py:400
  142.4 14.7 %collective-permute-start.13 = (bf16[384,512]{1,0:T(8,128)(2,1)}, bf16[384,512]{1,0:T(8,128)(2,1)}, u32[]{:S(2)}, u32[]{:S(2)}) collective-permute-start(bf16[384,512]{1,0:T(8,128)(2,1)} %add_convert_fusion.2), channel_id=1, source_target_pairs={{0,2},{1,5},{2,0},{3,7},{4,6},{5,1},{6,4},{7,3},{8,10},{9,13},{10,... | collective-permute-start | bytes 1179656 | tf_op jit(solution)/shard_map/ppermute | solution.py:385
  155.7 26.6 %collective-permute-start.34 = (bf16[512,1152]{1,0:T(8,128)(2,1)}, bf16[512,1152]{1,0:T(8,128)(2,1)}, u32[]{:S(2)}, u32[]{:S(2)}) collective-permute-start(bf16[512,1152]{1,0:T(8,128)(2,1)} %pad_maximum_fusion.1), channel_id=1, source_target_pairs={{0,2},{1,5},{2,0},{3,7},{4,6},{5,1},{6,4},{7,3},{8,10},{9,13},{10,... | collective-permute-start | bytes 3538952 | tf_op jit(solution)/shard_map/ppermute | solution.py:400
  158.3 7.8 %collective-permute-start.14 = (bf16[192,512]{1,0:T(8,128)(2,1)S(1)}, bf16[192,512]{1,0:T(8,128)(2,1)S(1)}, u32[]{:S(2)}, u32[]{:S(2)}) collective-permute-start(bf16[192,512]{1,0:T(8,128)(2,1)S(1)} %add_convert_fusion.3), channel_id=1, source_target_pairs={{0,4},{1,3},{2,6},{3,1},{4,0},{5,7},{6,2},{7,5},{8,12},{9,11},{10,... | collective-permute-start | bytes 589832 | tf_op jit(solution)/shard_map/ppermute | solution.py:385
  167.2 6.1 %collective-permute-start.17 = (bf16[48,512]{1,0:T(8,128)(2,1)S(1)}, bf16[48,512]{1,0:T(8,128)(2,1)S(1)}, u32[]{:S(2)}, u32[]{:S(2)}) collective-permute-start(bf16[48,512]{1,0:T(8,128)(2,1)S(1)} %get-tuple-element.61), channel_id=1, source_target_pairs={{0,24},{8,16},{16,8},{24,0},{1,25},{9,17},{17,9},{25,1},{2,26},{10... | collective-permute-start | bytes 147464 | tf_op jit(solution)/shard_map/ppermute | solution.py:391
  168.7 8.1 %collective-permute-start.16 = (bf16[48,512]{1,0:T(8,128)(2,1)S(1)}, bf16[48,512]{1,0:T(8,128)(2,1)S(1)}, u32[]{:S(2)}, u32[]{:S(2)}) collective-permute-start(bf16[48,512]{1,0:T(8,128)(2,1)S(1)} %get-tuple-element.62), channel_id=1, source_target_pairs={{0,16},{8,24},{16,0},{24,8},{1,17},{9,25},{17,1},{25,9},{2,18},{10... | collective-permute-start | bytes 147464 | tf_op jit(solution)/shard_map/ppermute | solution.py:391
  171.9 4.9 %collective-permute-start.15 = (bf16[48,512]{1,0:T(8,128)(2,1)S(1)}, bf16[48,512]{1,0:T(8,128)(2,1)S(1)}, u32[]{:S(2)}, u32[]{:S(2)}) collective-permute-start(bf16[48,512]{1,0:T(8,128)(2,1)S(1)} %get-tuple-element.60), channel_id=1, source_target_pairs={{0,8},{8,0},{16,24},{24,16},{1,9},{9,1},{17,25},{25,17},{2,10},{10... | collective-permute-start | bytes 147464 | tf_op jit(solution)/shard_map/ppermute | solution.py:391
  177.8 4.5 %collective-permute-start.18 = (bf16[48,512]{1,0:T(8,128)(2,1)S(1)}, bf16[48,512]{1,0:T(8,128)(2,1)S(1)}, u32[]{:S(2)}, u32[]{:S(2)}) collective-permute-start(bf16[48,512]{1,0:T(8,128)(2,1)S(1)} %get-tuple-element.56), channel_id=1, source_target_pairs={{0,8},{8,0},{16,24},{24,16},{1,9},{9,1},{17,25},{25,17},{2,10},{10... | collective-permute-start | bytes 147464 | tf_op jit(solution)/shard_map/ppermute | solution.py:397
  177.9 6.4 %collective-permute-start.19 = (bf16[48,512]{1,0:T(8,128)(2,1)S(1)}, bf16[48,512]{1,0:T(8,128)(2,1)S(1)}, u32[]{:S(2)}, u32[]{:S(2)}) collective-permute-start(bf16[48,512]{1,0:T(8,128)(2,1)S(1)} %get-tuple-element.56), channel_id=1, source_target_pairs={{0,16},{8,24},{16,0},{24,8},{1,17},{9,25},{17,1},{25,9},{2,18},{10... | collective-permute-start | bytes 147464 | tf_op jit(solution)/shard_map/ppermute | solution.py:397
  180.1 5.9 %collective-permute-start.20 = (bf16[48,512]{1,0:T(8,128)(2,1)S(1)}, bf16[48,512]{1,0:T(8,128)(2,1)S(1)}, u32[]{:S(2)}, u32[]{:S(2)}) collective-permute-start(bf16[48,512]{1,0:T(8,128)(2,1)S(1)} %get-tuple-element.56), channel_id=1, source_target_pairs={{0,24},{8,16},{16,8},{24,0},{1,25},{9,17},{17,9},{25,1},{2,26},{10... | collective-permute-start | bytes 147464 | tf_op jit(solution)/shard_map/ppermute | solution.py:397
  184.1 15.6 %copy-start = (bf16[1024,1152]{1,0:T(8,128)(2,1)}, bf16[1024,1152]{1,0:T(8,128)(2,1)S(1)}, u32[]{:S(2)}) copy-start(bf16[1024,1152]{1,0:T(8,128)(2,1)S(1)} %pad_maximum_fusion.own_ref) | copy-start | bytes 7077892
  184.2 41.6 %collective-permute-start.35 = (bf16[1024,1152]{1,0:T(8,128)(2,1)S(1)}, bf16[1024,1152]{1,0:T(8,128)(2,1)}, u32[]{:S(2)}, u32[]{:S(2)}) collective-permute-start(bf16[1024,1152]{1,0:T(8,128)(2,1)S(1)} %pad_maximum_fusion.own_ref), channel_id=1, source_target_pairs={{0,1},{1,0},{2,3},{3,2},{4,5},{5,4},{6,7},{7,6},{8,9},{9,8},{10,11... | collective-permute-start | bytes 7077896 | tf_op jit(solution)/shard_map/ppermute | solution.py:400
  186.0 5.7 %collective-permute-start.21 = (bf16[192,512]{1,0:T(8,128)(2,1)S(1)}, bf16[192,512]{1,0:T(8,128)(2,1)S(1)}, u32[]{:S(2)}, u32[]{:S(2)}) collective-permute-start(bf16[192,512]{1,0:T(8,128)(2,1)S(1)} %constant_dynamic-update-slice_fusion), channel_id=1, source_target_pairs={{0,4},{1,3},{2,6},{3,1},{4,0},{5,7},{6,2},{7,5},{8,12},{9,11},{10,... | collective-permute-start | bytes 589832 | tf_op jit(solution)/shard_map/ppermute | solution.py:400
  191.7 7.8 %collective-permute-start.22 = (bf16[384,512]{1,0:T(8,128)(2,1)S(1)}, bf16[384,512]{1,0:T(8,128)(2,1)S(1)}, u32[]{:S(2)}, u32[]{:S(2)}) collective-permute-start(bf16[384,512]{1,0:T(8,128)(2,1)S(1)} %pad_maximum_fusion.3), channel_id=1, source_target_pairs={{0,2},{1,5},{2,0},{3,7},{4,6},{5,1},{6,4},{7,3},{8,10},{9,13},{10,... | collective-permute-start | bytes 1179656 | tf_op jit(solution)/shard_map/ppermute | solution.py:400
  199.8 7.1 %copy-start.2 = (bf16[768,512]{1,0:T(8,128)(2,1)}, bf16[768,512]{1,0:T(8,128)(2,1)S(1)}, u32[]{:S(2)}) copy-start(bf16[768,512]{1,0:T(8,128)(2,1)S(1)} %pad_maximum_fusion.2.own_ref) | copy-start | bytes 2359300
  199.8 19.0 %collective-permute-start.23 = (bf16[768,512]{1,0:T(8,128)(2,1)S(1)}, bf16[768,512]{1,0:T(8,128)(2,1)}, u32[]{:S(2)}, u32[]{:S(2)}) collective-permute-start(bf16[768,512]{1,0:T(8,128)(2,1)S(1)} %pad_maximum_fusion.2.own_ref), channel_id=1, source_target_pairs={{0,1},{1,0},{2,3},{3,2},{4,5},{5,4},{6,7},{7,6},{8,9},{9,8},{10,11... | collective-permute-start | bytes 2359304 | tf_op jit(solution)/shard_map/ppermute | solution.py:400
  199.9 9.9 %copy-start.8 = (f32[512]{0:T(512)S(1)}, f32[512]{0:T(512)}, u32[]{:S(2)}) copy-start(f32[512]{0:T(512)} %param.12) | copy-start | bytes 6148
  207.0 9.9 %collective-permute-start.9 = (bf16[192,512]{1,0:T(8,128)(2,1)}, bf16[192,512]{1,0:T(8,128)(2,1)S(1)}, u32[]{:S(2)}, u32[]{:S(2)}) collective-permute-start(bf16[192,512]{1,0:T(8,128)(2,1)} %get-tuple-element.43), channel_id=1, source_target_pairs={{0,7},{1,0},{2,1},{3,2},{4,3},{5,4},{6,5},{7,6},{8,15},{9,8},{10,9... | collective-permute-start | bytes 589832 | tf_op jit(solution)/shard_map/ppermute | solution.py:331
  207.5 9.3 %collective-permute-start.10 = (bf16[144,512]{1,0:T(8,128)(2,1)}, bf16[144,512]{1,0:T(8,128)(2,1)S(1)}, u32[]{:S(2)}, u32[]{:S(2)}) collective-permute-start(bf16[144,512]{1,0:T(8,128)(2,1)} %get-tuple-element.44), channel_id=1, source_target_pairs={{0,24},{1,25},{2,26},{3,27},{4,28},{5,29},{6,30},{7,31},{8,0},{9,1... | collective-permute-start | bytes 442376 | tf_op jit(solution)/shard_map/ppermute | solution.py:331
  210.4 6.5 %collective-permute-start.11 = (bf16[24,512]{1,0:T(8,128)(2,1)}, bf16[24,512]{1,0:T(8,128)(2,1)S(1)}, u32[]{:S(2)}, u32[]{:S(2)}) collective-permute-start(bf16[24,512]{1,0:T(8,128)(2,1)} %get-tuple-element.45), channel_id=1, source_target_pairs={{0,31},{1,24},{2,25},{3,26},{4,27},{5,28},{6,29},{7,30},{8,7},{9,0... | collective-permute-start | bytes 73736 | tf_op jit(solution)/shard_map/ppermute | solution.py:331
  215.1 1.8 copy-start.3

commit v2 on v1

--- a/solution.py
+++ b/solution.py
@@ -56,8 +56,14 @@
     return even.astype(BF), (1.0 - even).astype(BF)
 
 
-def load_windows(own_ref, west_ref, south_ref, corner_ref, buf_ref, win_ref, stride):
-    step = pl.program_id(0)
+def load_rows(deep, own_ref, west_ref, south_ref, corner_ref, buf_ref, win_ref, stride):
+    tall, wide = win_ref.shape[0] // deep, buf_ref.shape[0] // deep
+    for k in range(deep):
+        load_windows(pl.program_id(0) * deep + k, k == 0, own_ref, west_ref, south_ref, corner_ref,
+                     buf_ref.at[pl.ds(k * wide, wide)], win_ref.at[pl.ds(k * tall, tall)], stride)
+
+
+def load_windows(step, first, own_ref, west_ref, south_ref, corner_ref, buf_ref, win_ref, stride):
     cols = south_ref.shape[0] // (WLAT // 2)
     wide = EDGE + cols
     half = WLAT // 2
@@ -66,20 +72,23 @@
         buf_ref[pl.ds(wide * r, EDGE), :] = edge.astype(F32)
         buf_ref[pl.ds(wide * r + EDGE, cols), :] = line.astype(F32)
 
-    @pl.when(step == 0)
-    def _():
-        for r in range(half):
-            put(r, corner_ref[r], south_ref[pl.ds(cols * r, cols), :])
-
-    @pl.when(step > 0)
-    def _():
-        for r in range(half):
-            row = WLAT * step - half + r
-            put(r, west_ref[row], own_ref[pl.ds(pl.multiple_of(cols * row, 16), cols), :])
-
-    for r in range(half, WLAT):
+    def later(r):
         row = WLAT * step - half + r
         put(r, west_ref[row], own_ref[pl.ds(pl.multiple_of(cols * row, 16), cols), :])
+
+    if first:
+        @pl.when(step == 0)
+        def _():
+            for r in range(half):
+                put(r, corner_ref[r], south_ref[pl.ds(cols * r, cols), :])
+
+        @pl.when(step > 0)
+        def _():
+            for r in range(half):
+                later(r)
+
+    for r in range(0 if not first else half, WLAT):
+        later(r)
     for b in range(cols // WLON):
         for r in range(WLAT):
             piece = buf_ref[pl.ds(wide * r + EDGE - WLON // 2 + WLON * b, WLON), :]
@@ -88,24 +97,34 @@
         win_ref[pl.ds(stride * (b + 1) - pad, pad), :] = jnp.zeros((pad, win_ref.shape[1]), F32)
 
 
-def unload_windows(win_ref, grid_ref, stride):
-    cols = grid_ref.shape[0] // WLAT
-    for b in range(cols // WLON):
-        for r in range(WLAT):
-            piece = win_ref[pl.ds(stride * b + WLON * r, WLON), :]
-            grid_ref[pl.ds(cols * r + WLON * b, WLON), :] = piece
-    return grid_ref[...]
+def unload_rows(deep, win_ref, grid_ref, stride, out_ref, lon_ref, lat_ref, corner_ref):
+    tall, block = win_ref.shape[0] // deep, grid_ref.shape[0] // deep
+    cols = block // WLAT
+    for k in range(deep):
+        for b in range(cols // WLON):
+            for r in range(WLAT):
+                piece = win_ref[pl.ds(k * tall + stride * b + WLON * r, WLON), :]
+                grid_ref[pl.ds(k * block + cols * r + WLON * b, WLON), :] = piece
+    out_ref[...] = grid_ref[...].astype(out_ref.dtype)
+    edge = [grid_ref[pl.ds(r * cols, EDGE), :] for r in range(deep * WLAT)]
+    edge = jnp.concatenate(edge, axis=0).astype(BF)
+    lon_ref[...] = edge
+
+    @pl.when(pl.program_id(0) == 0)
+    def _():
+        lat_ref[...] = grid_ref[pl.ds(0, lat_ref.shape[0]), :].astype(BF)
+        corner_ref[...] = edge[: corner_ref.shape[0]]
 
 
 def stack_heads(value, masks):
     return jnp.concatenate([value * masks[0], value * masks[1]], axis=0)
 
 
-def forward_kernel(stride, count_b, own_ref, west_ref, south_ref, corner_ref, allow_ref, gain_ref,
+def forward_kernel(deep, stride, count_b, own_ref, west_ref, south_ref, corner_ref, allow_ref, gain_ref,
                    w_ref, att_ref, qkv_ref, normed_ref, tok_ref, prob_ref, lon_ref, lat_ref,
                    corner_out_ref, buf_ref, win_ref, grid_ref):
     features = own_ref.shape[1]
-    load_windows(own_ref, west_ref, south_ref, corner_ref, buf_ref, win_ref, stride)
+    load_rows(deep, own_ref, west_ref, south_ref, corner_ref, buf_ref, win_ref, stride)
     x = win_ref[...]
     tok_ref[...] = x.astype(BF)
     average = jnp.mean(x, axis=-1, keepdims=True)
@@ -115,9 +134,9 @@
     normed_ref[...] = normed
     for t in range(3):
         qkv_ref[t] = dot_nn(normed, w_ref[:, features * t : features * (t + 1)]).astype(BF)
-    allow = allow_ref[0] > 0.5
     masks = lane_masks()
-    for b in range(count_b):
+    for b in range(deep * count_b):
+        allow = allow_ref[b // count_b] > 0.5
         rows = slice(b * stride, (b + 1) * stride)
         for pair in range(features // 128):
             lanes = pl.ds(128 * pair, 128)
@@ -131,23 +150,11 @@
             p2 = jnp.concatenate(probs, axis=0)
             prob_ref[pair, pl.ds(2 * stride * b, 2 * stride), :] = p2
             win_ref[rows, lanes] = dot_tn(p2, stack_heads(qkv_ref[2, rows, lanes], masks))
-    write_edges(unload_windows(win_ref, grid_ref, stride), att_ref, lon_ref, lat_ref, corner_out_ref)
-
-
-def write_edges(values, out_ref, lon_ref, lat_ref, corner_ref):
-    cols = values.shape[0] // WLAT
-    out_ref[...] = values.astype(out_ref.dtype)
-    edge = jnp.concatenate([values[r * cols : r * cols + EDGE] for r in range(WLAT)], axis=0).astype(BF)
-    lon_ref[...] = edge
-
-    @pl.when(pl.program_id(0) == 0)
-    def _():
-        lat_ref[...] = values[: lat_ref.shape[0]].astype(BF)
-        corner_ref[...] = edge[: corner_ref.shape[0]]
-
-
-def assemble_kernel(stride, own_ref, west_ref, south_ref, corner_ref, out_ref, buf_ref, win_ref):
-    load_windows(own_ref, west_ref, south_ref, corner_ref, buf_ref, win_ref, stride)
+    unload_rows(deep, win_ref, grid_ref, stride, att_ref, lon_ref, lat_ref, corner_out_ref)
+
+
+def assemble_kernel(deep, stride, own_ref, west_ref, south_ref, corner_ref, out_ref, buf_ref, win_ref):
+    load_rows(deep, own_ref, west_ref, south_ref, corner_ref, buf_ref, win_ref, stride)
     out_ref[...] = win_ref[...].astype(BF)
 
 
@@ -198,7 +205,7 @@
     out_ref[...] = dot_nt(gm_ref[...], w_merge_ref[...]).astype(BF)
 
 
-def merge_grad_kernel(merged_in_ref, gm_ref, att_ref, gmix_ref, out_ref):
+def merge_grad_kernel(_, merged_in_ref, gm_ref, att_ref, gmix_ref, out_ref):
     width = gm_ref.shape[1]
     out_ref[:, :width] = dot_tn(merged_in_ref[...], gm_ref[...]).astype(BF)
     out_ref[:, width:] = dot_tn(gmix_ref[...], att_ref[...]).T.astype(BF)
@@ -209,50 +216,25 @@
     return jnp.sum(total.T, axis=0, keepdims=True)
 
 
-def merge_last_kernel(half, keep_ref, own_ref, got_ref, w_ref, gain_ref, out_ref, out_o_ref, dgain_ref):
+def merge_last_kernel(_, value_ref, w_ref, gain_ref, *refs):
+    out_ref, out_o_ref, dgain_ref = refs[-3:]
     width = w_ref.shape[1]
-    here = pl.program_id(0) // half == keep_ref[0]
-
-    def finish(ref):
-        value = ref[:, :width].astype(F32)
-        out_ref[...] = value
-        out_o_ref[...] = ref[:, width:].astype(F32)
-        dgain_ref[...] = row_sums(value * w_ref[...].astype(F32)) / gain_ref[...]
-
-    @pl.when(here)
-    def _():
-        finish(own_ref)
-
-    @pl.when(jnp.logical_not(here))
-    def _():
-        finish(got_ref)
-
-
-def qkv_last_kernel(half, keep_ref, own_ref, got_ref, w_ref, gain_ref, out_ref, dgain_ref):
-    step = pl.program_id(0)
-    here = step // half == keep_ref[0]
-    side = pl.ds(step % 2, 1)
-
-    def finish(ref):
-        value = ref[...].astype(F32)
-        out_ref[...] = value
-        part = row_sums(value * w_ref[...].astype(F32))
-
-        @pl.when(step < 2)
-        def _():
-            dgain_ref[side, :] = part / gain_ref[side, :]
-
-        @pl.when(step >= 2)
-        def _():
-            dgain_ref[side, :] += part / gain_ref[side, :]
-
-    @pl.when(here)
-    def _():
-        finish(own_ref)
-
-    @pl.when(jnp.logical_not(here))
-    def _():
-        finish(got_ref)
+    value = value_ref[:, :width].astype(F32)
+    out_ref[...] = value
+    out_o_ref[...] = value_ref[:, width:].astype(F32)
+    dgain_ref[...] = row_sums(value * w_ref[...].astype(F32)) / gain_ref[...]
+
+
+def qkv_last_kernel(_, value_ref, w_ref, gain_ref, *refs):
+    out_ref, dgain_ref = refs[-2:]
+    height, features = value_ref.shape[0] // 3, value_ref.shape[1]
+    total = 0.0
+    for t in range(3):
+        lanes = slice(features * t, features * (t + 1))
+        value = value_ref[height * t : height * (t + 1), :].astype(F32)
+        out_ref[:, lanes] = value
+        total = total + value * w_ref[:, lanes].astype(F32)
+    dgain_ref[...] = row_sums(total) / gain_ref[...]
 
 
 def backward_kernel(stride, count_b, ga_ref, qkv_ref, prob_ref, prev_ref, gqkv_ref):
@@ -286,12 +268,13 @@
             gqkv_ref[1, rows, lanes] = jnp.where(low, dk[:stride], dk[stride:]).astype(BF)
 
 
-def qkv_grad_kernel(normed_ref, gqkv_ref, out_ref):
+def qkv_grad_kernel(_, normed_ref, gqkv_ref, out_ref):
+    height = normed_ref.shape[1]
     for t in range(3):
-        out_ref[t] = dot_tn(normed_ref[...], gqkv_ref[t]).astype(BF)
-
-
-def input_grad_kernel(stride, gqkv_ref, x_ref, gain_ref, w_ref, out_ref, lon_ref, lat_ref, corner_ref,
+        out_ref[height * t : height * (t + 1), :] = dot_tn(normed_ref[...], gqkv_ref[t]).astype(BF)
+
+
+def input_grad_kernel(deep, stride, gqkv_ref, x_ref, gain_ref, w_ref, out_ref, lon_ref, lat_ref, corner_ref,
                       win_ref, grid_ref):
     features = x_ref.shape[1]
     grad = sum(dot_nt(gqkv_ref[t], w_ref[:, features * t : features * (t + 1)]) for t in range(3))
@@ -303,7 +286,7 @@
     one = jnp.mean(grad, axis=-1, keepdims=True)
     two = jnp.mean(grad * hat, axis=-1, keepdims=True)
     win_ref[...] = (grad - one - hat * two) * inv
-    write_edges(unload_windows(win_ref, grid_ref, stride), out_ref, lon_ref, lat_ref, corner_ref)
+    unload_rows(deep, win_ref, grid_ref, stride, out_ref, lon_ref, lat_ref, corner_ref)
 
 
 def merged_kernel(a_ref, w_ref, out_ref):
@@ -367,19 +350,21 @@
     return jnp.concatenate([first, second], axis=0)
 
 
-def reduce_all(value):
+def reduce_all(sent, kept):
     count_lat, count_lon = lax.axis_size("lat"), lax.axis_size("lon")
     bits = count_lon.bit_length() - 1
     me, lat = lax.axis_index("lon"), lax.axis_index("lat")
     odd = lax.rem(me, 2)
-    plans = [([(i, i ^ 1) for i in range(count_lon)], odd)]
+    partner = [(i, i ^ 1) for i in range(count_lon)]
+    plans = []
     for k in range(bits - 1):
         low, high = 2 << k, 2 << (bits - 2 - k)
         pairs = [(i, i ^ (low if i % 2 == 0 else high)) for i in range(count_lon)]
         keep = jnp.where(odd == 0, lax.rem(me // low, 2), lax.rem(me // high, 2))
         plans.append((pairs, keep))
-    terms, height = [value], value.shape[0]
-    for pairs, keep in plans:
+    received = lax.ppermute(sent, "lon", partner)
+    terms, height = [kept, received], kept.shape[0]
+    for k, (pairs, keep) in enumerate(plans, 1):
         height = height // 2
         sent = part_sum(terms, 1 - keep, height)
         received = lax.ppermute(sent, "lon", pairs)
@@ -396,11 +381,11 @@
     for d in range(1, count_lat):
         received = lax.ppermute(mine, "lat", [(i, i ^ d) for i in range(count_lat)])
         value = lax.dynamic_update_slice_in_dim(value, received, (lat ^ d) * height, 0)
-    for k, (pairs, keep) in reversed(list(enumerate(plans))):
+    for k, (pairs, keep) in reversed(list(enumerate(plans, 1))):
         received = lax.ppermute(value, "lon", pairs)
-        if k:
-            value = join(value, received, keep)
-    return value, received, odd.astype(jnp.int32).reshape(1)
+        value = join(value, received, keep)
+    received = lax.ppermute(value, "lon", partner)
+    return value, received
 
 
 def on_device_body(tokens, lat_band, gain_attn, w_qkv, w_out, gain_merge, w_merge, grad_merged):
@@ -430,30 +415,31 @@
     own_tok = tokens.reshape(total, features)
     edge_shapes = [(rows * EDGE, features), (half_lat * cols, features), (half_lat * EDGE, features)]
     edge_types = [jax.ShapeDtypeStruct(shape, BF) for shape in edge_shapes]
-    edge_specs = [rows_of(WLAT * EDGE, features), whole(edge_shapes[1]), whole(edge_shapes[2])]
+    deep = 2 if count_a % 2 == 0 else 1
+    edge_specs = [rows_of(deep * WLAT * EDGE, features), whole(edge_shapes[1]), whole(edge_shapes[2])]
     halo_specs = [whole((total, features)), whole((rows, EDGE, features)), whole(edge_shapes[1]),
                   whole((half_lat, EDGE, features))]
-    win_scratch = pltpu.VMEM((padded, features), F32)
-    buf_scratch = pltpu.VMEM((wide, features), F32)
-    grid_scratch = pltpu.VMEM((block, features), F32)
+    win_scratch = pltpu.VMEM((deep * padded, features), F32)
+    buf_scratch = pltpu.VMEM((deep * wide, features), F32)
+    grid_scratch = pltpu.VMEM((deep * block, features), F32)
 
     def halo_args(parts):
         west, south, corner = parts
         return west.reshape(rows, EDGE, features), south, corner.reshape(half_lat, EDGE, features)
 
     tok_halos = exchange(edges(tokens), 1)
-    allow_spec = pl.BlockSpec((1, stride, stride), lambda i: (i, 0, 0))
+    allow_spec = pl.BlockSpec((deep, stride, stride), lambda i: (i, 0, 0))
     pairs = features // 128
     tall3 = count_a * padded
-    qkv_spec = pl.BlockSpec((3, padded, features), lambda i: (0, i, 0))
+    qkv_spec = pl.BlockSpec((3, deep * padded, features), lambda i: (0, i, 0))
     prob_rows = 2 * stride * count_b
     attended, qkv, normed, tok_win, probs, *att_edges = pl.pallas_call(
-        functools.partial(forward_kernel, stride, count_b),
-        grid=(count_a,),
+        functools.partial(forward_kernel, deep, stride, count_b),
+        grid=(count_a // deep,),
         in_specs=halo_specs + [allow_spec, whole((1, features)), whole((features, 3 * features))],
-        out_specs=[rows_of(block, features), qkv_spec, rows_of(padded, features),
-                   rows_of(padded, features),
-                   pl.BlockSpec((pairs, prob_rows, stride), lambda i: (0, i, 0))] + edge_specs,
+        out_specs=[rows_of(deep * block, features), qkv_spec, rows_of(deep * padded, features),
+                   rows_of(deep * padded, features),
+                   pl.BlockSpec((pairs, deep * prob_rows, stride), lambda i: (0, i, 0))] + edge_specs,
         out_shape=[jax.ShapeDtypeStruct((total, features), BF),
                    jax.ShapeDtypeStruct((3, tall3, features), BF),
                    jax.ShapeDtypeStruct((tall3, features), BF),
@@ -470,9 +456,9 @@
     gm = grad_merged.reshape(total // 4, width2)
     grad_in = pl.pallas_call(
         grad_in_kernel,
-        grid=(4,),
-        in_specs=[whole((total // 4, width2)), rows_of(features, width2)],
-        out_specs=pl.BlockSpec((total // 4, features), lambda i: (0, i)),
+        grid=(2,),
+        in_specs=[whole((total // 4, width2)), rows_of(2 * features, width2)],
+        out_specs=pl.BlockSpec((total // 4, 2 * features), lambda i: (0, i)),
         out_shape=jax.ShapeDtypeStruct((total // 4, 4 * features), BF),
         compiler_params=params(1),
         cost_estimate=cost(2 * total * features * width2, 2 * total * features * 4),
@@ -501,49 +487,58 @@
     att_halos = exchange(grad_edges, 1)
     pieces = 4
     rest = features // pieces
-    dw_merge = pl.pallas_call(
-        merge_grad_kernel,
-        grid=(pieces,),
-        in_specs=[pl.BlockSpec((total // 4, features), lambda i: (0, i)),
-                  whole((total // 4, width2)), whole((total, features)),
-                  pl.BlockSpec((total, rest), lambda i: (0, i))],
-        out_specs=rows_of(features, width2 + rest),
-        out_shape=jax.ShapeDtypeStruct((pieces * features, width2 + rest), BF),
-        compiler_params=params(1),
-        cost_estimate=cost(4 * total * features * features * 2, 2 * total * features * 6),
-        name="merge_dw",
-    )(merged_in, gm, own_att, grad_mixed)
-    sum_m = reduce_all(dw_merge)
+    odd = lax.rem(lax.axis_index("lon"), 2).astype(jnp.int32)
+    mine, theirs = odd.reshape(1), (1 - odd).reshape(1)
+
+    def merge_dw(side):
+        return pl.pallas_call(
+            merge_grad_kernel,
+            grid_spec=pltpu.PrefetchScalarGridSpec(
+                num_scalar_prefetch=1,
+                grid=(pieces // 2,),
+                in_specs=[pl.BlockSpec((total // 4, features), lambda i, k: (0, 2 * k[0] + i)),
+                          pl.BlockSpec((total // 4, width2), lambda i, k: (0, 0)),
+                          pl.BlockSpec((total, features), lambda i, k: (0, 0)),
+                          pl.BlockSpec((total, rest), lambda i, k: (0, 2 * k[0] + i))],
+                out_specs=pl.BlockSpec((features, width2 + rest), lambda i, k: (i, 0)),
+            ),
+            out_shape=jax.ShapeDtypeStruct((pieces // 2 * features, width2 + rest), BF),
+            compiler_params=params(1),
+            cost_estimate=cost(2 * total * features * features * 2, total * features * 6),
+            name="merge_dw",
+        )(side, merged_in, gm, own_att, grad_mixed)
+
+    m_own, m_got = reduce_all(merge_dw(theirs), merge_dw(mine))
 
     grad_win = pl.pallas_call(
-        functools.partial(assemble_kernel, stride),
-        grid=(count_a,),
+        functools.partial(assemble_kernel, count_a, stride),
+        grid=(1,),
         in_specs=halo_specs,
-        out_specs=rows_of(padded, features),
+        out_specs=rows_of(tall3, features),
         out_shape=jax.ShapeDtypeStruct((tall3, features), BF),
-        scratch_shapes=[buf_scratch, win_scratch],
+        scratch_shapes=[pltpu.VMEM((count_a * wide, features), F32), pltpu.VMEM((tall3, features), F32)],
         compiler_params=params(1),
         cost_estimate=cost(total * features * 1200, 2 * total * features * 3),
         name="assemble",
     )(grad_att, *halo_args(att_halos))
     calls = CALLS
-    wide = features // calls
+    lane_count = features // calls
     grad_qkv = None
     for j in range(calls):
-        spec = pl.BlockSpec((3, padded, wide), lambda i, j=j: (0, i, j))
+        spec = pl.BlockSpec((3, deep * padded, lane_count), lambda i, j=j: (0, i, j))
         operands = [grad_win, qkv, probs]
-        specs = [pl.BlockSpec((padded, wide), lambda i, j=j: (i, j)), spec,
-                 pl.BlockSpec((pairs // calls, prob_rows, stride), lambda i, j=j: (j, i, 0))]
+        specs = [pl.BlockSpec((deep * padded, lane_count), lambda i, j=j: (i, j)), spec,
+                 pl.BlockSpec((pairs // calls, deep * prob_rows, stride), lambda i, j=j: (j, i, 0))]
         if grad_qkv is not None:
             operands.append(grad_qkv)
             specs.append(pl.BlockSpec(memory_space=pl.ANY))
-            body = functools.partial(backward_kernel, stride, count_b)
+            body = functools.partial(backward_kernel, stride, deep * count_b)
         else:
             def body(ga_ref, qkv_ref, prob_ref, gqkv_ref):
-                backward_kernel(stride, count_b, ga_ref, qkv_ref, prob_ref, None, gqkv_ref)
+                backward_kernel(stride, deep * count_b, ga_ref, qkv_ref, prob_ref, None, gqkv_ref)
         grad_qkv = pl.pallas_call(
             body,
-            grid=(count_a,),
+            grid=(count_a // deep,),
             in_specs=specs,
             out_specs=spec,
             out_shape=jax.ShapeDtypeStruct((3, tall3, features), BF),
@@ -552,25 +547,32 @@
             cost_estimate=cost(4 * total * features * 3 * features // calls,
                                2 * total * features * 8 // calls),
         )(*operands)
-    dw_q = pl.pallas_call(
-        qkv_grad_kernel,
-        grid=(2,),
-        in_specs=[pl.BlockSpec((tall3, features // 2), lambda i: (0, i)),
-                  whole((3, tall3, features))],
-        out_specs=pl.BlockSpec((3, features // 2, features), lambda i: (0, i, 0)),
-        out_shape=jax.ShapeDtypeStruct((3, features, features), BF),
-        compiler_params=params(1),
-        cost_estimate=cost(2 * total * features * 3 * features, 2 * total * features * 5),
-        name="qkv_dw",
-    )(normed, grad_qkv)
-    sum_q = reduce_all(dw_q.reshape(3 * features, features))
+    tile = features // 2
+
+    def qkv_dw(side):
+        return pl.pallas_call(
+            qkv_grad_kernel,
+            grid_spec=pltpu.PrefetchScalarGridSpec(
+                num_scalar_prefetch=1,
+                grid=(1,),
+                in_specs=[pl.BlockSpec((tall3, tile), lambda i, k: (0, k[0])),
+                          pl.BlockSpec((3, tall3, features), lambda i, k: (0, 0, 0))],
+                out_specs=pl.BlockSpec((3 * tile, features), lambda i, k: (0, 0)),
+            ),
+            out_shape=jax.ShapeDtypeStruct((3 * tile, features), BF),
+            compiler_params=params(1),
+            cost_estimate=cost(total * features * 3 * features, total * features * 5),
+            name="qkv_dw",
+        )(side, normed, grad_qkv)
+
+    q_own, q_got = reduce_all(qkv_dw(theirs), qkv_dw(mine))
 
     grad_inputs, *in_edges = pl.pallas_call(
-        functools.partial(input_grad_kernel, stride),
-        grid=(count_a,),
-        in_specs=[qkv_spec, rows_of(padded, features), whole((1, features)),
+        functools.partial(input_grad_kernel, deep, stride),
+        grid=(count_a // deep,),
+        in_specs=[qkv_spec, rows_of(deep * padded, features), whole((1, features)),
                   whole((features, 3 * features))],
-        out_specs=[rows_of(block, features)] + edge_specs,
+        out_specs=[rows_of(deep * block, features)] + edge_specs,
         out_shape=[jax.ShapeDtypeStruct((total, features), BF)] + edge_types,
         scratch_shapes=[win_scratch, grid_scratch],
         compiler_params=params(1),
@@ -584,64 +586,62 @@
     merged = pl.pallas_call(
         merged_kernel,
         grid=(2,),
-        in_specs=[rows_of(total // 8, 4 * features), whole((4 * features, width2))],
-        out_specs=rows_of(total // 8, width2),
+        in_specs=[whole((total // 4, 4 * features)),
+                  pl.BlockSpec((4 * features, width2 // 2), lambda i: (0, i))],
+        out_specs=pl.BlockSpec((total // 4, width2 // 2), lambda i: (0, i)),
         out_shape=jax.ShapeDtypeStruct((total // 4, width2), BF),
         compiler_params=params(1),
         cost_estimate=cost(2 * total * features * width2, 2 * total * features * 4),
         name="merged",
     )(merged_in, w_merge).reshape(grad_merged.shape)
 
-    def halves(height, width, half):
-        def spot(mine):
-            def index(i, keep):
-                side, place = i // half, i % half
-                other = jnp.where(side < (keep[0] if mine else 1 - keep[0]), 0, half - 1)
-                return jnp.where((side == keep[0]) == mine, place, other), 0
-
-            return index
-
-        return [pl.BlockSpec((height, width), spot(True)), pl.BlockSpec((height, width), spot(False))]
-
-    m_own, m_got, keep = sum_m
-    grad_w_merge, grad_w_out, grad_gain_merge = pl.pallas_call(
-        functools.partial(merge_last_kernel, pieces // 2),
-        grid_spec=pltpu.PrefetchScalarGridSpec(
-            num_scalar_prefetch=1,
-            grid=(pieces,),
-            in_specs=halves(features, width2 + rest, pieces // 2) + [
-                pl.BlockSpec((features, width2), lambda i, k: (i, 0)),
-                pl.BlockSpec((1, features), lambda i, k: (0, i))],
-            out_specs=[pl.BlockSpec((features, width2), lambda i, k: (i, 0)),
-                       pl.BlockSpec((features, rest), lambda i, k: (0, i)),
-                       pl.BlockSpec((1, features), lambda i, k: (0, i))],
-        ),
-        out_shape=[jax.ShapeDtypeStruct((pieces * features, width2), F32),
-                   jax.ShapeDtypeStruct((features, features), F32),
-                   jax.ShapeDtypeStruct((1, pieces * features), F32)],
-        compiler_params=params(1),
-        cost_estimate=cost(total * features * 2000, 2 * total * features * 6),
-        name="m_last",
-    )(keep, m_own, m_got, w_merge, gain_m)
-    q_own, q_got, keep = sum_q
-    tile = features // 2
-    grad_w_qkv, grad_gain_attn = pl.pallas_call(
-        functools.partial(qkv_last_kernel, 3),
-        grid_spec=pltpu.PrefetchScalarGridSpec(
-            num_scalar_prefetch=1,
-            grid=(6,),
-            in_specs=halves(tile, features, 3) + [
-                pl.BlockSpec((tile, features), lambda i, k: (i % 2, i // 2)),
-                pl.BlockSpec((2, tile), lambda i, k: (0, 0))],
-            out_specs=[pl.BlockSpec((tile, features), lambda i, k: (i % 2, i // 2)),
-                       pl.BlockSpec((2, tile), lambda i, k: (0, 0))],
-        ),
-        out_shape=[jax.ShapeDtypeStruct((features, 3 * features), F32),
-                   jax.ShapeDtypeStruct((2, tile), F32)],
-        compiler_params=params(1),
-        cost_estimate=cost(total * features * 1000, 2 * total * features * 3),
-        name="q_last",
-    )(keep, q_own, q_got, w_qkv, gain_attn.reshape(2, tile))
+    def finish_merge(side, value, earlier=()):
+        return pl.pallas_call(
+            merge_last_kernel,
+            grid_spec=pltpu.PrefetchScalarGridSpec(
+                num_scalar_prefetch=1,
+                grid=(pieces // 2,),
+                in_specs=[pl.BlockSpec((features, width2 + rest), lambda i, k: (i, 0)),
+                          pl.BlockSpec((features, width2), lambda i, k: (2 * k[0] + i, 0)),
+                          pl.BlockSpec((1, features), lambda i, k: (0, 2 * k[0] + i))]
+                + [pl.BlockSpec(memory_space=pl.ANY)] * len(earlier),
+                out_specs=[pl.BlockSpec((features, width2), lambda i, k: (2 * k[0] + i, 0)),
+                           pl.BlockSpec((features, rest), lambda i, k: (0, 2 * k[0] + i)),
+                           pl.BlockSpec((1, features), lambda i, k: (0, 2 * k[0] + i))],
+            ),
+            out_shape=[jax.ShapeDtypeStruct((pieces * features, width2), F32),
+                       jax.ShapeDtypeStruct((features, features), F32),
+                       jax.ShapeDtypeStruct((1, pieces * features), F32)],
+            input_output_aliases={4 + n: n for n in range(len(earlier))},
+            compiler_params=params(1),
+            cost_estimate=cost(total * features * 1000, total * features * 6),
+            name="m_last",
+        )(side, value, w_merge, gain_m, *earlier)
+
+    def finish_qkv(side, value, earlier=()):
+        return pl.pallas_call(
+            qkv_last_kernel,
+            grid_spec=pltpu.PrefetchScalarGridSpec(
+                num_scalar_prefetch=1,
+                grid=(1,),
+                in_specs=[pl.BlockSpec((3 * tile, features), lambda i, k: (0, 0)),
+                          pl.BlockSpec((tile, 3 * features), lambda i, k: (k[0], 0)),
+                          pl.BlockSpec((1, tile), lambda i, k: (0, k[0]))]
+                + [pl.BlockSpec(memory_space=pl.ANY)] * len(earlier),
+                out_specs=[pl.BlockSpec((tile, 3 * features), lambda i, k: (k[0], 0)),
+                           pl.BlockSpec((1, tile), lambda i, k: (0, k[0]))],
+            ),
+            out_shape=[jax.ShapeDtypeStruct((features, 3 * features), F32),
+                       jax.ShapeDtypeStruct((1, features), F32)],
+            input_output_aliases={4 + n: n for n in range(len(earlier))},
+            compiler_params=params(1),
+            cost_estimate=cost(total * features * 500, total * features * 3),
+            name="q_last",
+        )(side, value, w_qkv, gain_a, *earlier)
+
+    grad_w_merge, grad_w_out, grad_gain_merge = finish_merge(
+        theirs, m_got, finish_merge(mine, m_own))
+    grad_w_qkv, grad_gain_attn = finish_qkv(theirs, q_got, finish_qkv(mine, q_own))
     grad_gain_merge = grad_gain_merge.reshape(-1)
     grad_gain_attn = grad_gain_attn.reshape(-1)
     return (merged, grad_tokens, grad_gain_attn, grad_w_qkv, grad_w_out, grad_gain_merge,

time: 235 us -> 228 us (0.970)
  local copies, waits for them, and re-layouts: 12.5 us -> 8.54 us
    ppermute x6 -> x4, waiting for transfers between devices: 21.6 us -> 14.9 us  [reduce_all(): received = lax.ppermute(value, 'lon', pairs)]
    ppermute x6, waiting for transfers between devices: 5.68 us -> 10.5 us  [reduce_all(): received = lax.ppermute(sent, 'lat', [(i, i ^ d) for i in range(count_lat)])]
    dynamic_slice x2 -> x0, local copies, waits for them, and re-layouts: 3.15 us -> none  [part_sum(): lax.dynamic_slice_in_dim(t, index * height, height, 0).astype(F32)]
    ppermute x6 -> x4, starting transfers between devices: 5.12 us -> 3.05 us  [reduce_all(): received = lax.ppermute(value, 'lon', pairs)]
    pallas_call x13 -> x17, Pallas kernels: 76.3 us -> 74.3 us  [the longest x4 13.1 us: on_device_body(): pl.pallas_call(body, grid=(count_a // deep,), in_specs=specs, out_specs=s...]
    ppermute x6 -> x4, waiting for transfers between devices: 27 us -> 25.5 us  [reduce_all(): received = lax.ppermute(sent, 'lon', pairs)]
  transfers between devices with their start and end apart: 36 -> 36, of which waited for: 14 -> 18; matrix products, arithmetic and copies ran while one was open for 9% -> 8% of each run, Pallas kernels for 21% -> 24%
where the time goes in v2:
time: 228 us; the launch traced here: 227 us
  Pallas kernels  81.1 us (36%)
  waiting for transfers between devices  75 us (33%)
  starting transfers between devices  39.4 us (17%)
  other arithmetic  22.1 us (10%)
  local copies, waits for them, and re-layouts  8.54 us (4%)
    ppermute x4, waiting for transfers between devices, reduce_all(): received = lax.ppermute(sent, 'lon', pairs)  25.5 us
    ppermute x4, waiting for transfers between devices, reduce_all(): received = lax.ppermute(value, 'lon', pairs)  14.9 us
    ppermute x12, starting transfers between devices, send(): return lax.ppermute(value, ('lat', 'lon'), pairs)  14.3 us
    ppermute x6, waiting for transfers between devices, reduce_all(): received = lax.ppermute(mine, 'lat', [(i, i ^ d) for i in range(count_lat)])  13.3 us
    pallas_call x4, Pallas kernels, on_device_body(): pl.pallas_call(body, grid=(count_a // deep,), in_specs=specs, out_specs=s...  13.1 us
    convert_element_type x6, other arithmetic, part_sum(): return sum(parts[1:], parts[0]).astype(BF)  11.8 us
    pallas_call x1, Pallas kernels, on_device_body(): pl.pallas_call(functools.partial(forward_kernel, deep, stride, count_b),...  11.4 us
    ppermute x12, waiting for transfers between devices, send(): return lax.ppermute(value, ('lat', 'lon'), pairs)  10.5 us
  transfers between devices with their start and end apart: 36, of which 18 were waited for; matrix products, arithmetic and copies ran while one was open for 8% of the time, Pallas kernels for 24%

profile of v2, /device:TPU:0, one launch (start us, length us, event | category | flops | bytes accessed | tf_op | source)
XLA Modules:
  0.0 227.0 jit_solution(11919950038046365118)
XLA Ops:
  1.4 2.5 %collective-permute-start.2 = (bf16[24,512]{1,0:T(8,128)(2,1)S(1)}, bf16[24,512]{1,0:T(8,128)(2,1)S(1)}, u32[]{:S(2)}, u32[]{:S(2)}) collective-permute-start(bf16[24,512]{1,0:T(8,128)(2,1)S(1)} %slice_bitcast_fusion.1), channel_id=1, source_target_pairs={{0,9},{1,10},{2,11},{3,12},{4,13},{5,14},{6,15},{7,8},{8,17},{9,18... | collective-permute-start | bytes 73736 | tf_op jit(solution)/shard_map/ppermute | solution.py:314
  4.8 1.6 collective-permute-start.1
  6.4 0.9 slice_bitcast_fusion
  7.4 1.4 collective-permute-start
  11.3 1.4 collective-permute-done.1.south_ref
  14.1 11.4 %attn_fwd.1 = (bf16[1152,512]{1,0:T(8,128)(2,1)}, bf16[3,1280,512]{2,1,0:T(8,128)(2,1)}, bf16[1280,512]{1,0:T(8,128)(2,1)}, bf16[1280,512]{1,0:T(8,128)(2,1)}, b...) custom-call(bf16[1152,512]{1,0:T(8,128)(2,1)} %bitcast.45, ...), custom_call_target="tpu_custom_call" | custom-call | flops 3623878656 | bytes 9437184 | tf_op jit(solution)/shard_map/attn_fwd/pallas_call | solution.py:436
  25.5 1.5 collective-permute-start.3
  27.8 1.5 collective-permute-start.5
  29.4 4.3 %grad_in.1.grad_in_ref = bf16[288,2048]{1,0:T(8,128)(2,1)} custom-call(bf16[288,1024]{1,0:T(8,128)(2,1)} %bitcast.35, bf16[2048,1024]{1,0:T(8,128)(2,1)} %w_ref.13), custom_call_target="tpu_custom_call" | custom-call | flops 1207959552 | bytes 4718592 | tf_op jit(solution)/shard_map/grad_in/pallas_call | solution.py:457
  34.2 1.2 maximum_maximum_fusion
  35.3 6.8 %merge_mid.1 = (bf16[288,2048]{1,0:T(8,128)(2,1)}, bf16[1152,512]{1,0:T(8,128)(2,1)}, bf16[1152,512]{1,0:T(8,128)(2,1)}, bf16[192,512]{1,0:T(8,128)(2,1)}, bf16[...) custom-call(bf16[1152,512]{1,0:T(8,128)(2,1)} %bitcast.46, bf16[1152,512]{1,0:T(8,128)(2,1)} %bitcast.31, ...), custom_call_target="tpu_custom_call" | custom-call | flops 2415919104 | bytes 7077888 | tf_op jit(solution)/shard_map/merge_mid/pallas_call | solution.py:471
  42.1 4.7 %merge_dw.3 = bf16[1024,1152]{1,0:T(8,128)(2,1)} custom-call(s32[1]{0:T(128)} %bitcast.22._, bf16[288,2048]{1,0:T(8,128)(2,1)} %get-tuple-element.39.a_ref.merged_in_ref, bf16[288,1024]{1,0:T(8,128)(2,1)} %bitcast.36, bf16[1152,512]{1,0:T(8,128)(2,1)} %bitcast.32, bf16[1152,512]{1,0:T(8,128)(2,1)} %get-tuple-element.51.gmix_ref), custom_call_target="tpu_custom_call" | custom-call | flops 1207959552 | bytes 3538944 | tf_op jit(solution)/shard_map/merge_dw/pallas_call | solution.py:494
  46.8 4.7 %merge_dw.2 = bf16[1024,1152]{1,0:T(8,128)(2,1)} custom-call(s32[1]{0:T(128)} %bitcast.23._, bf16[288,2048]{1,0:T(8,128)(2,1)} %get-tuple-element.39.a_ref.merged_in_ref, bf16[288,1024]{1,0:T(8,128)(2,1)} %bitcast.37, bf16[1152,512]{1,0:T(8,128)(2,1)} %bitcast.33, bf16[1152,512]{1,0:T(8,128)(2,1)} %get-tuple-element.51.gmix_ref), custom_call_target="tpu_custom_call" | custom-call | flops 1207959552 | bytes 3538944 | tf_op jit(solution)/shard_map/merge_dw/pallas_call | solution.py:494
  51.7 3.0 %add_convert_fusion = bf16[512,1152]{1,0:T(8,128)(2,1)} fusion(bf16[1024,1152]{1,0:T(8,128)(2,1)} %collective-permute-done.24, s32[]{:T(128)S(6)} %select_n.227, bf16[1024,1152]{1,0:T(8,128)(2,1)} %merge_dw.2), kind=kLoop, calls=%fused_computation.2 | loop fusion | flops 2359296 | bytes 3538948 | tf_op jit(solution)/shard_map/convert_element_type | solution.py:344
  55.3 15.9 %collective-permute-done.25 = bf16[512,1152]{1,0:T(8,128)(2,1)S(1)} collective-permute-done((bf16[512,1152]{1,0:T(8,128)(2,1)}, bf16[512,1152]{1,0:T(8,128)(2,1)S(1)}, u32[]{:S(2)}, u32[]{:S(2)}) %collective-permute-start.25) | collective-permute-done | bytes 1179680 | tf_op jit(solution)/shard_map/ppermute | solution.py:370
  71.2 2.7 %add_convert_fusion.1 = bf16[256,1152]{1,0:T(8,128)(2,1)} fusion(bf16[512,1152]{1,0:T(8,128)(2,1)S(1)} %collective-permute-done.25, s32[]{:T(128)S(6)} %select_n.228, bf16[1024,1152]{1,0:T(8,128)(2,1)} %collective-permute-done.24, s32[]{:T(128)S(6)} %dynamic_slice.253, bf16[1024,1152]{1,0:T(8,128)(2,1)S(1)} %copy-done.1), kind=kLoop, calls=%fused_computation.5 | loop fusion | flops 1769472 | bytes 2359304 | tf_op jit(solution)/shard_map/convert_element_type | solution.py:344
  74.8 1.0 collective-permute-start.7
  75.8 1.0 collective-permute-start.8
  76.8 8.1 %collective-permute-done.8 = bf16[24,512]{1,0:T(8,128)(2,1)} collective-permute-done((bf16[24,512]{1,0:T(8,128)(2,1)}, bf16[24,512]{1,0:T(8,128)(2,1)}, u32[]{:S(2)}, u32[]{:S(2)}) %collective-permute-start.8) | collective-permute-done | bytes 24608 | tf_op jit(solution)/shard_map/ppermute | solution.py:314
  85.2 3.0 %assemble.1.ga_ref = bf16[1280,512]{1,0:T(8,128)(2,1)} custom-call(bf16[1152,512]{1,0:T(8,128)(2,1)} %get-tuple-element.40.own_ref, bf16[24,8,512]{2,1,0:T(8,128)(2,1)} %bitcast.15.west_ref, bf16[144,512]{1,0:T(8,128)(2,1)} %collective-permute-done.7.south_ref, bf16[3,8,512]{2,1,0:T(8,128)(2,1)} %bitcast.16.corner_ref), custom_call_target="tpu_custom_call" | custom-call | flops 707788800 | bytes 3538944 | tf_op jit(solution)/shard_map/assemble/pallas_call | solution.py:513
  88.3 3.3 %shard_map.153.prev_ref = bf16[3,1280,512]{2,1,0:T(8,128)(2,1)} custom-call(bf16[1280,512]{1,0:T(8,128)(2,1)} %assemble.1.ga_ref, bf16[3,1280,512]{2,1,0:T(8,128)(2,1)} %get-tuple-element.44.qkv_ref, bf16[4,2560,80]{2,1,0:T(8,128)(2,1)} %get-tuple-element.45.prob_ref), custom_call_target="tpu_custom_call" | custom-call | flops 905969664 | bytes 2359296 | tf_op jit(solution)/shard_map/pallas_call | solution.py:539
  91.5 1.7 add_convert_fusion.7
  93.3 1.1 collective-permute-start.27
  94.3 2.0 collective-permute-start.29
  96.8 3.3 %shard_map.154.prev_ref = bf16[3,1280,512]{2,1,0:T(8,128)(2,1)} custom-call(bf16[1280,512]{1,0:T(8,128)(2,1)} %assemble.1.ga_ref, bf16[3,1280,512]{2,1,0:T(8,128)(2,1)} %get-tuple-element.44.qkv_ref, bf16[4,2560,80]{2,1,0:T(8,128)(2,1)} %get-tuple-element.45.prob_ref, bf16[3,1280,512]{2,1,0:T(8,128)(2,1)} %shard_map.153.prev_ref), custom_call_target="tpu_custom_call", output_to_operand_aliasing={{}: (3, {})} | custom-call | flops 905969664 | bytes 2359296 | tf_op jit(solution)/shard_map/pallas_call | solution.py:539
  100.1 3.3 %shard_map.155.prev_ref = bf16[3,1280,512]{2,1,0:T(8,128)(2,1)} custom-call(bf16[1280,512]{1,0:T(8,128)(2,1)} %assemble.1.ga_ref, bf16[3,1280,512]{2,1,0:T(8,128)(2,1)} %get-tuple-element.44.qkv_ref, bf16[4,2560,80]{2,1,0:T(8,128)(2,1)} %get-tuple-element.45.prob_ref, bf16[3,1280,512]{2,1,0:T(8,128)(2,1)} %shard_map.154.prev_ref), custom_call_target="tpu_custom_call", output_to_operand_aliasing={{}: (3, {})} | custom-call | flops 905969664 | bytes 2359296 | tf_op jit(solution)/shard_map/pallas_call | solution.py:539
  103.7 5.0 %collective-permute-done.28 = bf16[64,1152]{1,0:T(8,128)(2,1)S(1)} collective-permute-done((bf16[64,1152]{1,0:T(8,128)(2,1)S(1)}, bf16[64,1152]{1,0:T(8,128)(2,1)S(1)}, u32[]{:S(2)}, u32[]{:S(2)}) %collective-permute-start.28) | collective-permute-done | bytes 147488 | tf_op jit(solution)/shard_map/ppermute | solution.py:376
  108.8 1.3 constant_dynamic-update-slice_fusion.5
  110.1 3.3 %shard_map.156.gqkv_ref = bf16[3,1280,512]{2,1,0:T(8,128)(2,1)} custom-call(bf16[1280,512]{1,0:T(8,128)(2,1)} %assemble.1.ga_ref, bf16[3,1280,512]{2,1,0:T(8,128)(2,1)} %get-tuple-element.44.qkv_ref, bf16[4,2560,80]{2,1,0:T(8,128)(2,1)} %get-tuple-element.45.prob_ref, bf16[3,1280,512]{2,1,0:T(8,128)(2,1)} %shard_map.155.prev_ref), custom_call_target="tpu_custom_call", output_to_operand_aliasing={{}: (3, {})} | custom-call | flops 905969664 | bytes 2359296 | tf_op jit(solution)/shard_map/pallas_call | solution.py:539
  113.4 4.4 %qkv_dw.3 = bf16[768,512]{1,0:T(8,128)(2,1)} custom-call(s32[1]{0:T(128)} %bitcast.22._, bf16[1280,512]{1,0:T(8,128)(2,1)} %get-tuple-element.52.normed_ref, bf16[3,1280,512]{2,1,0:T(8,128)(2,1)} %shard_map.156.gqkv_ref), custom_call_target="tpu_custom_call" | custom-call | flops 905969664 | bytes 2949120 | tf_op jit(solution)/shard_map/qkv_dw/pallas_call | solution.py:553
  117.8 3.2 %collective-permute-start.31 = (bf16[64,1152]{1,0:T(8,128)(2,1)S(1)}, bf16[64,1152]{1,0:T(8,128)(2,1)S(1)}, u32[]{:S(2)}, u32[]{:S(2)}) collective-permute-start(bf16[64,1152]{1,0:T(8,128)(2,1)S(1)} %get-tuple-element.64), channel_id=1, source_target_pairs={{0,16},{8,24},{16,0},{24,8},{1,17},{9,25},{17,1},{25,9},{2,18},{10... | collective-permute-start | bytes 442376 | tf_op jit(solution)/shard_map/ppermute | solution.py:382
  121.0 1.2 collective-permute-start.32
  122.2 9.8 %collective-permute-done.31 = bf16[64,1152]{1,0:T(8,128)(2,1)S(1)} collective-permute-done((bf16[64,1152]{1,0:T(8,128)(2,1)S(1)}, bf16[64,1152]{1,0:T(8,128)(2,1)S(1)}, u32[]{:S(2)}, u32[]{:S(2)}) %collective-permute-start.31) | collective-permute-done | bytes 147488 | tf_op jit(solution)/shard_map/ppermute | solution.py:382
  132.7 4.4 %qkv_dw.2 = bf16[768,512]{1,0:T(8,128)(2,1)} custom-call(s32[1]{0:T(128)} %bitcast.23._, bf16[1280,512]{1,0:T(8,128)(2,1)} %get-tuple-element.52.normed_ref, bf16[3,1280,512]{2,1,0:T(8,128)(2,1)} %shard_map.156.gqkv_ref), custom_call_target="tpu_custom_call" | custom-call | flops 905969664 | bytes 2949120 | tf_op jit(solution)/shard_map/qkv_dw/pallas_call | solution.py:553
  137.1 2.1 add_convert_fusion.2
  140.1 2.7 %collective-permute-done.33 = bf16[256,1152]{1,0:T(8,128)(2,1)S(1)} collective-permute-done((bf16[256,1152]{1,0:T(8,128)(2,1)S(1)}, bf16[256,1152]{1,0:T(8,128)(2,1)S(1)}, u32[]{:S(2)}, u32[]{:S(2)}) %collective-permute-start.33) | collective-permute-done | bytes 589856 | tf_op jit(solution)/shard_map/ppermute | solution.py:385
  142.9 1.1 pad_maximum_fusion.1
  144.0 3.3 %collective-permute-done.13 = bf16[384,512]{1,0:T(8,128)(2,1)} collective-permute-done((bf16[384,512]{1,0:T(8,128)(2,1)}, bf16[384,512]{1,0:T(8,128)(2,1)}, u32[]{:S(2)}, u32[]{:S(2)}) %collective-permute-start.13) | collective-permute-done | bytes 393248 | tf_op jit(solution)/shard_map/ppermute | solution.py:370
  147.3 1.2 add_convert_fusion.3
  148.5 1.5 collective-permute-start.14
  150.0 6.3 %collective-permute-done.14 = bf16[192,512]{1,0:T(8,128)(2,1)S(1)} collective-permute-done((bf16[192,512]{1,0:T(8,128)(2,1)S(1)}, bf16[192,512]{1,0:T(8,128)(2,1)S(1)}, u32[]{:S(2)}, u32[]{:S(2)}) %collective-permute-start.14) | collective-permute-done | bytes 196640 | tf_op jit(solution)/shard_map/ppermute | solution.py:370
  156.3 1.1 add_convert_fusion.11
  157.4 3.5 %collective-permute-start.15 = (bf16[48,512]{1,0:T(8,128)(2,1)S(1)}, bf16[48,512]{1,0:T(8,128)(2,1)S(1)}, u32[]{:S(2)}, u32[]{:S(2)}) collective-permute-start(bf16[48,512]{1,0:T(8,128)(2,1)S(1)} %get-tuple-element.72), channel_id=1, source_target_pairs={{0,8},{8,0},{16,24},{24,16},{1,9},{9,1},{17,25},{25,17},{2,10},{10... | collective-permute-start | bytes 147464 | tf_op jit(solution)/shard_map/ppermute | solution.py:376
  160.9 2.1 collective-permute-start.17
  163.1 3.9 %collective-permute-done.17 = bf16[48,512]{1,0:T(8,128)(2,1)} collective-permute-done((bf16[48,512]{1,0:T(8,128)(2,1)S(1)}, bf16[48,512]{1,0:T(8,128)(2,1)}, u32[]{:S(2)}, u32[]{:S(2)}) %collective-permute-start.17) | collective-permute-done | bytes 49184 | tf_op jit(solution)/shard_map/ppermute | solution.py:376
  166.9 1.2 collective-permute-done.16
  168.2 1.6 constant_dynamic-update-slice_fusion.3
  169.8 2.5 %collective-permute-start.19 = (bf16[48,512]{1,0:T(8,128)(2,1)}, bf16[48,512]{1,0:T(8,128)(2,1)S(1)}, u32[]{:S(2)}, u32[]{:S(2)}) collective-permute-start(bf16[48,512]{1,0:T(8,128)(2,1)} %get-tuple-element.66), channel_id=1, source_target_pairs={{0,16},{8,24},{16,0},{24,8},{1,17},{9,25},{17,1},{25,9},{2,18},{10... | collective-permute-start | bytes 147464 | tf_op jit(solution)/shard_map/ppermute | solution.py:382
  172.3 1.9 collective-permute-start.20
  175.1 3.3 %collective-permute-done.20 = bf16[48,512]{1,0:T(8,128)(2,1)S(1)} collective-permute-done((bf16[48,512]{1,0:T(8,128)(2,1)}, bf16[48,512]{1,0:T(8,128)(2,1)S(1)}, u32[]{:S(2)}, u32[]{:S(2)}) %collective-permute-start.20) | collective-permute-done | bytes 49184 | tf_op jit(solution)/shard_map/ppermute | solution.py:382
  178.4 1.5 collective-permute-start.21
  179.9 5.3 %collective-permute-done.21 = bf16[192,512]{1,0:T(8,128)(2,1)S(1)} collective-permute-done((bf16[192,512]{1,0:T(8,128)(2,1)S(1)}, bf16[192,512]{1,0:T(8,128)(2,1)S(1)}, u32[]{:S(2)}, u32[]{:S(2)}) %collective-permute-start.21) | collective-permute-done | bytes 196640 | tf_op jit(solution)/shard_map/ppermute | solution.py:385
  186.2 6.9 %collective-permute-done.22 = bf16[384,512]{1,0:T(8,128)(2,1)S(1)} collective-permute-done((bf16[384,512]{1,0:T(8,128)(2,1)S(1)}, bf16[384,512]{1,0:T(8,128)(2,1)S(1)}, u32[]{:S(2)}, u32[]{:S(2)}) %collective-permute-start.22) | collective-permute-done | bytes 393248 | tf_op jit(solution)/shard_map/ppermute | solution.py:385
  193.4 6.7 %input_grad.1 = (bf16[1152,512]{1,0:T(8,128)(2,1)}, bf16[192,512]{1,0:T(8,128)(2,1)}, bf16[144,512]{1,0:T(8,128)(2,1)}, bf16[24,512]{1,0:T(8,128)(2,1)}) custom-call(bf16[3,1280,512]{2,1,0:T(8,128)(2,1)} %shard_map.156.gqkv_ref, bf16[1280,512]{1,0:T(8,128)(2,1)} %get-tuple-element.46.x_ref, f32[1,512]{1,0:T(1,128)} %bitcast.52, bf16[512,1536]{1,0:T(8,128)(2,1)} %w_ref.11), custom_call_target="tpu_custom_call" | custom-call | flops 1811939328 | bytes 7077888 | tf_op jit(solution)/shard_map/input_grad/pallas_call | solution.py:570
  200.1 1.2 collective-permute-start.9
  201.3 1.7 collective-permute-start.10
  203.0 4.2 %merged.1 = bf16[288,1024]{1,0:T(8,128)(2,1)} custom-call(bf16[288,2048]{1,0:T(8,128)(2,1)} %get-tuple-element.39.a_ref.merged_in_ref, bf16[2048,1024]{1,0:T(8,128)(2,1)} %w_ref.13), custom_call_target="tpu_custom_call" | custom-call | flops 1207959552 | bytes 4718592 | tf_op jit(solution)/shard_map/merged/pallas_call | solution.py:586
  207.2 1.7 slice.52
  209.0 0.9 slice.54
  210.0 2.6 %convert_add_fusion = f32[24,48,512]{2,1,0:T(8,128)} fusion(bf16[24,48,512]{2,1,0:T(8,128)(2,1)S(1)} %bitcast.34, bf16[3,6,512]{2,1,0:T(8,128)(2,1)} %bitcast.30, bf16[3,42,512]{2,1,0:T(8,128)(2,1)S(1)} %slice.54, bf16[21,6,512]{2,1,0:T(8,128)(2,1)S(1)} %slice.53, bf16[21,42,512]{2,1,0:T(8,128)(2,1)S(1)} %slice.52), kind=kLoop, calls=%fused_computation.1 | loop fusion | flops 5898240 | bytes 4718592 | tf_op jit(solution)/shard_map/add | solution.py:584
  212.6 2.7 %q_last.2 = (f32[512,1536]{1,0:T(8,128)}, f32[1,512]{1,0:T(1,128)}) custom-call(s32[1]{0:T(128)} %bitcast.23._, bf16[768,512]{1,0:T(8,128)(2,1)} %copy-done.4, bf16[512,1536]{1,0:T(8,128)(2,1)} %w_ref.11, f32[1,512]{1,0:T(1,128)} %bitcast.53), custom_call_target="tpu_custom_call" | custom-call | flops 294912000 | bytes 1769472 | tf_op jit(solution)/shard_map/q_last/pallas_call | solution.py:622
  216.2 2.7 %q_last.3 = (f32[512,1536]{1,0:T(8,128)}, f32[1,512]{1,0:T(1,128)}) custom-call(s32[1]{0:T(128)} %bitcast.22._, bf16[768,512]{1,0:T(8,128)(2,1)} %copy-done.7, bf16[512,1536]{1,0:T(8,128)(2,1)} %w_ref.11, f32[1,512]{1,0:T(1,128)} %bitcast.54, f32[512,1536]{1,0:T(8,128)} %get-tuple-element.53.refs_0_, ...), custom_call_target="tpu_custom_call", output_to_operand_aliasing={{0}: (4, {}), {1}: (5, {})} | custom-call | flops 294912000 | bytes 1769472 | tf_op jit(solution)/shard_map/q_last/pallas_call | solution.py:622
  218.9 4.0 %m_last.2 = (f32[2048,1024]{1,0:T(8,128)}, f32[512,512]{1,0:T(8,128)}, f32[1,2048]{1,0:T(1,128)}) custom-call(s32[1]{0:T(128)} %bitcast.23._, bf16[1024,1152]{1,0:T(8,128)(2,1)} %copy-done.2, bf16[2048,1024]{1,0:T(8,128)(2,1)} %w_ref.13, f32[1,2048]{1,0:T(1,128)} %bitcast.48), custom_call_target="tpu_custom_call" | custom-call | flops 589824000 | bytes 3538944 | tf_op jit(solution)/shard_map/m_last/pallas_call | solution.py:599
  222.9 4.1 %m_last.3 = (f32[2048,1024]{1,0:T(8,128)}, f32[512,512]{1,0:T(8,128)}, f32[1,2048]{1,0:T(1,128)}) custom-call(s32[1]{0:T(128)} %bitcast.22._, bf16[1024,1152]{1,0:T(8,128)(2,1)} %collective-permute-done.35.value_ref, bf16[2048,1024]{1,0:T(8,128)(2,1)} %w_ref.13, f32[1,2048]{1,0:T(1,128)} %bitcast.49, ...), custom_call_target="tpu_custom_call", output_to_operand_aliasing={{0}: (4, {}), {1}: (5, {}), {2}: (6, {})} | custom-call | flops 589824000 | bytes 3538944 | tf_op jit(solution)/shard_map/m_last/pallas_call | solution.py:599
  (95 shorter events, 14.7 us)
Async XLA Ops:
  1.4 9.9 %collective-permute-start.2 = (bf16[24,512]{1,0:T(8,128)(2,1)S(1)}, bf16[24,512]{1,0:T(8,128)(2,1)S(1)}, u32[]{:S(2)}, u32[]{:S(2)}) collective-permute-start(bf16[24,512]{1,0:T(8,128)(2,1)S(1)} %slice_bitcast_fusion.1), channel_id=1, source_target_pairs={{0,9},{1,10},{2,11},{3,12},{4,13},{5,14},{6,15},{7,8},{8,17},{9,18... | collective-permute-start | bytes 73736 | tf_op jit(solution)/shard_map/ppermute | solution.py:314
  4.8 7.9 %collective-permute-start.1 = (bf16[144,512]{1,0:T(8,128)(2,1)S(1)}, bf16[144,512]{1,0:T(8,128)(2,1)S(1)}, u32[]{:S(2)}, u32[]{:S(2)}) collective-permute-start(bf16[144,512]{1,0:T(8,128)(2,1)S(1)} %bitcast.43), channel_id=1, source_target_pairs={{0,8},{1,9},{2,10},{3,11},{4,12},{5,13},{6,14},{7,15},{8,16},{9,17... | collective-permute-start | bytes 442376 | tf_op jit(solution)/shard_map/ppermute | solution.py:314
  7.4 6.0 %collective-permute-start = (bf16[192,512]{1,0:T(8,128)(2,1)S(1)}, bf16[192,512]{1,0:T(8,128)(2,1)S(1)}, u32[]{:S(2)}, u32[]{:S(2)}) collective-permute-start(bf16[192,512]{1,0:T(8,128)(2,1)S(1)} %slice_bitcast_fusion), channel_id=1, source_target_pairs={{0,1},{1,2},{2,3},{3,4},{4,5},{5,6},{6,7},{7,0},{8,9},{9,10},{10,1... | collective-permute-start | bytes 589832 | tf_op jit(solution)/shard_map/ppermute | solution.py:314
  11.3 2.1 copy-start.12
  12.7 0.7 copy-start.11
  13.4 0.7 copy-start.10
  25.5 8.7 %collective-permute-start.3 = (bf16[192,512]{1,0:T(8,128)(2,1)}, bf16[192,512]{1,0:T(8,128)(2,1)S(1)}, u32[]{:S(2)}, u32[]{:S(2)}) collective-permute-start(bf16[192,512]{1,0:T(8,128)(2,1)} %get-tuple-element.36), channel_id=1, source_target_pairs={{0,7},{1,0},{2,1},{3,2},{4,3},{5,4},{6,5},{7,6},{8,15},{9,8},{10,9... | collective-permute-start | bytes 589832 | tf_op jit(solution)/shard_map/ppermute | solution.py:314
  26.9 7.1 %collective-permute-start.4 = (bf16[144,512]{1,0:T(8,128)(2,1)}, bf16[144,512]{1,0:T(8,128)(2,1)S(1)}, u32[]{:S(2)}, u32[]{:S(2)}) collective-permute-start(bf16[144,512]{1,0:T(8,128)(2,1)} %get-tuple-element.37), channel_id=1, source_target_pairs={{0,24},{1,25},{2,26},{3,27},{4,28},{5,29},{6,30},{7,31},{8,0},{9,1... | collective-permute-start | bytes 442376 | tf_op jit(solution)/shard_map/ppermute | solution.py:314
  27.8 6.3 %collective-permute-start.5 = (bf16[24,512]{1,0:T(8,128)(2,1)}, bf16[24,512]{1,0:T(8,128)(2,1)S(1)}, u32[]{:S(2)}, u32[]{:S(2)}) collective-permute-start(bf16[24,512]{1,0:T(8,128)(2,1)} %get-tuple-element.38), channel_id=1, source_target_pairs={{0,31},{1,24},{2,25},{3,26},{4,27},{5,28},{6,29},{7,30},{8,7},{9,0... | collective-permute-start | bytes 73736 | tf_op jit(solution)/shard_map/ppermute | solution.py:314
  29.4 4.3 %copy-start.6 = (bf16[1152,512]{1,0:T(8,128)(2,1)S(1)}, bf16[1152,512]{1,0:T(8,128)(2,1)}, u32[]{:S(2)}) copy-start(bf16[1152,512]{1,0:T(8,128)(2,1)} %get-tuple-element.35) | copy-start | bytes 3538948
  46.8 4.9 %collective-permute-start.24 = (bf16[1024,1152]{1,0:T(8,128)(2,1)}, bf16[1024,1152]{1,0:T(8,128)(2,1)}, u32[]{:S(2)}, u32[]{:S(2)}) collective-permute-start(bf16[1024,1152]{1,0:T(8,128)(2,1)} %merge_dw.3), channel_id=1, source_target_pairs={{0,1},{1,0},{2,3},{3,2},{4,5},{5,4},{6,7},{7,6},{8,9},{9,8},{10,11... | collective-permute-start | bytes 7077896 | tf_op jit(solution)/shard_map/ppermute | solution.py:365
  51.5 19.7 %copy-start.1 = (bf16[1024,1152]{1,0:T(8,128)(2,1)S(1)}, bf16[1024,1152]{1,0:T(8,128)(2,1)}, u32[]{:S(2)}) copy-start(bf16[1024,1152]{1,0:T(8,128)(2,1)} %merge_dw.2) | copy-start | bytes 7077892
  54.8 16.4 %collective-permute-start.25 = (bf16[512,1152]{1,0:T(8,128)(2,1)}, bf16[512,1152]{1,0:T(8,128)(2,1)S(1)}, u32[]{:S(2)}, u32[]{:S(2)}) collective-permute-start(bf16[512,1152]{1,0:T(8,128)(2,1)} %add_convert_fusion), channel_id=1, source_target_pairs={{0,2},{1,5},{2,0},{3,7},{4,6},{5,1},{6,4},{7,3},{8,10},{9,13},{10,... | collective-permute-start | bytes 3538952 | tf_op jit(solution)/shard_map/ppermute | solution.py:370
  71.2 20.4 %copy-start.5 = (bf16[512,1152]{1,0:T(8,128)(2,1)}, bf16[512,1152]{1,0:T(8,128)(2,1)S(1)}, u32[]{:S(2)}) copy-start(bf16[512,1152]{1,0:T(8,128)(2,1)S(1)} %collective-permute-done.25) | copy-start | bytes 3538948
  73.9 17.7 %collective-permute-start.26 = (bf16[256,1152]{1,0:T(8,128)(2,1)}, bf16[256,1152]{1,0:T(8,128)(2,1)}, u32[]{:S(2)}, u32[]{:S(2)}) collective-permute-start(bf16[256,1152]{1,0:T(8,128)(2,1)} %add_convert_fusion.1), channel_id=1, source_target_pairs={{0,4},{1,3},{2,6},{3,1},{4,0},{5,7},{6,2},{7,5},{8,12},{9,11},{10,... | collective-permute-start | bytes 1769480 | tf_op jit(solution)/shard_map/ppermute | solution.py:370
  74.8 10.4 %collective-permute-start.6 = (bf16[192,512]{1,0:T(8,128)(2,1)}, bf16[192,512]{1,0:T(8,128)(2,1)}, u32[]{:S(2)}, u32[]{:S(2)}) collective-permute-start(bf16[192,512]{1,0:T(8,128)(2,1)} %get-tuple-element.41), channel_id=1, source_target_pairs={{0,1},{1,2},{2,3},{3,4},{4,5},{5,6},{6,7},{7,0},{8,9},{9,10},{10,1... | collective-permute-start | bytes 589832 | tf_op jit(solution)/shard_map/ppermute | solution.py:314
  74.8 10.1 %collective-permute-start.7 = (bf16[144,512]{1,0:T(8,128)(2,1)}, bf16[144,512]{1,0:T(8,128)(2,1)}, u32[]{:S(2)}, u32[]{:S(2)}) collective-permute-start(bf16[144,512]{1,0:T(8,128)(2,1)} %get-tuple-element.42), channel_id=1, source_target_pairs={{0,8},{1,9},{2,10},{3,11},{4,12},{5,13},{6,14},{7,15},{8,16},{9,17... | collective-permute-start | bytes 442376 | tf_op jit(solution)/shard_map/ppermute | solution.py:314
  75.8 9.1 %collective-permute-start.8 = (bf16[24,512]{1,0:T(8,128)(2,1)}, bf16[24,512]{1,0:T(8,128)(2,1)}, u32[]{:S(2)}, u32[]{:S(2)}) collective-permute-start(bf16[24,512]{1,0:T(8,128)(2,1)} %get-tuple-element.43), channel_id=1, source_target_pairs={{0,9},{1,10},{2,11},{3,12},{4,13},{5,14},{6,15},{7,8},{8,17},{9,18... | collective-permute-start | bytes 73736 | tf_op jit(solution)/shard_map/ppermute | solution.py:314
  93.3 10.1 %collective-permute-start.27 = (bf16[64,1152]{1,0:T(8,128)(2,1)S(1)}, bf16[64,1152]{1,0:T(8,128)(2,1)S(1)}, u32[]{:S(2)}, u32[]{:S(2)}) collective-permute-start(bf16[64,1152]{1,0:T(8,128)(2,1)S(1)} %get-tuple-element.67), channel_id=1, source_target_pairs={{0,8},{8,0},{16,24},{24,16},{1,9},{9,1},{17,25},{25,17},{2,10},{10... | collective-permute-start | bytes 442376 | tf_op jit(solution)/shard_map/ppermute | solution.py:376
  94.3 9.4 %collective-permute-start.29 = (bf16[64,1152]{1,0:T(8,128)(2,1)S(1)}, bf16[64,1152]{1,0:T(8,128)(2,1)S(1)}, u32[]{:S(2)}, u32[]{:S(2)}) collective-permute-start(bf16[64,1152]{1,0:T(8,128)(2,1)S(1)} %get-tuple-element.68), channel_id=1, source_target_pairs={{0,24},{8,16},{16,8},{24,0},{1,25},{9,17},{17,9},{25,1},{2,26},{10... | collective-permute-start | bytes 442376 | tf_op jit(solution)/shard_map/ppermute | solution.py:376
  96.3 12.4 %collective-permute-start.28 = (bf16[64,1152]{1,0:T(8,128)(2,1)S(1)}, bf16[64,1152]{1,0:T(8,128)(2,1)S(1)}, u32[]{:S(2)}, u32[]{:S(2)}) collective-permute-start(bf16[64,1152]{1,0:T(8,128)(2,1)S(1)} %get-tuple-element.69), channel_id=1, source_target_pairs={{0,16},{8,24},{16,0},{24,8},{1,17},{9,25},{17,1},{25,9},{2,18},{10... | collective-permute-start | bytes 442376 | tf_op jit(solution)/shard_map/ppermute | solution.py:376
  110.1 12.1 %collective-permute-start.30 = (bf16[64,1152]{1,0:T(8,128)(2,1)S(1)}, bf16[64,1152]{1,0:T(8,128)(2,1)S(1)}, u32[]{:S(2)}, u32[]{:S(2)}) collective-permute-start(bf16[64,1152]{1,0:T(8,128)(2,1)S(1)} %get-tuple-element.64), channel_id=1, source_target_pairs={{0,8},{8,0},{16,24},{24,16},{1,9},{9,1},{17,25},{25,17},{2,10},{10... | collective-permute-start | bytes 442376 | tf_op jit(solution)/shard_map/ppermute | solution.py:382
  117.8 19.3 %collective-permute-start.12 = (bf16[768,512]{1,0:T(8,128)(2,1)}, bf16[768,512]{1,0:T(8,128)(2,1)S(1)}, u32[]{:S(2)}, u32[]{:S(2)}) collective-permute-start(bf16[768,512]{1,0:T(8,128)(2,1)} %qkv_dw.3), channel_id=1, source_target_pairs={{0,1},{1,0},{2,3},{3,2},{4,5},{5,4},{6,7},{7,6},{8,9},{9,8},{10,11... | collective-permute-start | bytes 2359304 | tf_op jit(solution)/shard_map/ppermute | solution.py:365
  117.8 14.2 %collective-permute-start.31 = (bf16[64,1152]{1,0:T(8,128)(2,1)S(1)}, bf16[64,1152]{1,0:T(8,128)(2,1)S(1)}, u32[]{:S(2)}, u32[]{:S(2)}) collective-permute-start(bf16[64,1152]{1,0:T(8,128)(2,1)S(1)} %get-tuple-element.64), channel_id=1, source_target_pairs={{0,16},{8,24},{16,0},{24,8},{1,17},{9,25},{17,1},{25,9},{2,18},{10... | collective-permute-start | bytes 442376 | tf_op jit(solution)/shard_map/ppermute | solution.py:382
  121.0 11.0 %collective-permute-start.32 = (bf16[64,1152]{1,0:T(8,128)(2,1)S(1)}, bf16[64,1152]{1,0:T(8,128)(2,1)S(1)}, u32[]{:S(2)}, u32[]{:S(2)}) collective-permute-start(bf16[64,1152]{1,0:T(8,128)(2,1)S(1)} %get-tuple-element.64), channel_id=1, source_target_pairs={{0,24},{8,16},{16,8},{24,0},{1,25},{9,17},{17,9},{25,1},{2,26},{10... | collective-permute-start | bytes 442376 | tf_op jit(solution)/shard_map/ppermute | solution.py:382
  132.1 10.7 %collective-permute-start.33 = (bf16[256,1152]{1,0:T(8,128)(2,1)S(1)}, bf16[256,1152]{1,0:T(8,128)(2,1)S(1)}, u32[]{:S(2)}, u32[]{:S(2)}) collective-permute-start(bf16[256,1152]{1,0:T(8,128)(2,1)S(1)} %constant_dynamic-update-slice_fusion.6), channel_id=1, source_target_pairs={{0,4},{1,3},{2,6},{3,1},{4,0},{5,7},{6,2},{7,5},{8,12},{9,11},{10,... | collective-permute-start | bytes 1769480 | tf_op jit(solution)/shard_map/ppermute | solution.py:385
  137.1 3.0 %copy-start.8 = (bf16[768,512]{1,0:T(8,128)(2,1)}, bf16[768,512]{1,0:T(8,128)(2,1)S(1)}, u32[]{:S(2)}) copy-start(bf16[768,512]{1,0:T(8,128)(2,1)S(1)} %collective-permute-done.12) | copy-start | bytes 2359300
  139.2 8.1 %copy-start.3 = (bf16[768,512]{1,0:T(8,128)(2,1)S(1)}, bf16[768,512]{1,0:T(8,128)(2,1)}, u32[]{:S(2)}) copy-start(bf16[768,512]{1,0:T(8,128)(2,1)} %qkv_dw.2) | copy-start | bytes 2359300
  139.2 8.1 %collective-permute-start.13 = (bf16[384,512]{1,0:T(8,128)(2,1)}, bf16[384,512]{1,0:T(8,128)(2,1)}, u32[]{:S(2)}, u32[]{:S(2)}) collective-permute-start(bf16[384,512]{1,0:T(8,128)(2,1)} %add_convert_fusion.2), channel_id=1, source_target_pairs={{0,2},{1,5},{2,0},{3,7},{4,6},{5,1},{6,4},{7,3},{8,10},{9,13},{10,... | collective-permute-start | bytes 1179656 | tf_op jit(solution)/shard_map/ppermute | solution.py:370
  144.0 30.3 %collective-permute-start.34 = (bf16[512,1152]{1,0:T(8,128)(2,1)}, bf16[512,1152]{1,0:T(8,128)(2,1)S(1)}, u32[]{:S(2)}, u32[]{:S(2)}) collective-permute-start(bf16[512,1152]{1,0:T(8,128)(2,1)} %pad_maximum_fusion.1), channel_id=1, source_target_pairs={{0,2},{1,5},{2,0},{3,7},{4,6},{5,1},{6,4},{7,3},{8,10},{9,13},{10,... | collective-permute-start | bytes 3538952 | tf_op jit(solution)/shard_map/ppermute | solution.py:385
  148.5 7.8 %collective-permute-start.14 = (bf16[192,512]{1,0:T(8,128)(2,1)S(1)}, bf16[192,512]{1,0:T(8,128)(2,1)S(1)}, u32[]{:S(2)}, u32[]{:S(2)}) collective-permute-start(bf16[192,512]{1,0:T(8,128)(2,1)S(1)} %add_convert_fusion.3), channel_id=1, source_target_pairs={{0,4},{1,3},{2,6},{3,1},{4,0},{5,7},{6,2},{7,5},{8,12},{9,11},{10,... | collective-permute-start | bytes 589832 | tf_op jit(solution)/shard_map/ppermute | solution.py:370
  157.4 5.6 %collective-permute-start.15 = (bf16[48,512]{1,0:T(8,128)(2,1)S(1)}, bf16[48,512]{1,0:T(8,128)(2,1)S(1)}, u32[]{:S(2)}, u32[]{:S(2)}) collective-permute-start(bf16[48,512]{1,0:T(8,128)(2,1)S(1)} %get-tuple-element.72), channel_id=1, source_target_pairs={{0,8},{8,0},{16,24},{24,16},{1,9},{9,1},{17,25},{25,17},{2,10},{10... | collective-permute-start | bytes 147464 | tf_op jit(solution)/shard_map/ppermute | solution.py:376
  160.9 6.0 %collective-permute-start.17 = (bf16[48,512]{1,0:T(8,128)(2,1)S(1)}, bf16[48,512]{1,0:T(8,128)(2,1)}, u32[]{:S(2)}, u32[]{:S(2)}) collective-permute-start(bf16[48,512]{1,0:T(8,128)(2,1)S(1)} %get-tuple-element.73), channel_id=1, source_target_pairs={{0,24},{8,16},{16,8},{24,0},{1,25},{9,17},{17,9},{25,1},{2,26},{10... | collective-permute-start | bytes 147464 | tf_op jit(solution)/shard_map/ppermute | solution.py:376
  163.0 5.1 %collective-permute-start.16 = (bf16[48,512]{1,0:T(8,128)(2,1)S(1)}, bf16[48,512]{1,0:T(8,128)(2,1)}, u32[]{:S(2)}, u32[]{:S(2)}) collective-permute-start(bf16[48,512]{1,0:T(8,128)(2,1)S(1)} %get-tuple-element.74), channel_id=1, source_target_pairs={{0,16},{8,24},{16,0},{24,8},{1,17},{9,25},{17,1},{25,9},{2,18},{10... | collective-permute-start | bytes 147464 | tf_op jit(solution)/shard_map/ppermute | solution.py:376
  163.0 3.9 %copy-start.9 = (bf16[48,512]{1,0:T(8,128)(2,1)}, bf16[48,512]{1,0:T(8,128)(2,1)S(1)}, u32[]{:S(2)}) copy-start(bf16[48,512]{1,0:T(8,128)(2,1)S(1)} %collective-permute-done.15) | copy-start | bytes 147460
  169.8 4.6 %collective-permute-start.18 = (bf16[48,512]{1,0:T(8,128)(2,1)}, bf16[48,512]{1,0:T(8,128)(2,1)S(1)}, u32[]{:S(2)}, u32[]{:S(2)}) collective-permute-start(bf16[48,512]{1,0:T(8,128)(2,1)} %get-tuple-element.66), channel_id=1, source_target_pairs={{0,8},{8,0},{16,24},{24,16},{1,9},{9,1},{17,25},{25,17},{2,10},{10... | collective-permute-start | bytes 147464 | tf_op jit(solution)/shard_map/ppermute | solution.py:382
  169.8 5.4 %collective-permute-start.19 = (bf16[48,512]{1,0:T(8,128)(2,1)}, bf16[48,512]{1,0:T(8,128)(2,1)S(1)}, u32[]{:S(2)}, u32[]{:S(2)}) collective-permute-start(bf16[48,512]{1,0:T(8,128)(2,1)} %get-tuple-element.66), channel_id=1, source_target_pairs={{0,16},{8,24},{16,0},{24,8},{1,17},{9,25},{17,1},{25,9},{2,18},{10... | collective-permute-start | bytes 147464 | tf_op jit(solution)/shard_map/ppermute | solution.py:382
  172.3 6.1 %collective-permute-start.20 = (bf16[48,512]{1,0:T(8,128)(2,1)}, bf16[48,512]{1,0:T(8,128)(2,1)S(1)}, u32[]{:S(2)}, u32[]{:S(2)}) collective-permute-start(bf16[48,512]{1,0:T(8,128)(2,1)} %get-tuple-element.66), channel_id=1, source_target_pairs={{0,24},{8,16},{16,8},{24,0},{1,25},{9,17},{17,9},{25,1},{2,26},{10... | collective-permute-start | bytes 147464 | tf_op jit(solution)/shard_map/ppermute | solution.py:382
  175.0 18.3 %copy-start.2 = (bf16[1024,1152]{1,0:T(8,128)(2,1)}, bf16[1024,1152]{1,0:T(8,128)(2,1)S(1)}, u32[]{:S(2)}) copy-start(bf16[1024,1152]{1,0:T(8,128)(2,1)S(1)} %pad_maximum_fusion.value_ref) | copy-start | bytes 7077892
  175.0 47.9 %collective-permute-start.35 = (bf16[1024,1152]{1,0:T(8,128)(2,1)S(1)}, bf16[1024,1152]{1,0:T(8,128)(2,1)}, u32[]{:S(2)}, u32[]{:S(2)}) collective-permute-start(bf16[1024,1152]{1,0:T(8,128)(2,1)S(1)} %pad_maximum_fusion.value_ref), channel_id=1, source_target_pairs={{0,1},{1,0},{2,3},{3,2},{4,5},{5,4},{6,7},{7,6},{8,9},{9,8},{10,11... | collective-permute-start | bytes 7077896 | tf_op jit(solution)/shard_map/ppermute | solution.py:387
  178.4 6.8 %collective-permute-start.21 = (bf16[192,512]{1,0:T(8,128)(2,1)S(1)}, bf16[192,512]{1,0:T(8,128)(2,1)S(1)}, u32[]{:S(2)}, u32[]{:S(2)}) collective-permute-start(bf16[192,512]{1,0:T(8,128)(2,1)S(1)} %constant_dynamic-update-slice_fusion), channel_id=1, source_target_pairs={{0,4},{1,3},{2,6},{3,1},{4,0},{5,7},{6,2},{7,5},{8,12},{9,11},{10,... | collective-permute-start | bytes 589832 | tf_op jit(solution)/shard_map/ppermute | solution.py:385
  185.3 7.8 %collective-permute-start.22 = (bf16[384,512]{1,0:T(8,128)(2,1)S(1)}, bf16[384,512]{1,0:T(8,128)(2,1)S(1)}, u32[]{:S(2)}, u32[]{:S(2)}) collective-permute-start(bf16[384,512]{1,0:T(8,128)(2,1)S(1)} %pad_maximum_fusion.3), channel_id=1, source_target_pairs={{0,2},{1,5},{2,0},{3,7},{4,6},{5,1},{6,4},{7,3},{8,10},{9,13},{10,... | collective-permute-start | bytes 1179656 | tf_op jit(solution)/shard_map/ppermute | solution.py:385
  193.3 6.8 %copy-start.4 = (bf16[768,512]{1,0:T(8,128)(2,1)}, bf16[768,512]{1,0:T(8,128)(2,1)S(1)}, u32[]{:S(2)}) copy-start(bf16[768,512]{1,0:T(8,128)(2,1)S(1)} %pad_maximum_fusion.2.value_ref) | copy-start | bytes 2359300
  193.3 22.0 %collective-permute-start.23 = (bf16[768,512]{1,0:T(8,128)(2,1)S(1)}, bf16[768,512]{1,0:T(8,128)(2,1)S(1)}, u32[]{:S(2)}, u32[]{:S(2)}) collective-permute-start(bf16[768,512]{1,0:T(8,128)(2,1)S(1)} %pad_maximum_fusion.2.value_ref), channel_id=1, source_target_pairs={{0,1},{1,0},{2,3},{3,2},{4,5},{5,4},{6,7},{7,6},{8,9},{9,8},{10,11... | collective-permute-start | bytes 2359304 | tf_op jit(solution)/shard_map/ppermute | solution.py:387
  200.1 9.8 %collective-permute-start.9 = (bf16[192,512]{1,0:T(8,128)(2,1)}, bf16[192,512]{1,0:T(8,128)(2,1)S(1)}, u32[]{:S(2)}, u32[]{:S(2)}) collective-permute-start(bf16[192,512]{1,0:T(8,128)(2,1)} %get-tuple-element.48), channel_id=1, source_target_pairs={{0,7},{1,0},{2,1},{3,2},{4,3},{5,4},{6,5},{7,6},{8,15},{9,8},{10,9... | collective-permute-start | bytes 589832 | tf_op jit(solution)/shard_map/ppermute | solution.py:314
  201.3 7.7 %collective-permute-start.10 = (bf16[144,512]{1,0:T(8,128)(2,1)}, bf16[144,512]{1,0:T(8,128)(2,1)}, u32[]{:S(2)}, u32[]{:S(2)}) collective-permute-start(bf16[144,512]{1,0:T(8,128)(2,1)} %get-tuple-element.49), channel_id=1, source_target_pairs={{0,24},{1,25},{2,26},{3,27},{4,28},{5,29},{6,30},{7,31},{8,0},{9,1... | collective-permute-start | bytes 442376 | tf_op jit(solution)/shard_map/ppermute | solution.py:314
  203.0 6.9 %collective-permute-start.11 = (bf16[24,512]{1,0:T(8,128)(2,1)}, bf16[24,512]{1,0:T(8,128)(2,1)}, u32[]{:S(2)}, u32[]{:S(2)}) collective-permute-start(bf16[24,512]{1,0:T(8,128)(2,1)} %get-tuple-element.50), channel_id=1, source_target_pairs={{0,31},{1,24},{2,25},{3,26},{4,27},{5,28},{6,29},{7,30},{8,7},{9,0... | collective-permute-start | bytes 73736 | tf_op jit(solution)/shard_map/ppermute | solution.py:314
  207.2 2.7 %copy-start = (bf16[1152,512]{1,0:T(8,128)(2,1)S(1)}, bf16[1152,512]{1,0:T(8,128)(2,1)}, u32[]{:S(2)}) copy-start(bf16[1152,512]{1,0:T(8,128)(2,1)} %get-tuple-element.51.gmix_ref) | copy-start | bytes 3538948
  215.3 0.9 copy-start.7

commit v3 on v2

--- a/solution.py
+++ b/solution.py
@@ -205,10 +205,8 @@
     out_ref[...] = dot_nt(gm_ref[...], w_merge_ref[...]).astype(BF)
 
 
-def merge_grad_kernel(_, merged_in_ref, gm_ref, att_ref, gmix_ref, out_ref):
-    width = gm_ref.shape[1]
-    out_ref[:, :width] = dot_tn(merged_in_ref[...], gm_ref[...]).astype(BF)
-    out_ref[:, width:] = dot_tn(gmix_ref[...], att_ref[...]).T.astype(BF)
+def merge_grad_kernel(_, merged_in_ref, gm_ref, out_ref):
+    out_ref[...] = dot_tn(merged_in_ref[...], gm_ref[...]).astype(BF)
 
 
 def row_sums(value):
@@ -217,17 +215,16 @@
 
 
 def merge_last_kernel(_, value_ref, w_ref, gain_ref, *refs):
+    out_ref, dgain_ref = refs[-2:]
+    value = value_ref[...].astype(F32)
+    out_ref[...] = value
+    dgain_ref[...] = row_sums(value * w_ref[...].astype(F32)) / gain_ref[...]
+
+
+def qkv_last_kernel(_, value_ref, w_ref, gain_ref, *refs):
     out_ref, out_o_ref, dgain_ref = refs[-3:]
-    width = w_ref.shape[1]
-    value = value_ref[:, :width].astype(F32)
-    out_ref[...] = value
-    out_o_ref[...] = value_ref[:, width:].astype(F32)
-    dgain_ref[...] = row_sums(value * w_ref[...].astype(F32)) / gain_ref[...]
-
-
-def qkv_last_kernel(_, value_ref, w_ref, gain_ref, *refs):
-    out_ref, dgain_ref = refs[-2:]
-    height, features = value_ref.shape[0] // 3, value_ref.shape[1]
+    height, features = value_ref.shape[0] // 4, value_ref.shape[1]
+    out_o_ref[...] = value_ref[3 * height :, :].astype(F32)
     total = 0.0
     for t in range(3):
         lanes = slice(features * t, features * (t + 1))
@@ -268,10 +265,11 @@
             gqkv_ref[1, rows, lanes] = jnp.where(low, dk[:stride], dk[stride:]).astype(BF)
 
 
-def qkv_grad_kernel(_, normed_ref, gqkv_ref, out_ref):
+def qkv_grad_kernel(_, normed_ref, gqkv_ref, att_ref, gmix_ref, out_ref):
     height = normed_ref.shape[1]
     for t in range(3):
         out_ref[height * t : height * (t + 1), :] = dot_tn(normed_ref[...], gqkv_ref[t]).astype(BF)
+    out_ref[3 * height :, :] = dot_tn(att_ref[...], gmix_ref[...]).astype(BF)
 
 
 def input_grad_kernel(deep, stride, gqkv_ref, x_ref, gain_ref, w_ref, out_ref, lon_ref, lat_ref, corner_ref,
@@ -486,7 +484,6 @@
 
     att_halos = exchange(grad_edges, 1)
     pieces = 4
-    rest = features // pieces
     odd = lax.rem(lax.axis_index("lon"), 2).astype(jnp.int32)
     mine, theirs = odd.reshape(1), (1 - odd).reshape(1)
 
@@ -497,16 +494,14 @@
                 num_scalar_prefetch=1,
                 grid=(pieces // 2,),
                 in_specs=[pl.BlockSpec((total // 4, features), lambda i, k: (0, 2 * k[0] + i)),
-                          pl.BlockSpec((total // 4, width2), lambda i, k: (0, 0)),
-                          pl.BlockSpec((total, features), lambda i, k: (0, 0)),
-                          pl.BlockSpec((total, rest), lambda i, k: (0, 2 * k[0] + i))],
-                out_specs=pl.BlockSpec((features, width2 + rest), lambda i, k: (i, 0)),
+                          pl.BlockSpec((total // 4, width2), lambda i, k: (0, 0))],
+                out_specs=pl.BlockSpec((features, width2), lambda i, k: (i, 0)),
             ),
-            out_shape=jax.ShapeDtypeStruct((pieces // 2 * features, width2 + rest), BF),
+            out_shape=jax.ShapeDtypeStruct((pieces // 2 * features, width2), BF),
             compiler_params=params(1),
             cost_estimate=cost(2 * total * features * features * 2, total * features * 6),
             name="merge_dw",
-        )(side, merged_in, gm, own_att, grad_mixed)
+        )(side, merged_in, gm)
 
     m_own, m_got = reduce_all(merge_dw(theirs), merge_dw(mine))
 
@@ -556,14 +551,16 @@
                 num_scalar_prefetch=1,
                 grid=(1,),
                 in_specs=[pl.BlockSpec((tall3, tile), lambda i, k: (0, k[0])),
-                          pl.BlockSpec((3, tall3, features), lambda i, k: (0, 0, 0))],
-                out_specs=pl.BlockSpec((3 * tile, features), lambda i, k: (0, 0)),
+                          pl.BlockSpec((3, tall3, features), lambda i, k: (0, 0, 0)),
+                          pl.BlockSpec((total, tile), lambda i, k: (0, k[0])),
+                          pl.BlockSpec((total, features), lambda i, k: (0, 0))],
+                out_specs=pl.BlockSpec((4 * tile, features), lambda i, k: (0, 0)),
             ),
-            out_shape=jax.ShapeDtypeStruct((3 * tile, features), BF),
+            out_shape=jax.ShapeDtypeStruct((4 * tile, features), BF),
             compiler_params=params(1),
             cost_estimate=cost(total * features * 3 * features, total * features * 5),
             name="qkv_dw",
-        )(side, normed, grad_qkv)
+        )(side, normed, grad_qkv, own_att, grad_mixed)
 
     q_own, q_got = reduce_all(qkv_dw(theirs), qkv_dw(mine))
 
@@ -601,16 +598,14 @@
             grid_spec=pltpu.PrefetchScalarGridSpec(
                 num_scalar_prefetch=1,
                 grid=(pieces // 2,),
-                in_specs=[pl.BlockSpec((features, width2 + rest), lambda i, k: (i, 0)),
+                in_specs=[pl.BlockSpec((features, width2), lambda i, k: (i, 0)),
                           pl.BlockSpec((features, width2), lambda i, k: (2 * k[0] + i, 0)),
                           pl.BlockSpec((1, features), lambda i, k: (0, 2 * k[0] + i))]
                 + [pl.BlockSpec(memory_space=pl.ANY)] * len(earlier),
                 out_specs=[pl.BlockSpec((features, width2), lambda i, k: (2 * k[0] + i, 0)),
-                           pl.BlockSpec((features, rest), lambda i, k: (0, 2 * k[0] + i)),
                            pl.BlockSpec((1, features), lambda i, k: (0, 2 * k[0] + i))],
             ),
             out_shape=[jax.ShapeDtypeStruct((pieces * features, width2), F32),
-                       jax.ShapeDtypeStruct((features, features), F32),
                        jax.ShapeDtypeStruct((1, pieces * features), F32)],
             input_output_aliases={4 + n: n for n in range(len(earlier))},
             compiler_params=params(1),
@@ -624,14 +619,16 @@
             grid_spec=pltpu.PrefetchScalarGridSpec(
                 num_scalar_prefetch=1,
                 grid=(1,),
-                in_specs=[pl.BlockSpec((3 * tile, features), lambda i, k: (0, 0)),
+                in_specs=[pl.BlockSpec((4 * tile, features), lambda i, k: (0, 0)),
                           pl.BlockSpec((tile, 3 * features), lambda i, k: (k[0], 0)),
                           pl.BlockSpec((1, tile), lambda i, k: (0, k[0]))]
                 + [pl.BlockSpec(memory_space=pl.ANY)] * len(earlier),
                 out_specs=[pl.BlockSpec((tile, 3 * features), lambda i, k: (k[0], 0)),
+                           pl.BlockSpec((tile, features), lambda i, k: (k[0], 0)),
                            pl.BlockSpec((1, tile), lambda i, k: (0, k[0]))],
             ),
             out_shape=[jax.ShapeDtypeStruct((features, 3 * features), F32),
+                       jax.ShapeDtypeStruct((features, features), F32),
                        jax.ShapeDtypeStruct((1, features), F32)],
             input_output_aliases={4 + n: n for n in range(len(earlier))},
             compiler_params=params(1),
@@ -639,9 +636,10 @@
             name="q_last",
         )(side, value, w_qkv, gain_a, *earlier)
 
-    grad_w_merge, grad_w_out, grad_gain_merge = finish_merge(
+    grad_w_merge, grad_gain_merge = finish_merge(
         theirs, m_got, finish_merge(mine, m_own))
-    grad_w_qkv, grad_gain_attn = finish_qkv(theirs, q_got, finish_qkv(mine, q_own))
+    grad_w_qkv, grad_w_out, grad_gain_attn = finish_qkv(
+        theirs, q_got, finish_qkv(mine, q_own))
     grad_gain_merge = grad_gain_merge.reshape(-1)
     grad_gain_attn = grad_gain_attn.reshape(-1)
     return (merged, grad_tokens, grad_gain_attn, grad_w_qkv, grad_w_out, grad_gain_merge,

time: 228 us -> 211 us (0.925)
  waiting for transfers between devices: 75 us -> 61.1 us
    ppermute x4, waiting for transfers between devices: 25.5 us -> 18 us  [reduce_all(): received = lax.ppermute(sent, 'lon', pairs)]
    ppermute x6, waiting for transfers between devices: 10.5 us -> 6.8 us  [reduce_all(): received = lax.ppermute(sent, 'lat', [(i, i ^ d) for i in range(count_lat)])]
    select_n x4, other arithmetic: 0.71 us -> 3.12 us  [join(): first = jnp.where(keep == 0, value, received)]
  transfers between devices with their start and end apart: 36 -> 36, of which waited for: 18 -> 15; matrix products, arithmetic and copies ran while one was open for 8% -> 10% of each run, Pallas kernels for 24% -> 26%
where the time goes in v3:
time: 211 us
  Pallas kernels  81.2 us (38%)
  waiting for transfers between devices  61.1 us (29%)
  starting transfers between devices  38.2 us (18%)
  other arithmetic  21.6 us (10%)
  local copies, waits for them, and re-layouts  7.46 us (4%)
    ppermute x4, waiting for transfers between devices, reduce_all(): received = lax.ppermute(sent, 'lon', pairs)  18 us
    ppermute x12, starting transfers between devices, send(): return lax.ppermute(value, ('lat', 'lon'), pairs)  15.2 us
    ppermute x4, waiting for transfers between devices, reduce_all(): received = lax.ppermute(value, 'lon', pairs)  13.9 us
    pallas_call x4, Pallas kernels, on_device_body(): pl.pallas_call(body, grid=(count_a // deep,), in_specs=specs, out_specs=s...  13 us
    ppermute x6, waiting for transfers between devices, reduce_all(): received = lax.ppermute(mine, 'lat', [(i, i ^ d) for i in range(count_lat)])  11.9 us
    pallas_call x1, Pallas kernels, on_device_body(): pl.pallas_call(functools.partial(forward_kernel, deep, stride, count_b),...  11.4 us
    pallas_call x2, Pallas kernels, qkv_dw(): pl.pallas_call(qkv_grad_kernel, grid_spec=pltpu.PrefetchScalarGridSpec(nu...  10.7 us
    convert_element_type x6, other arithmetic, part_sum(): return sum(parts[1:], parts[0]).astype(BF)  10.3 us
  transfers between devices with their start and end apart: 36, of which 15 were waited for; matrix products, arithmetic and copies ran while one was open for 10% of the time, Pallas kernels for 26%

profile of v3, /device:TPU:0, one launch (start us, length us, event | category | flops | bytes accessed | tf_op | source)
XLA Modules:
  0.0 210.6 jit_solution(5381843055869723505)
XLA Ops:
  1.4 2.5 %collective-permute-start.2 = (bf16[24,512]{1,0:T(8,128)(2,1)S(1)}, bf16[24,512]{1,0:T(8,128)(2,1)S(1)}, u32[]{:S(2)}, u32[]{:S(2)}) collective-permute-start(bf16[24,512]{1,0:T(8,128)(2,1)S(1)} %slice_bitcast_fusion.1), channel_id=1, source_target_pairs={{0,9},{1,10},{2,11},{3,12},{4,13},{5,14},{6,15},{7,8},{8,17},{9,18... | collective-permute-start | bytes 73736 | tf_op jit(solution)/shard_map/ppermute | solution.py:312
  3.9 0.9 slice.37
  4.8 1.6 collective-permute-start.1
  6.4 0.9 slice_bitcast_fusion
  7.4 1.4 collective-permute-start
  11.3 1.4 collective-permute-done.1.south_ref
  14.1 11.4 %attn_fwd.1 = (bf16[1152,512]{1,0:T(8,128)(2,1)}, bf16[3,1280,512]{2,1,0:T(8,128)(2,1)}, bf16[1280,512]{1,0:T(8,128)(2,1)}, bf16[1280,512]{1,0:T(8,128)(2,1)}, b...) custom-call(bf16[1152,512]{1,0:T(8,128)(2,1)} %bitcast.47, ...), custom_call_target="tpu_custom_call" | custom-call | flops 3623878656 | bytes 9437184 | tf_op jit(solution)/shard_map/attn_fwd/pallas_call | solution.py:434
  25.5 1.5 collective-permute-start.3
  27.8 1.5 collective-permute-start.5
  29.4 4.3 %grad_in.1.grad_in_ref = bf16[288,2048]{1,0:T(8,128)(2,1)} custom-call(bf16[288,1024]{1,0:T(8,128)(2,1)} %bitcast.37, bf16[2048,1024]{1,0:T(8,128)(2,1)} %w_ref.13), custom_call_target="tpu_custom_call" | custom-call | flops 1207959552 | bytes 4718592 | tf_op jit(solution)/shard_map/grad_in/pallas_call | solution.py:455
  34.2 1.2 maximum_maximum_fusion
  35.3 6.8 %merge_mid.1 = (bf16[288,2048]{1,0:T(8,128)(2,1)}, bf16[1152,512]{1,0:T(8,128)(2,1)}, bf16[1152,512]{1,0:T(8,128)(2,1)}, bf16[192,512]{1,0:T(8,128)(2,1)}, bf16[...) custom-call(bf16[1152,512]{1,0:T(8,128)(2,1)} %bitcast.48, bf16[1152,512]{1,0:T(8,128)(2,1)} %bitcast.31, ...), custom_call_target="tpu_custom_call" | custom-call | flops 2415919104 | bytes 7077888 | tf_op jit(solution)/shard_map/merge_mid/pallas_call | solution.py:469
  42.2 3.7 %merge_dw.3 = bf16[1024,1024]{1,0:T(8,128)(2,1)} custom-call(s32[1]{0:T(128)} %bitcast.22._, bf16[288,2048]{1,0:T(8,128)(2,1)} %get-tuple-element.39.a_ref.merged_in_ref, bf16[288,1024]{1,0:T(8,128)(2,1)} %bitcast.38), custom_call_target="tpu_custom_call" | custom-call | flops 1207959552 | bytes 3538944 | tf_op jit(solution)/shard_map/merge_dw/pallas_call | solution.py:491
  45.8 3.7 %merge_dw.2 = bf16[1024,1024]{1,0:T(8,128)(2,1)} custom-call(s32[1]{0:T(128)} %bitcast.23._, bf16[288,2048]{1,0:T(8,128)(2,1)} %get-tuple-element.39.a_ref.merged_in_ref, bf16[288,1024]{1,0:T(8,128)(2,1)} %bitcast.39), custom_call_target="tpu_custom_call" | custom-call | flops 1207959552 | bytes 3538944 | tf_op jit(solution)/shard_map/merge_dw/pallas_call | solution.py:491
  50.2 3.3 %add_convert_fusion = bf16[512,1024]{1,0:T(8,128)(2,1)} fusion(bf16[1024,1024]{1,0:T(8,128)(2,1)S(1)} %collective-permute-done.24, s32[]{:T(128)S(6)} %select_n.176, bf16[1024,1024]{1,0:T(8,128)(2,1)} %merge_dw.2), kind=kLoop, calls=%fused_computation.2 | loop fusion | flops 2097152 | bytes 3145732 | tf_op jit(solution)/shard_map/convert_element_type | solution.py:342
  54.4 1.0 collective-permute-start.7
  55.4 1.4 collective-permute-start.8
  56.8 7.6 %collective-permute-done.8 = bf16[24,512]{1,0:T(8,128)(2,1)S(1)} collective-permute-done((bf16[24,512]{1,0:T(8,128)(2,1)S(1)}, bf16[24,512]{1,0:T(8,128)(2,1)S(1)}, u32[]{:S(2)}, u32[]{:S(2)}) %collective-permute-start.8) | collective-permute-done | bytes 24608 | tf_op jit(solution)/shard_map/ppermute | solution.py:312
  65.1 3.1 %assemble.1.ga_ref = bf16[1280,512]{1,0:T(8,128)(2,1)} custom-call(bf16[1152,512]{1,0:T(8,128)(2,1)} %get-tuple-element.40.own_ref, bf16[24,8,512]{2,1,0:T(8,128)(2,1)} %bitcast.41, bf16[144,512]{1,0:T(8,128)(2,1)} %copy-done.9, bf16[3,8,512]{2,1,0:T(8,128)(2,1)} %bitcast.54), custom_call_target="tpu_custom_call" | custom-call | flops 707788800 | bytes 3538944 | tf_op jit(solution)/shard_map/assemble/pallas_call | solution.py:508
  68.2 3.3 %shard_map.153.prev_ref = bf16[3,1280,512]{2,1,0:T(8,128)(2,1)} custom-call(bf16[1280,512]{1,0:T(8,128)(2,1)} %assemble.1.ga_ref, bf16[3,1280,512]{2,1,0:T(8,128)(2,1)} %get-tuple-element.44.qkv_ref, bf16[4,2560,80]{2,1,0:T(8,128)(2,1)} %get-tuple-element.45.prob_ref), custom_call_target="tpu_custom_call" | custom-call | flops 905969664 | bytes 2359296 | tf_op jit(solution)/shard_map/pallas_call | solution.py:534
  71.5 3.2 %shard_map.154.prev_ref = bf16[3,1280,512]{2,1,0:T(8,128)(2,1)} custom-call(bf16[1280,512]{1,0:T(8,128)(2,1)} %assemble.1.ga_ref, bf16[3,1280,512]{2,1,0:T(8,128)(2,1)} %get-tuple-element.44.qkv_ref, bf16[4,2560,80]{2,1,0:T(8,128)(2,1)} %get-tuple-element.45.prob_ref, bf16[3,1280,512]{2,1,0:T(8,128)(2,1)} %shard_map.153.prev_ref), custom_call_target="tpu_custom_call", output_to_operand_aliasing={{}: (3, {})} | custom-call | flops 905969664 | bytes 2359296 | tf_op jit(solution)/shard_map/pallas_call | solution.py:534
  74.7 3.3 %shard_map.155.prev_ref = bf16[3,1280,512]{2,1,0:T(8,128)(2,1)} custom-call(bf16[1280,512]{1,0:T(8,128)(2,1)} %assemble.1.ga_ref, bf16[3,1280,512]{2,1,0:T(8,128)(2,1)} %get-tuple-element.44.qkv_ref, bf16[4,2560,80]{2,1,0:T(8,128)(2,1)} %get-tuple-element.45.prob_ref, bf16[3,1280,512]{2,1,0:T(8,128)(2,1)} %shard_map.154.prev_ref), custom_call_target="tpu_custom_call", output_to_operand_aliasing={{}: (3, {})} | custom-call | flops 905969664 | bytes 2359296 | tf_op jit(solution)/shard_map/pallas_call | solution.py:534
  78.0 3.3 %shard_map.156.gqkv_ref = bf16[3,1280,512]{2,1,0:T(8,128)(2,1)} custom-call(bf16[1280,512]{1,0:T(8,128)(2,1)} %assemble.1.ga_ref, bf16[3,1280,512]{2,1,0:T(8,128)(2,1)} %get-tuple-element.44.qkv_ref, bf16[4,2560,80]{2,1,0:T(8,128)(2,1)} %get-tuple-element.45.prob_ref, bf16[3,1280,512]{2,1,0:T(8,128)(2,1)} %shard_map.155.prev_ref), custom_call_target="tpu_custom_call", output_to_operand_aliasing={{}: (3, {})} | custom-call | flops 905969664 | bytes 2359296 | tf_op jit(solution)/shard_map/pallas_call | solution.py:534
  81.2 5.3 %qkv_dw.3 = bf16[1024,512]{1,0:T(8,128)(2,1)} custom-call(s32[1]{0:T(128)} %bitcast.22._, bf16[1280,512]{1,0:T(8,128)(2,1)} %get-tuple-element.52.normed_ref, bf16[3,1280,512]{2,1,0:T(8,128)(2,1)} %shard_map.156.gqkv_ref, bf16[1152,512]{1,0:T(8,128)(2,1)} %bitcast.32, bf16[1152,512]{1,0:T(8,128)(2,1)} %get-tuple-element.51.gmix_ref), custom_call_target="tpu_custom_call" | custom-call | flops 905969664 | bytes 2949120 | tf_op jit(solution)/shard_map/qkv_dw/pallas_call | solution.py:548
  86.6 2.3 %add_convert_fusion.1 = bf16[256,1024]{1,0:T(8,128)(2,1)} fusion(bf16[512,1024]{1,0:T(8,128)(2,1)} %collective-permute-done.25, s32[]{:T(128)S(6)} %select_n.177, bf16[1024,1024]{1,0:T(8,128)(2,1)S(1)} %collective-permute-done.24, s32[]{:T(128)S(6)} %dynamic_slice.199, bf16[1024,1024]{1,0:T(8,128)(2,1)} %merge_dw.2), kind=kLoop, calls=%fused_computation.6 | loop fusion | flops 1572864 | bytes 2097160 | tf_op jit(solution)/shard_map/convert_element_type | solution.py:342
  88.9 1.3 collective-permute-start.26
  90.2 8.2 %collective-permute-done.26 = bf16[256,1024]{1,0:T(8,128)(2,1)} collective-permute-done((bf16[256,1024]{1,0:T(8,128)(2,1)}, bf16[256,1024]{1,0:T(8,128)(2,1)}, u32[]{:S(2)}, u32[]{:S(2)}) %collective-permute-start.26) | collective-permute-done | bytes 524320 | tf_op jit(solution)/shard_map/ppermute | solution.py:368
  98.4 1.7 add_convert_fusion.7
  100.2 1.9 collective-permute-start.29
  102.1 1.6 collective-permute-start.28
  103.7 5.3 %qkv_dw.2 = bf16[1024,512]{1,0:T(8,128)(2,1)} custom-call(s32[1]{0:T(128)} %bitcast.23._, bf16[1280,512]{1,0:T(8,128)(2,1)} %get-tuple-element.52.normed_ref, bf16[3,1280,512]{2,1,0:T(8,128)(2,1)} %shard_map.156.gqkv_ref, bf16[1152,512]{1,0:T(8,128)(2,1)} %bitcast.33, bf16[1152,512]{1,0:T(8,128)(2,1)} %get-tuple-element.51.gmix_ref), custom_call_target="tpu_custom_call" | custom-call | flops 905969664 | bytes 2949120 | tf_op jit(solution)/shard_map/qkv_dw/pallas_call | solution.py:548
  109.1 1.6 add_convert_fusion.2
  111.3 3.6 %collective-permute-done.28 = bf16[64,1024]{1,0:T(8,128)(2,1)S(1)} collective-permute-done((bf16[64,1024]{1,0:T(8,128)(2,1)S(1)}, bf16[64,1024]{1,0:T(8,128)(2,1)S(1)}, u32[]{:S(2)}, u32[]{:S(2)}) %collective-permute-start.28) | collective-permute-done | bytes 131104 | tf_op jit(solution)/shard_map/ppermute | solution.py:374
  114.9 1.3 constant_dynamic-update-slice_fusion.3
  116.3 2.3 %collective-permute-start.31 = (bf16[64,1024]{1,0:T(8,128)(2,1)S(1)}, bf16[64,1024]{1,0:T(8,128)(2,1)S(1)}, u32[]{:S(2)}, u32[]{:S(2)}) collective-permute-start(bf16[64,1024]{1,0:T(8,128)(2,1)S(1)} %get-tuple-element.64), channel_id=1, source_target_pairs={{0,16},{8,24},{16,0},{24,8},{1,17},{9,25},{17,1},{25,9},{2,18},{10... | collective-permute-start | bytes 393224 | tf_op jit(solution)/shard_map/ppermute | solution.py:380
  118.7 2.0 collective-permute-start.32
  120.7 1.8 collective-permute-done.30
  122.5 6.3 %collective-permute-done.31 = bf16[64,1024]{1,0:T(8,128)(2,1)S(1)} collective-permute-done((bf16[64,1024]{1,0:T(8,128)(2,1)S(1)}, bf16[64,1024]{1,0:T(8,128)(2,1)S(1)}, u32[]{:S(2)}, u32[]{:S(2)}) %collective-permute-start.31) | collective-permute-done | bytes 131104 | tf_op jit(solution)/shard_map/ppermute | solution.py:380
  128.8 1.5 collective-permute-start.33
  131.1 9.8 %collective-permute-done.14 = bf16[256,512]{1,0:T(8,128)(2,1)} collective-permute-done((bf16[256,512]{1,0:T(8,128)(2,1)S(1)}, bf16[256,512]{1,0:T(8,128)(2,1)}, u32[]{:S(2)}, u32[]{:S(2)}) %collective-permute-start.14) | collective-permute-done | bytes 262176 | tf_op jit(solution)/shard_map/ppermute | solution.py:368
  140.9 1.1 add_convert_fusion.11
  142.0 2.0 collective-permute-start.15
  144.0 1.7 collective-permute-start.17
  145.7 1.1 broadcast_select_fusion.3
  146.9 1.0 pad_maximum_fusion.2
  148.3 1.8 collective-permute-done.17
  150.1 1.4 collective-permute-done.16
  151.5 1.1 constant_dynamic-update-slice_fusion
  152.7 2.2 %collective-permute-start.19 = (bf16[64,512]{1,0:T(8,128)(2,1)S(1)}, bf16[64,512]{1,0:T(8,128)(2,1)S(1)}, u32[]{:S(2)}, u32[]{:S(2)}) collective-permute-start(bf16[64,512]{1,0:T(8,128)(2,1)S(1)} %get-tuple-element.66), channel_id=1, source_target_pairs={{0,16},{8,24},{16,0},{24,8},{1,17},{9,25},{17,1},{25,9},{2,18},{10... | collective-permute-start | bytes 196616 | tf_op jit(solution)/shard_map/ppermute | solution.py:380
  154.9 2.1 %collective-permute-start.20 = (bf16[64,512]{1,0:T(8,128)(2,1)S(1)}, bf16[64,512]{1,0:T(8,128)(2,1)S(1)}, u32[]{:S(2)}, u32[]{:S(2)}) collective-permute-start(bf16[64,512]{1,0:T(8,128)(2,1)S(1)} %get-tuple-element.66), channel_id=1, source_target_pairs={{0,24},{8,16},{16,8},{24,0},{1,25},{9,17},{17,9},{25,1},{2,26},{10... | collective-permute-start | bytes 196616 | tf_op jit(solution)/shard_map/ppermute | solution.py:380
  157.9 3.1 %collective-permute-done.20 = bf16[64,512]{1,0:T(8,128)(2,1)S(1)} collective-permute-done((bf16[64,512]{1,0:T(8,128)(2,1)S(1)}, bf16[64,512]{1,0:T(8,128)(2,1)S(1)}, u32[]{:S(2)}, u32[]{:S(2)}) %collective-permute-start.20) | collective-permute-done | bytes 65568 | tf_op jit(solution)/shard_map/ppermute | solution.py:380
  161.0 1.3 collective-permute-start.21
  162.3 5.1 %collective-permute-done.21 = bf16[256,512]{1,0:T(8,128)(2,1)S(1)} collective-permute-done((bf16[256,512]{1,0:T(8,128)(2,1)S(1)}, bf16[256,512]{1,0:T(8,128)(2,1)S(1)}, u32[]{:S(2)}, u32[]{:S(2)}) %collective-permute-start.21) | collective-permute-done | bytes 262176 | tf_op jit(solution)/shard_map/ppermute | solution.py:383
  167.5 1.8 broadcast_select_fusion.1
  170.0 8.8 %collective-permute-done.22 = bf16[512,512]{1,0:T(8,128)(2,1)S(1)} collective-permute-done((bf16[512,512]{1,0:T(8,128)(2,1)S(1)}, bf16[512,512]{1,0:T(8,128)(2,1)S(1)}, u32[]{:S(2)}, u32[]{:S(2)}) %collective-permute-start.22) | collective-permute-done | bytes 524320 | tf_op jit(solution)/shard_map/ppermute | solution.py:383
  179.2 6.8 %input_grad.1 = (bf16[1152,512]{1,0:T(8,128)(2,1)}, bf16[192,512]{1,0:T(8,128)(2,1)}, bf16[144,512]{1,0:T(8,128)(2,1)}, bf16[24,512]{1,0:T(8,128)(2,1)}) custom-call(bf16[3,1280,512]{2,1,0:T(8,128)(2,1)} %shard_map.156.gqkv_ref, bf16[1280,512]{1,0:T(8,128)(2,1)} %get-tuple-element.46.x_ref, f32[1,512]{1,0:T(1,128)} %bitcast.56, bf16[512,1536]{1,0:T(8,128)(2,1)} %w_ref.11), custom_call_target="tpu_custom_call" | custom-call | flops 1811939328 | bytes 7077888 | tf_op jit(solution)/shard_map/input_grad/pallas_call | solution.py:567
  186.8 2.3 %collective-permute-start.10 = (bf16[144,512]{1,0:T(8,128)(2,1)}, bf16[144,512]{1,0:T(8,128)(2,1)S(1)}, u32[]{:S(2)}, u32[]{:S(2)}) collective-permute-start(bf16[144,512]{1,0:T(8,128)(2,1)} %get-tuple-element.49), channel_id=1, source_target_pairs={{0,24},{1,25},{2,26},{3,27},{4,28},{5,29},{6,30},{7,31},{8,0},{9,1... | collective-permute-start | bytes 442376 | tf_op jit(solution)/shard_map/ppermute | solution.py:312
  189.1 4.2 %merged.1 = bf16[288,1024]{1,0:T(8,128)(2,1)} custom-call(bf16[288,2048]{1,0:T(8,128)(2,1)} %get-tuple-element.39.a_ref.merged_in_ref, bf16[2048,1024]{1,0:T(8,128)(2,1)} %w_ref.13), custom_call_target="tpu_custom_call" | custom-call | flops 1207959552 | bytes 4718592 | tf_op jit(solution)/shard_map/merged/pallas_call | solution.py:583
  193.2 1.7 slice.52
  195.1 1.9 convert_add_fusion
  197.0 3.0 %q_last.2 = (f32[512,1536]{1,0:T(8,128)}, f32[512,512]{1,0:T(8,128)}, f32[1,512]{1,0:T(1,128)}) custom-call(s32[1]{0:T(128)} %bitcast.23._, bf16[1024,512]{1,0:T(8,128)(2,1)} %copy-done.3, bf16[512,1536]{1,0:T(8,128)(2,1)} %w_ref.11, f32[1,512]{1,0:T(1,128)} %bitcast.57), custom_call_target="tpu_custom_call" | custom-call | flops 294912000 | bytes 1769472 | tf_op jit(solution)/shard_map/q_last/pallas_call | solution.py:617
  200.0 3.0 %q_last.3 = (f32[512,1536]{1,0:T(8,128)}, f32[512,512]{1,0:T(8,128)}, f32[1,512]{1,0:T(1,128)}) custom-call(s32[1]{0:T(128)} %bitcast.22._, bf16[1024,512]{1,0:T(8,128)(2,1)} %collective-permute-done.23.value_ref, bf16[512,1536]{1,0:T(8,128)(2,1)} %w_ref.11, f32[1,512]{1,0:T(1,128)} %bitcast.58, ...), custom_call_target="tpu_custom_call", output_to_operand_aliasing={{0}: (4, {}), {1}: (5, {}), {2}: (6, {})} | custom-call | flops 294912000 | bytes 1769472 | tf_op jit(solution)/shard_map/q_last/pallas_call | solution.py:617
  202.9 3.8 %m_last.2 = (f32[2048,1024]{1,0:T(8,128)}, f32[1,2048]{1,0:T(1,128)}) custom-call(s32[1]{0:T(128)} %bitcast.23._, bf16[1024,1024]{1,0:T(8,128)(2,1)} %copy-done.1, bf16[2048,1024]{1,0:T(8,128)(2,1)} %w_ref.13, f32[1,2048]{1,0:T(1,128)} %bitcast.50), custom_call_target="tpu_custom_call" | custom-call | flops 589824000 | bytes 3538944 | tf_op jit(solution)/shard_map/m_last/pallas_call | solution.py:596
  206.8 3.8 %m_last.3 = (f32[2048,1024]{1,0:T(8,128)}, f32[1,2048]{1,0:T(1,128)}) custom-call(s32[1]{0:T(128)} %bitcast.22._, bf16[1024,1024]{1,0:T(8,128)(2,1)} %collective-permute-done.35.value_ref, bf16[2048,1024]{1,0:T(8,128)(2,1)} %w_ref.13, f32[1,2048]{1,0:T(1,128)} %bitcast.51, ...), custom_call_target="tpu_custom_call", output_to_operand_aliasing={{0}: (4, {}), {1}: (5, {})} | custom-call | flops 589824000 | bytes 3538944 | tf_op jit(solution)/shard_map/m_last/pallas_call | solution.py:596
  (103 shorter events, 13.4 us)
Async XLA Ops:
  1.4 9.9 %collective-permute-start.2 = (bf16[24,512]{1,0:T(8,128)(2,1)S(1)}, bf16[24,512]{1,0:T(8,128)(2,1)S(1)}, u32[]{:S(2)}, u32[]{:S(2)}) collective-permute-start(bf16[24,512]{1,0:T(8,128)(2,1)S(1)} %slice_bitcast_fusion.1), channel_id=1, source_target_pairs={{0,9},{1,10},{2,11},{3,12},{4,13},{5,14},{6,15},{7,8},{8,17},{9,18... | collective-permute-start | bytes 73736 | tf_op jit(solution)/shard_map/ppermute | solution.py:312
  4.8 7.9 %collective-permute-start.1 = (bf16[144,512]{1,0:T(8,128)(2,1)S(1)}, bf16[144,512]{1,0:T(8,128)(2,1)S(1)}, u32[]{:S(2)}, u32[]{:S(2)}) collective-permute-start(bf16[144,512]{1,0:T(8,128)(2,1)S(1)} %bitcast.44), channel_id=1, source_target_pairs={{0,8},{1,9},{2,10},{3,11},{4,12},{5,13},{6,14},{7,15},{8,16},{9,17... | collective-permute-start | bytes 442376 | tf_op jit(solution)/shard_map/ppermute | solution.py:312
  7.4 6.0 %collective-permute-start = (bf16[192,512]{1,0:T(8,128)(2,1)S(1)}, bf16[192,512]{1,0:T(8,128)(2,1)S(1)}, u32[]{:S(2)}, u32[]{:S(2)}) collective-permute-start(bf16[192,512]{1,0:T(8,128)(2,1)S(1)} %slice_bitcast_fusion), channel_id=1, source_target_pairs={{0,1},{1,2},{2,3},{3,4},{4,5},{5,6},{6,7},{7,0},{8,9},{9,10},{10,1... | collective-permute-start | bytes 589832 | tf_op jit(solution)/shard_map/ppermute | solution.py:312
  11.3 2.1 %copy-start.16 = (bf16[24,512]{1,0:T(8,128)(2,1)}, bf16[24,512]{1,0:T(8,128)(2,1)S(1)}, u32[]{:S(2)}) copy-start(bf16[24,512]{1,0:T(8,128)(2,1)S(1)} %collective-permute-done.2) | copy-start | bytes 73732
  12.7 0.7 copy-start.14
  13.4 0.7 copy-start.12
  25.5 8.7 %collective-permute-start.3 = (bf16[192,512]{1,0:T(8,128)(2,1)}, bf16[192,512]{1,0:T(8,128)(2,1)S(1)}, u32[]{:S(2)}, u32[]{:S(2)}) collective-permute-start(bf16[192,512]{1,0:T(8,128)(2,1)} %get-tuple-element.36), channel_id=1, source_target_pairs={{0,7},{1,0},{2,1},{3,2},{4,3},{5,4},{6,5},{7,6},{8,15},{9,8},{10,9... | collective-permute-start | bytes 589832 | tf_op jit(solution)/shard_map/ppermute | solution.py:312
  26.9 7.2 %collective-permute-start.4 = (bf16[144,512]{1,0:T(8,128)(2,1)}, bf16[144,512]{1,0:T(8,128)(2,1)S(1)}, u32[]{:S(2)}, u32[]{:S(2)}) collective-permute-start(bf16[144,512]{1,0:T(8,128)(2,1)} %get-tuple-element.37), channel_id=1, source_target_pairs={{0,24},{1,25},{2,26},{3,27},{4,28},{5,29},{6,30},{7,31},{8,0},{9,1... | collective-permute-start | bytes 442376 | tf_op jit(solution)/shard_map/ppermute | solution.py:312
  27.8 6.3 %collective-permute-start.5 = (bf16[24,512]{1,0:T(8,128)(2,1)}, bf16[24,512]{1,0:T(8,128)(2,1)S(1)}, u32[]{:S(2)}, u32[]{:S(2)}) collective-permute-start(bf16[24,512]{1,0:T(8,128)(2,1)} %get-tuple-element.38), channel_id=1, source_target_pairs={{0,31},{1,24},{2,25},{3,26},{4,27},{5,28},{6,29},{7,30},{8,7},{9,0... | collective-permute-start | bytes 73736 | tf_op jit(solution)/shard_map/ppermute | solution.py:312
  29.4 4.3 %copy-start.6 = (bf16[1152,512]{1,0:T(8,128)(2,1)S(1)}, bf16[1152,512]{1,0:T(8,128)(2,1)}, u32[]{:S(2)}) copy-start(bf16[1152,512]{1,0:T(8,128)(2,1)} %get-tuple-element.35) | copy-start | bytes 3538948
  45.8 4.4 %collective-permute-start.24 = (bf16[1024,1024]{1,0:T(8,128)(2,1)}, bf16[1024,1024]{1,0:T(8,128)(2,1)S(1)}, u32[]{:S(2)}, u32[]{:S(2)}) collective-permute-start(bf16[1024,1024]{1,0:T(8,128)(2,1)} %merge_dw.3), channel_id=1, source_target_pairs={{0,1},{1,0},{2,3},{3,2},{4,5},{5,4},{6,7},{7,6},{8,9},{9,8},{10,11... | collective-permute-start | bytes 6291464 | tf_op jit(solution)/shard_map/ppermute | solution.py:363
  49.5 4.5 %copy-start.11 = (bf16[192,512]{1,0:T(8,128)(2,1)S(1)}, bf16[192,512]{1,0:T(8,128)(2,1)}, u32[]{:S(2)}) copy-start(bf16[192,512]{1,0:T(8,128)(2,1)} %get-tuple-element.41) | copy-start | bytes 589828
  49.5 4.9 %copy-start.13 = (bf16[144,512]{1,0:T(8,128)(2,1)S(1)}, bf16[144,512]{1,0:T(8,128)(2,1)}, u32[]{:S(2)}) copy-start(bf16[144,512]{1,0:T(8,128)(2,1)} %get-tuple-element.42) | copy-start | bytes 442372
  49.5 5.9 %copy-start.15 = (bf16[24,512]{1,0:T(8,128)(2,1)S(1)}, bf16[24,512]{1,0:T(8,128)(2,1)}, u32[]{:S(2)}) copy-start(bf16[24,512]{1,0:T(8,128)(2,1)} %get-tuple-element.43) | copy-start | bytes 73732
  50.2 48.2 %copy-start.4 = (bf16[1024,1024]{1,0:T(8,128)(2,1)}, bf16[1024,1024]{1,0:T(8,128)(2,1)S(1)}, u32[]{:S(2)}) copy-start(bf16[1024,1024]{1,0:T(8,128)(2,1)S(1)} %collective-permute-done.24) | copy-start | bytes 6291460
  53.5 33.0 %collective-permute-start.25 = (bf16[512,1024]{1,0:T(8,128)(2,1)}, bf16[512,1024]{1,0:T(8,128)(2,1)}, u32[]{:S(2)}, u32[]{:S(2)}) collective-permute-start(bf16[512,1024]{1,0:T(8,128)(2,1)} %add_convert_fusion), channel_id=1, source_target_pairs={{0,2},{1,5},{2,0},{3,7},{4,6},{5,1},{6,4},{7,3},{8,10},{9,13},{10,... | collective-permute-start | bytes 3145736 | tf_op jit(solution)/shard_map/ppermute | solution.py:368
  54.0 10.4 %collective-permute-start.6 = (bf16[192,512]{1,0:T(8,128)(2,1)S(1)}, bf16[192,512]{1,0:T(8,128)(2,1)S(1)}, u32[]{:S(2)}, u32[]{:S(2)}) collective-permute-start(bf16[192,512]{1,0:T(8,128)(2,1)S(1)} %copy-done.11), channel_id=1, source_target_pairs={{0,1},{1,2},{2,3},{3,4},{4,5},{5,6},{6,7},{7,0},{8,9},{9,10},{10,1... | collective-permute-start | bytes 589832 | tf_op jit(solution)/shard_map/ppermute | solution.py:312
  54.4 10.0 %collective-permute-start.7 = (bf16[144,512]{1,0:T(8,128)(2,1)S(1)}, bf16[144,512]{1,0:T(8,128)(2,1)S(1)}, u32[]{:S(2)}, u32[]{:S(2)}) collective-permute-start(bf16[144,512]{1,0:T(8,128)(2,1)S(1)} %copy-done.13), channel_id=1, source_target_pairs={{0,8},{1,9},{2,10},{3,11},{4,12},{5,13},{6,14},{7,15},{8,16},{9,17... | collective-permute-start | bytes 442376 | tf_op jit(solution)/shard_map/ppermute | solution.py:312
  55.4 9.0 %collective-permute-start.8 = (bf16[24,512]{1,0:T(8,128)(2,1)S(1)}, bf16[24,512]{1,0:T(8,128)(2,1)S(1)}, u32[]{:S(2)}, u32[]{:S(2)}) collective-permute-start(bf16[24,512]{1,0:T(8,128)(2,1)S(1)} %copy-done.15), channel_id=1, source_target_pairs={{0,9},{1,10},{2,11},{3,12},{4,13},{5,14},{6,15},{7,8},{8,17},{9,18... | collective-permute-start | bytes 73736 | tf_op jit(solution)/shard_map/ppermute | solution.py:312
  64.4 0.6 copy-start.10
  64.4 0.7 copy-start.9
  64.4 0.7 copy-start.8
  86.6 22.5 %collective-permute-start.12 = (bf16[1024,512]{1,0:T(8,128)(2,1)}, bf16[1024,512]{1,0:T(8,128)(2,1)S(1)}, u32[]{:S(2)}, u32[]{:S(2)}) collective-permute-start(bf16[1024,512]{1,0:T(8,128)(2,1)} %qkv_dw.3), channel_id=1, source_target_pairs={{0,1},{1,0},{2,3},{3,2},{4,5},{5,4},{6,7},{7,6},{8,9},{9,8},{10,11... | collective-permute-start | bytes 3145736 | tf_op jit(solution)/shard_map/ppermute | solution.py:363
  88.9 9.5 %collective-permute-start.26 = (bf16[256,1024]{1,0:T(8,128)(2,1)}, bf16[256,1024]{1,0:T(8,128)(2,1)}, u32[]{:S(2)}, u32[]{:S(2)}) collective-permute-start(bf16[256,1024]{1,0:T(8,128)(2,1)} %add_convert_fusion.1), channel_id=1, source_target_pairs={{0,4},{1,3},{2,6},{3,1},{4,0},{5,7},{6,2},{7,5},{8,12},{9,11},{10,... | collective-permute-start | bytes 1572872 | tf_op jit(solution)/shard_map/ppermute | solution.py:368
  100.1 11.1 %collective-permute-start.27 = (bf16[64,1024]{1,0:T(8,128)(2,1)S(1)}, bf16[64,1024]{1,0:T(8,128)(2,1)S(1)}, u32[]{:S(2)}, u32[]{:S(2)}) collective-permute-start(bf16[64,1024]{1,0:T(8,128)(2,1)S(1)} %get-tuple-element.67), channel_id=1, source_target_pairs={{0,8},{8,0},{16,24},{24,16},{1,9},{9,1},{17,25},{25,17},{2,10},{10... | collective-permute-start | bytes 393224 | tf_op jit(solution)/shard_map/ppermute | solution.py:374
  100.2 11.1 %collective-permute-start.29 = (bf16[64,1024]{1,0:T(8,128)(2,1)S(1)}, bf16[64,1024]{1,0:T(8,128)(2,1)S(1)}, u32[]{:S(2)}, u32[]{:S(2)}) collective-permute-start(bf16[64,1024]{1,0:T(8,128)(2,1)S(1)} %get-tuple-element.68), channel_id=1, source_target_pairs={{0,24},{8,16},{16,8},{24,0},{1,25},{9,17},{17,9},{25,1},{2,26},{10... | collective-permute-start | bytes 393224 | tf_op jit(solution)/shard_map/ppermute | solution.py:374
  102.1 12.8 %collective-permute-start.28 = (bf16[64,1024]{1,0:T(8,128)(2,1)S(1)}, bf16[64,1024]{1,0:T(8,128)(2,1)S(1)}, u32[]{:S(2)}, u32[]{:S(2)}) collective-permute-start(bf16[64,1024]{1,0:T(8,128)(2,1)S(1)} %get-tuple-element.69), channel_id=1, source_target_pairs={{0,16},{8,24},{16,0},{24,8},{1,17},{9,25},{17,1},{25,9},{2,18},{10... | collective-permute-start | bytes 393224 | tf_op jit(solution)/shard_map/ppermute | solution.py:374
  109.0 21.2 %copy-start.2 = (bf16[1024,512]{1,0:T(8,128)(2,1)S(1)}, bf16[1024,512]{1,0:T(8,128)(2,1)}, u32[]{:S(2)}) copy-start(bf16[1024,512]{1,0:T(8,128)(2,1)} %qkv_dw.2) | copy-start | bytes 3145732
  109.1 31.9 %copy-start.5 = (bf16[1024,512]{1,0:T(8,128)(2,1)}, bf16[1024,512]{1,0:T(8,128)(2,1)S(1)}, u32[]{:S(2)}) copy-start(bf16[1024,512]{1,0:T(8,128)(2,1)S(1)} %collective-permute-done.12) | copy-start | bytes 3145732
  110.7 19.6 %collective-permute-start.13 = (bf16[512,512]{1,0:T(8,128)(2,1)S(1)}, bf16[512,512]{1,0:T(8,128)(2,1)S(1)}, u32[]{:S(2)}, u32[]{:S(2)}) collective-permute-start(bf16[512,512]{1,0:T(8,128)(2,1)S(1)} %add_convert_fusion.2), channel_id=1, source_target_pairs={{0,2},{1,5},{2,0},{3,7},{4,6},{5,1},{6,4},{7,3},{8,10},{9,13},{10,... | collective-permute-start | bytes 1572872 | tf_op jit(solution)/shard_map/ppermute | solution.py:368
  116.2 6.2 %collective-permute-start.30 = (bf16[64,1024]{1,0:T(8,128)(2,1)S(1)}, bf16[64,1024]{1,0:T(8,128)(2,1)S(1)}, u32[]{:S(2)}, u32[]{:S(2)}) collective-permute-start(bf16[64,1024]{1,0:T(8,128)(2,1)S(1)} %get-tuple-element.64), channel_id=1, source_target_pairs={{0,8},{8,0},{16,24},{24,16},{1,9},{9,1},{17,25},{25,17},{2,10},{10... | collective-permute-start | bytes 393224 | tf_op jit(solution)/shard_map/ppermute | solution.py:380
  116.3 12.4 %collective-permute-start.31 = (bf16[64,1024]{1,0:T(8,128)(2,1)S(1)}, bf16[64,1024]{1,0:T(8,128)(2,1)S(1)}, u32[]{:S(2)}, u32[]{:S(2)}) collective-permute-start(bf16[64,1024]{1,0:T(8,128)(2,1)S(1)} %get-tuple-element.64), channel_id=1, source_target_pairs={{0,16},{8,24},{16,0},{24,8},{1,17},{9,25},{17,1},{25,9},{2,18},{10... | collective-permute-start | bytes 393224 | tf_op jit(solution)/shard_map/ppermute | solution.py:380
  118.7 10.1 %collective-permute-start.32 = (bf16[64,1024]{1,0:T(8,128)(2,1)S(1)}, bf16[64,1024]{1,0:T(8,128)(2,1)S(1)}, u32[]{:S(2)}, u32[]{:S(2)}) collective-permute-start(bf16[64,1024]{1,0:T(8,128)(2,1)S(1)} %get-tuple-element.64), channel_id=1, source_target_pairs={{0,24},{8,16},{16,8},{24,0},{1,25},{9,17},{17,9},{25,1},{2,26},{10... | collective-permute-start | bytes 393224 | tf_op jit(solution)/shard_map/ppermute | solution.py:380
  128.8 16.9 %collective-permute-start.33 = (bf16[256,1024]{1,0:T(8,128)(2,1)S(1)}, bf16[256,1024]{1,0:T(8,128)(2,1)}, u32[]{:S(2)}, u32[]{:S(2)}) collective-permute-start(bf16[256,1024]{1,0:T(8,128)(2,1)S(1)} %constant_dynamic-update-slice_fusion.1), channel_id=1, source_target_pairs={{0,4},{1,3},{2,6},{3,1},{4,0},{5,7},{6,2},{7,5},{8,12},{9,11},{10,... | collective-permute-start | bytes 1572872 | tf_op jit(solution)/shard_map/ppermute | solution.py:383
  130.3 15.4 %copy-start.7 = (bf16[512,512]{1,0:T(8,128)(2,1)}, bf16[512,512]{1,0:T(8,128)(2,1)S(1)}, u32[]{:S(2)}) copy-start(bf16[512,512]{1,0:T(8,128)(2,1)S(1)} %collective-permute-done.13) | copy-start | bytes 1572868
  130.5 10.5 %collective-permute-start.14 = (bf16[256,512]{1,0:T(8,128)(2,1)S(1)}, bf16[256,512]{1,0:T(8,128)(2,1)}, u32[]{:S(2)}, u32[]{:S(2)}) collective-permute-start(bf16[256,512]{1,0:T(8,128)(2,1)S(1)} %add_convert_fusion.3), channel_id=1, source_target_pairs={{0,4},{1,3},{2,6},{3,1},{4,0},{5,7},{6,2},{7,5},{8,12},{9,11},{10,... | collective-permute-start | bytes 786440 | tf_op jit(solution)/shard_map/ppermute | solution.py:368
  142.0 6.3 %collective-permute-start.15 = (bf16[64,512]{1,0:T(8,128)(2,1)S(1)}, bf16[64,512]{1,0:T(8,128)(2,1)S(1)}, u32[]{:S(2)}, u32[]{:S(2)}) collective-permute-start(bf16[64,512]{1,0:T(8,128)(2,1)S(1)} %get-tuple-element.70), channel_id=1, source_target_pairs={{0,8},{8,0},{16,24},{24,16},{1,9},{9,1},{17,25},{25,17},{2,10},{10... | collective-permute-start | bytes 196616 | tf_op jit(solution)/shard_map/ppermute | solution.py:374
  144.0 6.1 %collective-permute-start.17 = (bf16[64,512]{1,0:T(8,128)(2,1)S(1)}, bf16[64,512]{1,0:T(8,128)(2,1)S(1)}, u32[]{:S(2)}, u32[]{:S(2)}) collective-permute-start(bf16[64,512]{1,0:T(8,128)(2,1)S(1)} %get-tuple-element.71), channel_id=1, source_target_pairs={{0,24},{8,16},{16,8},{24,0},{1,25},{9,17},{17,9},{25,1},{2,26},{10... | collective-permute-start | bytes 196616 | tf_op jit(solution)/shard_map/ppermute | solution.py:374
  145.7 5.8 %collective-permute-start.16 = (bf16[64,512]{1,0:T(8,128)(2,1)S(1)}, bf16[64,512]{1,0:T(8,128)(2,1)S(1)}, u32[]{:S(2)}, u32[]{:S(2)}) collective-permute-start(bf16[64,512]{1,0:T(8,128)(2,1)S(1)} %get-tuple-element.72), channel_id=1, source_target_pairs={{0,16},{8,24},{16,0},{24,8},{1,17},{9,25},{17,1},{25,9},{2,18},{10... | collective-permute-start | bytes 196616 | tf_op jit(solution)/shard_map/ppermute | solution.py:374
  147.9 19.6 %collective-permute-start.34 = (bf16[512,1024]{1,0:T(8,128)(2,1)}, bf16[512,1024]{1,0:T(8,128)(2,1)}, u32[]{:S(2)}, u32[]{:S(2)}) collective-permute-start(bf16[512,1024]{1,0:T(8,128)(2,1)} %pad_maximum_fusion.2), channel_id=1, source_target_pairs={{0,2},{1,5},{2,0},{3,7},{4,6},{5,1},{6,4},{7,3},{8,10},{9,13},{10,... | collective-permute-start | bytes 3145736 | tf_op jit(solution)/shard_map/ppermute | solution.py:383
  152.6 4.5 %collective-permute-start.18 = (bf16[64,512]{1,0:T(8,128)(2,1)S(1)}, bf16[64,512]{1,0:T(8,128)(2,1)S(1)}, u32[]{:S(2)}, u32[]{:S(2)}) collective-permute-start(bf16[64,512]{1,0:T(8,128)(2,1)S(1)} %get-tuple-element.66), channel_id=1, source_target_pairs={{0,8},{8,0},{16,24},{24,16},{1,9},{9,1},{17,25},{25,17},{2,10},{10... | collective-permute-start | bytes 196616 | tf_op jit(solution)/shard_map/ppermute | solution.py:380
  152.7 5.2 %collective-permute-start.19 = (bf16[64,512]{1,0:T(8,128)(2,1)S(1)}, bf16[64,512]{1,0:T(8,128)(2,1)S(1)}, u32[]{:S(2)}, u32[]{:S(2)}) collective-permute-start(bf16[64,512]{1,0:T(8,128)(2,1)S(1)} %get-tuple-element.66), channel_id=1, source_target_pairs={{0,16},{8,24},{16,0},{24,8},{1,17},{9,25},{17,1},{25,9},{2,18},{10... | collective-permute-start | bytes 196616 | tf_op jit(solution)/shard_map/ppermute | solution.py:380
  154.9 6.1 %collective-permute-start.20 = (bf16[64,512]{1,0:T(8,128)(2,1)S(1)}, bf16[64,512]{1,0:T(8,128)(2,1)S(1)}, u32[]{:S(2)}, u32[]{:S(2)}) collective-permute-start(bf16[64,512]{1,0:T(8,128)(2,1)S(1)} %get-tuple-element.66), channel_id=1, source_target_pairs={{0,24},{8,16},{16,8},{24,0},{1,25},{9,17},{17,9},{25,1},{2,26},{10... | collective-permute-start | bytes 196616 | tf_op jit(solution)/shard_map/ppermute | solution.py:380
  161.0 6.4 %collective-permute-start.21 = (bf16[256,512]{1,0:T(8,128)(2,1)S(1)}, bf16[256,512]{1,0:T(8,128)(2,1)S(1)}, u32[]{:S(2)}, u32[]{:S(2)}) collective-permute-start(bf16[256,512]{1,0:T(8,128)(2,1)S(1)} %constant_dynamic-update-slice_fusion.4), channel_id=1, source_target_pairs={{0,4},{1,3},{2,6},{3,1},{4,0},{5,7},{6,2},{7,5},{8,12},{9,11},{10,... | collective-permute-start | bytes 786440 | tf_op jit(solution)/shard_map/ppermute | solution.py:383
  169.4 9.7 %copy-start.1 = (bf16[1024,1024]{1,0:T(8,128)(2,1)}, bf16[1024,1024]{1,0:T(8,128)(2,1)S(1)}, u32[]{:S(2)}) copy-start(bf16[1024,1024]{1,0:T(8,128)(2,1)S(1)} %pad_maximum_fusion.value_ref) | copy-start | bytes 6291460
  169.4 37.3 %collective-permute-start.35 = (bf16[1024,1024]{1,0:T(8,128)(2,1)S(1)}, bf16[1024,1024]{1,0:T(8,128)(2,1)}, u32[]{:S(2)}, u32[]{:S(2)}) collective-permute-start(bf16[1024,1024]{1,0:T(8,128)(2,1)S(1)} %pad_maximum_fusion.value_ref), channel_id=1, source_target_pairs={{0,1},{1,0},{2,3},{3,2},{4,5},{5,4},{6,7},{7,6},{8,9},{9,8},{10,11... | collective-permute-start | bytes 6291464 | tf_op jit(solution)/shard_map/ppermute | solution.py:385
  169.6 9.2 %collective-permute-start.22 = (bf16[512,512]{1,0:T(8,128)(2,1)S(1)}, bf16[512,512]{1,0:T(8,128)(2,1)S(1)}, u32[]{:S(2)}, u32[]{:S(2)}) collective-permute-start(bf16[512,512]{1,0:T(8,128)(2,1)S(1)} %pad_maximum_fusion.3), channel_id=1, source_target_pairs={{0,2},{1,5},{2,0},{3,7},{4,6},{5,1},{6,4},{7,3},{8,10},{9,13},{10,... | collective-permute-start | bytes 1572872 | tf_op jit(solution)/shard_map/ppermute | solution.py:383
  179.1 6.9 %copy-start.3 = (bf16[1024,512]{1,0:T(8,128)(2,1)}, bf16[1024,512]{1,0:T(8,128)(2,1)S(1)}, u32[]{:S(2)}) copy-start(bf16[1024,512]{1,0:T(8,128)(2,1)S(1)} %pad_maximum_fusion.1.value_ref) | copy-start | bytes 3145732
  179.1 20.8 %collective-permute-start.23 = (bf16[1024,512]{1,0:T(8,128)(2,1)S(1)}, bf16[1024,512]{1,0:T(8,128)(2,1)}, u32[]{:S(2)}, u32[]{:S(2)}) collective-permute-start(bf16[1024,512]{1,0:T(8,128)(2,1)S(1)} %pad_maximum_fusion.1.value_ref), channel_id=1, source_target_pairs={{0,1},{1,0},{2,3},{3,2},{4,5},{5,4},{6,7},{7,6},{8,9},{9,8},{10,11... | collective-permute-start | bytes 3145736 | tf_op jit(solution)/shard_map/ppermute | solution.py:385
  186.0 9.0 %collective-permute-start.9 = (bf16[192,512]{1,0:T(8,128)(2,1)}, bf16[192,512]{1,0:T(8,128)(2,1)S(1)}, u32[]{:S(2)}, u32[]{:S(2)}) collective-permute-start(bf16[192,512]{1,0:T(8,128)(2,1)} %get-tuple-element.48), channel_id=1, source_target_pairs={{0,7},{1,0},{2,1},{3,2},{4,3},{5,4},{6,5},{7,6},{8,15},{9,8},{10,9... | collective-permute-start | bytes 589832 | tf_op jit(solution)/shard_map/ppermute | solution.py:312
  186.8 8.2 %collective-permute-start.10 = (bf16[144,512]{1,0:T(8,128)(2,1)}, bf16[144,512]{1,0:T(8,128)(2,1)S(1)}, u32[]{:S(2)}, u32[]{:S(2)}) collective-permute-start(bf16[144,512]{1,0:T(8,128)(2,1)} %get-tuple-element.49), channel_id=1, source_target_pairs={{0,24},{1,25},{2,26},{3,27},{4,28},{5,29},{6,30},{7,31},{8,0},{9,1... | collective-permute-start | bytes 442376 | tf_op jit(solution)/shard_map/ppermute | solution.py:312
  189.1 6.0 %collective-permute-start.11 = (bf16[24,512]{1,0:T(8,128)(2,1)}, bf16[24,512]{1,0:T(8,128)(2,1)S(1)}, u32[]{:S(2)}, u32[]{:S(2)}) collective-permute-start(bf16[24,512]{1,0:T(8,128)(2,1)} %get-tuple-element.50), channel_id=1, source_target_pairs={{0,31},{1,24},{2,25},{3,26},{4,27},{5,28},{6,29},{7,30},{8,7},{9,0... | collective-permute-start | bytes 73736 | tf_op jit(solution)/shard_map/ppermute | solution.py:312
  193.2 1.8 copy-start
